TPU v7x, 32 devices: a whole 2x2x4 slice. The times are simulated.
32 devices in a mesh: nodes: 8 (over y, x, core), heads: 4 (over z).
Axes of the slice: x: 2, y: 2, z: 4, core: 2. Of those that a mesh axis runs over, the one named last changes fastest.
Arguments:
- features: bfloat16 [32768, 256], P(('nodes', 'heads')), may hold values from -6 to 6
- target: float32 [32768], P(('nodes', 'heads')), may hold values from -6 to 6
- counts: int32 [256], replicated, may hold values from 1 to 128, as said below
- neighbours: int32 [256, 8], P('nodes'), may hold values from 0 to 255, as said below
- edge_kinds: int32 [256, 9], P('nodes'), may hold values from 0 to 63
- enc_weight: float32 [256, 512], P('heads'), may hold values from -0.375 to 0.375
- enc_first: float32 [256, 512], P('heads'), may hold values from -0.0625 to 0.0625
- enc_second: float32 [256, 512], P('heads'), may hold values from 1.5258789e-05 to 0.00048828125
- qkv_weight: float32 [512, 1536], P('heads'), may hold values from -0.25 to 0.25
- qkv_first: float32 [512, 1536], P('heads'), may hold values from -0.0625 to 0.0625
- qkv_second: float32 [512, 1536], P('heads'), may hold values from 1.5258789e-05 to 0.00048828125
- out_weight: float32 [512, 512], P('heads'), may hold values from -2 to 2
- out_first: float32 [512, 512], P('heads'), may hold values from -0.125 to 0.125
- out_second: float32 [512, 512], P('heads'), may hold values from 6.1035156e-05 to 0.001953125
- up_weight: float32 [512, 2048], P('heads'), may hold values from -0.25 to 0.25
- up_first: float32 [512, 2048], P('heads'), may hold values from -0.0625 to 0.0625
- up_second: float32 [512, 2048], P('heads'), may hold values from 1.5258789e-05 to 0.00048828125
- down_weight: float32 [2048, 512], P('heads'), may hold values from -0.125 to 0.125
- down_first: float32 [2048, 512], P('heads'), may hold values from -0.0625 to 0.0625
- down_second: float32 [2048, 512], P('heads'), may hold values from 1.5258789e-05 to 0.00048828125
- vec_weight: float32 [6, 512], P(None, 'heads')
- vec_first: float32 [6, 512], P(None, 'heads'), may hold values from -0.125 to 0.125
- vec_second: float32 [6, 512], P(None, 'heads'), may hold values from 6.1035156e-05 to 0.001953125
Outputs:
- loss_out: float32 [1], replicated
- enc_new: float32 [256, 512], P('heads')
- enc_first_new: float32 [256, 512], P('heads')
- enc_second_new: float32 [256, 512], P('heads')
- qkv_new: float32 [512, 1536], P('heads')
- qkv_first_new: float32 [512, 1536], P('heads')
- qkv_second_new: float32 [512, 1536], P('heads')
- out_new: float32 [512, 512], P('heads')
- out_first_new: float32 [512, 512], P('heads')
- out_second_new: float32 [512, 512], P('heads')
- up_new: float32 [512, 2048], P('heads')
- up_first_new: float32 [512, 2048], P('heads')
- up_second_new: float32 [512, 2048], P('heads')
- down_new: float32 [2048, 512], P('heads')
- down_first_new: float32 [2048, 512], P('heads')
- down_second_new: float32 [2048, 512], P('heads')
- vec_new: float32 [6, 512], P(None, 'heads')
- vec_first_new: float32 [6, 512], P(None, 'heads')
- vec_second_new: float32 [6, 512], P(None, 'heads')
- enc_copy: bfloat16 [256, 512], P('heads')
- qkv_copy: bfloat16 [512, 1536], P('heads')
- out_copy: bfloat16 [512, 512], P('heads')
- up_copy: bfloat16 [512, 2048], P('heads')
- down_copy: bfloat16 [2048, 512], P('heads')
Inputs may be any that keep to these rules, and one draw needn't show every extreme that they name: `counts`: live slots of a block come first; the first block of every 32 consecutive blocks is full. Each block's 8 neighbours are distinct, differ from the block, and lie among the blocks of its own run of 32 consecutive blocks or of the runs just before and after it, the last run followed by the first.
All inputs are finite; a program needn't handle non-finite values.
Results may differ from a plain program's by a relative error of at most 0.0019.
The roundings to bfloat16 on the way count: a program that leaves them out, or rounds other values in their place, can miss the bound.
Values may be sent and summed in bfloat16 or wider, within the bound.
A program may use at most 256 MiB of HBM per device.

v0:
```python
import jax
import jax.numpy as jnp
from jax import lax
from jax.sharding import PartitionSpec as P

D = 512
HEADS = 8
BLOCK = 128
NBR = 8
ADAM_STEP = 3


highest = lax.Precision.HIGHEST
beta_one = 0.5
beta_two = 0.5
learn_rate = 0.02
weight_decay = 0.1
adam_eps = 1e-08
norm_eps = 1e-05


def with_halo(cells, sides, width):
    for axis, dim in sides:
        count = lax.axis_size(axis)
        head = lax.slice_in_dim(cells, 0, width, axis=dim)
        tail = lax.slice_in_dim(cells, cells.shape[dim] - width, cells.shape[dim], axis=dim)
        cells = jnp.concatenate(
            [
                lax.ppermute(tail, axis, [(i, (i + 1) % count) for i in range(count)]),
                cells,
                lax.ppermute(head, axis, [((i + 1) % count, i) for i in range(count)]),
            ],
            axis=dim,
        )
    return cells


def from_behind(value, axis, steps):
    count = lax.axis_size(axis)
    pairs = [(source, (source + steps) % count) for source in range(count)]
    return lax.ppermute(value, axis, pairs)


def normalize(values):
    average = jnp.mean(values, axis=-1, keepdims=True)
    centred = values - average
    variance = jnp.mean(centred * centred, axis=-1, keepdims=True)
    return centred * lax.rsqrt(variance + norm_eps)


def adamw(weight, first_moment, second, gradient):
    first_new = beta_one * first_moment + (1.0 - beta_one) * gradient
    second_new = beta_two * second + (1.0 - beta_two) * gradient * gradient
    first_hat = first_new / (1.0 - beta_one**ADAM_STEP)
    second_hat = second_new / (1.0 - beta_two**ADAM_STEP)
    weight_new = weight - learn_rate * (
        first_hat / (jnp.sqrt(second_hat) + adam_eps) + weight_decay * weight
    )
    return (weight_new, first_new, second_new)


def spread_flat(gradient, heads_count, nodes_count):
    return jnp.transpose(gradient.reshape(heads_count, nodes_count, -1), (1, 0, 2)).reshape(-1)


def local(
    features,
    target,
    counts,
    neighbours,
    edge_kinds,
    enc_weight,
    enc_first,
    enc_second,
    qkv_weight,
    qkv_first,
    qkv_second,
    out_weight,
    out_first,
    out_second,
    up_weight,
    up_first,
    up_second,
    down_weight,
    down_first,
    down_second,
    vec_weight,
    vec_first,
    vec_second,
):
    heads_count = lax.axis_size("heads")
    nodes_count = lax.axis_size("nodes")
    head_index = lax.axis_index("heads")
    node_index = lax.axis_index("nodes")
    row_count = features.shape[0]
    own_blocks = row_count // BLOCK
    group_blocks = own_blocks * heads_count
    group_rows = group_blocks * BLOCK
    head_local = HEADS // heads_count
    head_size = D // HEADS
    kind_count = D // HEADS
    slot_count = NBR + 1
    step_count = group_blocks // 4
    score_scale = head_size ** (-0.5)
    enc_copy, qkv_copy, out_copy, up_copy, down_copy, vec_copy = (
        lax.all_gather(enc_weight.astype(jnp.bfloat16), "heads", axis=0, tiled=True),
        lax.all_gather(qkv_weight.astype(jnp.bfloat16), "heads", axis=0, tiled=True),
        lax.all_gather(out_weight.astype(jnp.bfloat16), "heads", axis=0, tiled=True),
        lax.all_gather(up_weight.astype(jnp.bfloat16), "heads", axis=0, tiled=True),
        lax.all_gather(down_weight.astype(jnp.bfloat16), "heads", axis=0, tiled=True),
        lax.all_gather(vec_weight.astype(jnp.bfloat16), "heads", axis=1, tiled=True),
    )
    vectors = vec_copy.astype(jnp.float32)
    enc_bias = vectors[0]
    gain_one = vectors[1]
    gain_two = vectors[2]
    gain_three = vectors[3]
    head_vec = vectors[4]
    edge_local = lax.dynamic_slice_in_dim(
        vectors[5].reshape(kind_count, HEADS), head_index * head_local, head_local, 1
    )
    own_counts = lax.dynamic_slice_in_dim(
        counts, (node_index * heads_count + head_index) * own_blocks, own_blocks
    )
    row_live = (
        (jnp.arange(BLOCK, dtype=jnp.int32)[None, :] < own_counts[:, None])
        .reshape(row_count)
        .astype(jnp.float32)
    )
    live_total = jnp.sum(counts).astype(jnp.float32)
    resid_in = jnp.dot(features, enc_copy, preferred_element_type=jnp.float32) + enc_bias
    norm_one, norm_one_pull = jax.vjp(normalize, resid_in)
    act_one = (norm_one * gain_one).astype(jnp.bfloat16)
    qkv_rows = jnp.dot(act_one, qkv_copy, preferred_element_type=jnp.float32).astype(jnp.bfloat16)
    group_qkv = lax.all_to_all(
        qkv_rows.reshape(row_count, HEADS, 3 * head_size),
        "heads",
        split_axis=1,
        concat_axis=0,
        tiled=True,
    )
    query_all = group_qkv[:, :, :head_size]
    key_value = group_qkv[:, :, head_size:]
    key_pool = with_halo(key_value, (("nodes", 0),), group_rows)
    pool_blocks = key_pool.reshape(3 * group_blocks, BLOCK, head_local, 2 * head_size)

    def group_counts(offset):
        return lax.dynamic_slice_in_dim(
            counts, (node_index + offset) % nodes_count * group_blocks, group_blocks
        )

    pool_counts = jnp.concatenate([group_counts(nodes_count - 1), group_counts(0), group_counts(1)])
    relative = (neighbours // group_blocks - node_index + 1) % nodes_count
    nbr_pos = relative * group_blocks + neighbours % group_blocks
    self_pos = group_blocks + jnp.arange(group_blocks, dtype=jnp.int32)
    key_pos = jnp.concatenate([self_pos[:, None], nbr_pos], axis=1)
    kind_hot = jax.nn.one_hot(edge_kinds, kind_count, dtype=jnp.float32)
    slot_bias = jnp.einsum("bst,th->bsh", kind_hot, edge_local, precision=highest)
    key_live = jnp.arange(BLOCK, dtype=jnp.int32)[None, None, :] < pool_counts[key_pos][:, :, None]
    query_steps = query_all.reshape(step_count, 4, BLOCK, head_local, head_size)
    pos_steps = key_pos.reshape(step_count, 4, slot_count)
    bias_steps = slot_bias.reshape(step_count, 4, slot_count, head_local)
    live_steps = key_live.reshape(step_count, 4, slot_count, BLOCK)
    kind_steps = kind_hot.reshape(step_count, 4, slot_count, kind_count)

    def scored(query_part, key_part, bias_part, live_part):
        raw_scores = (
            jnp.einsum("bqhe,bkhe->bhqk", query_part, key_part, preferred_element_type=jnp.float32)
            * score_scale
        )
        bias_keys = jnp.transpose(jnp.repeat(bias_part, BLOCK, axis=1), (0, 2, 1))
        return jnp.where(
            live_part.reshape(4, 1, 1, slot_count * BLOCK),
            raw_scores + bias_keys[:, :, None, :],
            -1e30,
        )

    def fetch_keys(source, pos_part):
        fetched = source[pos_part].reshape(4, slot_count * BLOCK, head_local, 2 * head_size)
        return (fetched[..., :head_size], fetched[..., head_size:])

    def attend_step(loop_state, inputs):
        query_part, pos_part, bias_part, live_part = inputs
        key_part, value_part = fetch_keys(pool_blocks, pos_part)
        scores = scored(query_part, key_part, bias_part, live_part)
        top_score = jnp.max(scores, axis=-1, keepdims=True)
        exponent = jnp.exp(scores - top_score)
        row_total = jnp.sum(exponent, axis=-1, keepdims=True)
        attn_probs = (exponent / row_total).astype(jnp.bfloat16)
        out_part = jnp.einsum(
            "bhqk,bkhe->bqhe", attn_probs, value_part, preferred_element_type=jnp.float32
        )
        return (
            loop_state,
            (
                out_part.astype(jnp.bfloat16).reshape(4 * BLOCK, head_local, head_size),
                top_score + jnp.log(row_total),
            ),
        )

    _, (attn_group, log_totals) = lax.scan(
        attend_step, jnp.float32(0.0), (query_steps, pos_steps, bias_steps, live_steps)
    )
    attn_rows = lax.all_to_all(
        attn_group.reshape(group_rows, head_local, head_size),
        "heads",
        split_axis=0,
        concat_axis=1,
        tiled=True,
    ).reshape(row_count, D)
    hidden_one = resid_in + jnp.dot(attn_rows, out_copy, preferred_element_type=jnp.float32)
    norm_two, norm_two_pull = jax.vjp(normalize, hidden_one)
    act_two = (norm_two * gain_two).astype(jnp.bfloat16)
    up_val = jnp.dot(act_two, up_copy, preferred_element_type=jnp.float32)
    gelu_val, gelu_pull = jax.vjp(jax.nn.gelu, up_val)
    act_up = gelu_val.astype(jnp.bfloat16)
    hidden_two = hidden_one + jnp.dot(act_up, down_copy, preferred_element_type=jnp.float32)
    norm_three, norm_three_pull = jax.vjp(normalize, hidden_two)
    scaled = norm_three * gain_three
    predicted = jnp.sum(scaled * head_vec, axis=-1)
    pred_error = predicted - target
    local_loss = jnp.sum(row_live * pred_error * pred_error)
    total_loss = lax.psum(local_loss, ("nodes", "heads"))
    grad_pred = 2.0 * row_live * pred_error / live_total
    grad_scaled = grad_pred[:, None] * head_vec
    grad_head_vec = jnp.sum(grad_pred[:, None] * scaled, axis=0)
    grad_gain_three = jnp.sum(grad_scaled * norm_three, axis=0)
    grad_two = norm_three_pull(grad_scaled * gain_three)[0]
    grad_two_low = grad_two.astype(jnp.bfloat16)
    grad_down_weight = jnp.einsum(
        "rf,rd->fd", act_up, grad_two_low, preferred_element_type=jnp.float32
    )
    grad_act = jnp.einsum("rd,fd->rf", grad_two_low, down_copy, preferred_element_type=jnp.float32)
    grad_up_low = gelu_pull(grad_act)[0].astype(jnp.bfloat16)
    grad_up_weight = jnp.einsum(
        "rd,rf->df", act_two, grad_up_low, preferred_element_type=jnp.float32
    )
    grad_act_two = jnp.einsum("rf,df->rd", grad_up_low, up_copy, preferred_element_type=jnp.float32)
    grad_gain_two = jnp.sum(grad_act_two * norm_two, axis=0)
    grad_one = grad_two + norm_two_pull(grad_act_two * gain_two)[0]
    grad_one_low = grad_one.astype(jnp.bfloat16)
    grad_out_weight = jnp.einsum(
        "rc,rd->cd", attn_rows, grad_one_low, preferred_element_type=jnp.float32
    )
    grad_attn = jnp.einsum(
        "rd,cd->rc", grad_one_low, out_copy, preferred_element_type=jnp.float32
    ).astype(jnp.bfloat16)
    grad_heads = lax.all_to_all(
        grad_attn.reshape(row_count, HEADS, head_size),
        "heads",
        split_axis=1,
        concat_axis=0,
        tiled=True,
    )

    def back_step(loop_state, inputs):
        pool_grad, edge_grad = loop_state
        query_part, pos_part, bias_part, live_part, kind_part, lse_part, dout_part = inputs
        key_part, value_part = fetch_keys(pool_blocks, pos_part)
        scores = scored(query_part, key_part, bias_part, live_part)
        attn_probs = jnp.exp(scores - lse_part)
        probs_low = attn_probs.astype(jnp.bfloat16)
        grad_probs = jnp.einsum(
            "bqhe,bkhe->bhqk", dout_part, value_part, preferred_element_type=jnp.float32
        )
        grad_value = jnp.einsum(
            "bhqk,bqhe->bkhe", probs_low, dout_part, preferred_element_type=jnp.float32
        )
        grad_scores = attn_probs * (
            grad_probs - jnp.sum(attn_probs * grad_probs, axis=-1, keepdims=True)
        )
        scores_low = grad_scores.astype(jnp.bfloat16)
        grad_query = (
            jnp.einsum("bhqk,bkhe->bqhe", scores_low, key_part, preferred_element_type=jnp.float32)
            * score_scale
        )
        grad_key = (
            jnp.einsum(
                "bhqk,bqhe->bkhe", scores_low, query_part, preferred_element_type=jnp.float32
            )
            * score_scale
        )
        slot_sums = jnp.sum(
            grad_scores.reshape(4, head_local, BLOCK, slot_count, BLOCK), axis=(2, 4)
        )
        edge_grad = edge_grad + jnp.einsum("bst,bhs->th", kind_part, slot_sums, precision=highest)
        contrib = jnp.concatenate([grad_key, grad_value], axis=-1).reshape(
            4 * slot_count, BLOCK, head_local, 2 * head_size
        )
        pool_grad = pool_grad.at[pos_part.reshape(-1)].add(contrib)
        return ((pool_grad, edge_grad), grad_query.reshape(4 * BLOCK, head_local, head_size))

    start_state = (
        jnp.zeros((3 * group_blocks, BLOCK, head_local, 2 * head_size), jnp.float32),
        jnp.zeros((kind_count, head_local), jnp.float32),
    )
    grad_steps = grad_heads.reshape(step_count, 4, BLOCK, head_local, head_size)
    (pool_grad, edge_grad), grad_query = lax.scan(
        back_step,
        start_state,
        (query_steps, pos_steps, bias_steps, live_steps, kind_steps, log_totals, grad_steps),
    )
    pool_grad = pool_grad.reshape(3, group_rows, head_local, 2 * head_size)
    from_next = from_behind(pool_grad[0].astype(jnp.bfloat16), "nodes", -1).astype(jnp.float32)
    from_prev = from_behind(pool_grad[2].astype(jnp.bfloat16), "nodes", 1).astype(jnp.float32)
    grad_kv = pool_grad[1] + from_next + from_prev
    grad_group = jnp.concatenate(
        [grad_query.reshape(group_rows, head_local, head_size), grad_kv], axis=-1
    ).astype(jnp.bfloat16)
    grad_qkv = lax.all_to_all(grad_group, "heads", split_axis=0, concat_axis=1, tiled=True).reshape(
        row_count, 3 * D
    )
    grad_qkv_weight = jnp.einsum("rd,rc->dc", act_one, grad_qkv, preferred_element_type=jnp.float32)
    grad_act_one = jnp.einsum("rc,dc->rd", grad_qkv, qkv_copy, preferred_element_type=jnp.float32)
    grad_gain_one = jnp.sum(grad_act_one * norm_one, axis=0)
    grad_in = grad_one + norm_one_pull(grad_act_one * gain_one)[0]
    grad_enc_bias = jnp.sum(grad_in, axis=0)
    grad_enc_weight = jnp.einsum(
        "rf,rd->fd", features, grad_in.astype(jnp.bfloat16), preferred_element_type=jnp.float32
    )
    edge_full = lax.dynamic_update_slice(
        jnp.zeros((kind_count, HEADS), jnp.float32),
        edge_grad,
        (jnp.int32(0), head_index * head_local),
    )
    grad_vec = jnp.stack(
        [
            grad_enc_bias,
            grad_gain_one,
            grad_gain_two,
            grad_gain_three,
            grad_head_vec,
            edge_full.reshape(D),
        ]
    )
    vec_rows = jnp.transpose(grad_vec.reshape(6, heads_count, -1), (1, 0, 2))
    pieces = (
        lax.psum_scatter(
            spread_flat(grad_enc_weight, heads_count, nodes_count),
            ("nodes", "heads"),
            scatter_dimension=0,
            tiled=True,
        ),
        lax.psum_scatter(
            spread_flat(grad_qkv_weight, heads_count, nodes_count),
            ("nodes", "heads"),
            scatter_dimension=0,
            tiled=True,
        ),
        lax.psum_scatter(
            spread_flat(grad_out_weight, heads_count, nodes_count),
            ("nodes", "heads"),
            scatter_dimension=0,
            tiled=True,
        ),
        lax.psum_scatter(
            spread_flat(grad_up_weight, heads_count, nodes_count),
            ("nodes", "heads"),
            scatter_dimension=0,
            tiled=True,
        ),
        lax.psum_scatter(
            spread_flat(grad_down_weight, heads_count, nodes_count),
            ("nodes", "heads"),
            scatter_dimension=0,
            tiled=True,
        ),
        lax.psum_scatter(
            spread_flat(vec_rows, heads_count, nodes_count),
            ("nodes", "heads"),
            scatter_dimension=0,
            tiled=True,
        ),
    )
    joined = (
        lax.all_gather(pieces[0], "nodes", axis=0, tiled=True),
        lax.all_gather(pieces[1], "nodes", axis=0, tiled=True),
        lax.all_gather(pieces[2], "nodes", axis=0, tiled=True),
        lax.all_gather(pieces[3], "nodes", axis=0, tiled=True),
        lax.all_gather(pieces[4], "nodes", axis=0, tiled=True),
        lax.all_gather(pieces[5], "nodes", axis=0, tiled=True),
    )
    summed = (
        joined[0].reshape(enc_weight.shape),
        joined[1].reshape(qkv_weight.shape),
        joined[2].reshape(out_weight.shape),
        joined[3].reshape(up_weight.shape),
        joined[4].reshape(down_weight.shape),
        joined[5].reshape(vec_weight.shape),
    )
    enc_res = adamw(enc_weight, enc_first, enc_second, summed[0])
    qkv_res = adamw(qkv_weight, qkv_first, qkv_second, summed[1])
    out_res = adamw(out_weight, out_first, out_second, summed[2])
    up_res = adamw(up_weight, up_first, up_second, summed[3])
    down_res = adamw(down_weight, down_first, down_second, summed[4])
    vec_res = adamw(vec_weight, vec_first, vec_second, summed[5])
    loss_value = (total_loss / live_total).reshape(1)
    return (
        loss_value,
        enc_res[0],
        enc_res[1],
        enc_res[2],
        qkv_res[0],
        qkv_res[1],
        qkv_res[2],
        out_res[0],
        out_res[1],
        out_res[2],
        up_res[0],
        up_res[1],
        up_res[2],
        down_res[0],
        down_res[1],
        down_res[2],
        vec_res[0],
        vec_res[1],
        vec_res[2],
        enc_res[0].astype(jnp.bfloat16),
        qkv_res[0].astype(jnp.bfloat16),
        out_res[0].astype(jnp.bfloat16),
        up_res[0].astype(jnp.bfloat16),
        down_res[0].astype(jnp.bfloat16),
    )


def solution(mesh):
    in_specs = (
        P(("nodes", "heads"), None),
        P(("nodes", "heads")),
        P(),
        P("nodes", None),
        P("nodes", None),
        P("heads", None),
        P("heads", None),
        P("heads", None),
        P("heads", None),
        P("heads", None),
        P("heads", None),
        P("heads", None),
        P("heads", None),
        P("heads", None),
        P("heads", None),
        P("heads", None),
        P("heads", None),
        P("heads", None),
        P("heads", None),
        P("heads", None),
        P(None, "heads"),
        P(None, "heads"),
        P(None, "heads"),
    )
    out_specs = (
        P(),
        P("heads", None),
        P("heads", None),
        P("heads", None),
        P("heads", None),
        P("heads", None),
        P("heads", None),
        P("heads", None),
        P("heads", None),
        P("heads", None),
        P("heads", None),
        P("heads", None),
        P("heads", None),
        P("heads", None),
        P("heads", None),
        P("heads", None),
        P(None, "heads"),
        P(None, "heads"),
        P(None, "heads"),
        P("heads", None),
        P("heads", None),
        P("heads", None),
        P("heads", None),
        P("heads", None),
    )
    return jax.shard_map(local, mesh=mesh, in_specs=in_specs, out_specs=out_specs, check_vma=False)
```

profile of v0, /device:TPU:0, one launch (start us, length us, event | category | flops | bytes accessed | tf_op | source)
XLA Modules:
  0.0 1457.6 jit_solution(14408467626932349410)
XLA Ops:
  10.9 13.7 all_gather.37
  24.6 16.3 %all_gather.36 = bf16[256,512]{1,0:T(8,128)(2,1)S(1)} all-gather(bf16[64,512]{1,0:T(8,128)(2,1)S(1)} %convert_element_type.102), channel_id=1, replica_groups=mesh['nodes'=8,'heads'=4] {'heads'}, dimensions={0}, use_global_device_ids=true | all-gather | bytes 327680 | tf_op jit(solution)/shard_map/all_gather | solution.py:106
  41.9 12.3 all-gather.6.cloned.1.call-done
  69.7 103.3 %all-to-all-done = bf16[1024,8,192]{0,2,1:T(8,128)(2,1)} async-done(((bf16[1024,8,192]{0,2,1:T(8,128)(2,1)}), bf16[1024,8,192]{0,2,1:T(8,128)(2,1)}, u32[]{:S(2)}, u32[]{:S(2)}) %all-to-all-start) | async-done | bytes 3145760 | tf_op jit(solution)/shard_map/all_to_all | solution.py:135
  190.8 33.4 %collective-permute-done.1 = bf16[4096,2,128]{0,2,1:T(8,128)(2,1)} collective-permute-done((bf16[4096,2,128]{0,2,1:T(8,128)(2,1)S(1)}, bf16[4096,2,128]{0,2,1:T(8,128)(2,1)}, u32[]{:S(2)}, u32[]{:S(2)}) %collective-permute-start.1) | collective-permute-done | bytes 2097184 | tf_op jit(solution)/shard_map/ppermute | solution.py:31
  233.2 9.1 copy.214
  242.3 90.3 %while.27 = (s32[]{:T(128)}, bf16[8,512,2,64]{1,3,2,0:T(8,128)(2,1)}, f32[8,4,2,128,1]{3,2,1,4,0:T(2,128)}, s32[8,4,9]{2,1,0:T(4,128)S(1)}, bf16[96,128,2,128]{3...) while((s32[]{:T(128)}, ...), condition=%wide.region_5.6_spmd, body=%wide.region_2.5_spmd.sunk | while | flops 312672384 | bytes 31929212 | solution.py:201
  344.7 33.3 %all_gather.39 = bf16[512,512]{1,0:T(8,128)(2,1)S(1)} all-gather(bf16[128,512]{1,0:T(8,128)(2,1)S(1)} %convert_element_type.108), channel_id=1, replica_groups=mesh['nodes'=8,'heads'=4] {'heads'}, dimensions={0}, use_global_device_ids=true | all-gather | bytes 655360 | tf_op jit(solution)/shard_map/all_gather | solution.py:108
  391.3 8.0 fusion.79
  409.9 8.3 fusion.41
  431.9 21.7 %all-to-all-done.2 = bf16[1024,8,64]{0,2,1:T(8,128)(2,1)S(1)} async-done(((bf16[1024,8,64]{0,2,1:T(8,128)(2,1)}), bf16[1024,8,64]{0,2,1:T(8,128)(2,1)S(1)}, u32[]{:S(2)}, u32[]{:S(2)}) %all-to-all-start.2) | async-done | bytes 1048608 | tf_op jit(solution)/shard_map/all_to_all | solution.py:248
  461.7 416.9 %while.28 = (s32[]{:T(128)}, f32[96,128,2,128]{3,1,2,0:T(8,128)}, f32[64,2]{0,1:T(2,128)S(1)}, bf16[8,512,2,64]{1,3,2,0:T(8,128)(2,1)}, s32[8,4,9]{2,1,0:T(4,128...) while((s32[]{:T(128)}, f32[96,128,2,128]{3,1,2,0:T(8,128)}, ...), condition=%wide.region_23.24_spmd.clone, body=%wide.region_18.23_spmd.clone.sunk | while | flops 771086784 | bytes 123601624 | solution.py:298
  499.5 14.3 scatter_fusion
  551.6 14.2 scatter_fusion
  603.6 14.3 scatter_fusion
  655.7 14.4 scatter_fusion
  707.9 14.2 scatter_fusion
  760.0 14.3 scatter_fusion
  812.1 14.2 scatter_fusion
  864.1 14.3 scatter_fusion
  888.3 11.3 copy.229
  901.6 30.0 %collective-permute-done.3 = bf16[4096,2,128]{2,0,1:T(8,128)(2,1)} collective-permute-done((bf16[4096,2,128]{2,0,1:T(8,128)(2,1)}, bf16[4096,2,128]{2,0,1:T(8,128)(2,1)}, u32[]{:S(2)}, u32[]{:S(2)}) %collective-permute-start.3) | collective-permute-done | bytes 2097184 | tf_op jit(solution)/shard_map/ppermute | solution.py:41
  937.5 27.2 %copy.231 = bf16[4096,2,192]{2,1,0:T(2,128)(2,1)} copy(bf16[4096,2,192]{2,0,1:T(8,128)(2,1)S(1)} %pad_maximum_fusion.2) | data formatting | bytes 6291456 | tf_op jit(solution)/shard_map/concatenate | solution.py:307
  969.8 9.8 fusion.56
  1018.4 45.8 %all-to-all-done.3 = bf16[4096,2,192]{2,1,0:T(2,128)(2,1)} async-done(((bf16[4096,2,192]{2,1,0:T(2,128)(2,1)}), bf16[4096,2,192]{2,1,0:T(2,128)(2,1)}, u32[]{:S(2)}, u32[]{:S(2)}) %all-to-all-start.3) | async-done | bytes 3145760 | tf_op jit(solution)/shard_map/all_to_all | solution.py:310
  1064.2 11.8 copy.250
  1105.9 234.8 %all-reduce.11.cloned.1.call-done = (f32[131072]{0:T(1024)}, f32[786432]{0:T(1024)}, f32[262144]{0:T(1024)}, f32[1048576]{0:T(1024)}, f32[1048576]{0:T(1024)}) async-done(((f32[131072]{0:T(1024)}, f32[786432]{0:T(1024)}, f32[262144]{0:T(1024)}, f32[1048576]{0:T(1024)}, f32[1048576]{0:T(1024)}), (f32[131072]{0:T(1024)}, f32[786432]{0:T(1024)}, f32[262144]{0:T(1024)}, f32[1048576]{0:T(1024)}, ...) | async-done | bytes 13107216
  1344.5 39.7 %all-reduce.7 = (f32[]{:T(128)}, f32[3072]{0:T(1024)S(1)}) all-reduce(f32[]{:T(128)} %get-tuple-element.369, f32[3072]{0:T(1024)S(1)} %reshape.508), channel_id=1, replica_groups=mesh['nodes'=8,'heads'=4] {'nodes','heads'}, use_global_device_ids=true, to_apply=%region_12.13 | all-reduce | flops 3073 | bytes 24584 | tf_op jit(solution)/shard_map/psum | solution.py:223
  1385.1 13.1 all-reduce
  1402.9 9.2 all_gather.44
  1412.1 9.8 all_gather.43
  1421.9 9.1 all_gather.42
  (808 shorter events, 611.6 us)
Async XLA Ops:
  7.2 33.8 %copy-start = (bf16[1024,256]{1,0:T(8,128)(2,1)S(1)}, bf16[1024,256]{1,0:T(8,128)(2,1)}, u32[]{:S(2)}) copy-start(bf16[1024,256]{1,0:T(8,128)(2,1)} %param.27) | copy-start | bytes 1572868
  7.2 47.0 %all-gather.6.cloned.1.call-start = ((), (), s32[]{:S(2)}) async-start(), calls=%async_computation.4 | async-start | bytes 1966080 | tf_op jit(solution)/shard_map/all_gather | solution.py:107
  40.9 347.6 %copy-start.41 = (f32[1,512]{1,0:T(1,128)}, f32[1,512]{1,0:T(1,128)S(1)}, u32[]{:S(2)}) copy-start(f32[1,512]{1,0:T(1,128)S(1)} %get-tuple-element.373) | copy-start | bytes 6148
  40.9 381.1 %copy-start.43 = (f32[1,512]{1,0:T(1,128)}, f32[1,512]{1,0:T(1,128)S(1)}, u32[]{:S(2)}) copy-start(f32[1,512]{1,0:T(1,128)S(1)} %get-tuple-element.370) | copy-start | bytes 6148
  41.0 381.1 %copy-start.45 = (f32[1,512]{1,0:T(1,128)}, f32[1,512]{1,0:T(1,128)S(1)}, u32[]{:S(2)}) copy-start(f32[1,512]{1,0:T(1,128)S(1)} %get-tuple-element.371) | copy-start | bytes 6148
  41.0 381.1 %copy-start.55 = (f32[1,512]{1,0:T(1,128)}, f32[1,512]{1,0:T(1,128)S(1)}, u32[]{:S(2)}) copy-start(f32[1,512]{1,0:T(1,128)S(1)} %get-tuple-element.372) | copy-start | bytes 6148
  41.5 17.7 %copy-start.8 = (f32[1024,512]{0,1:T(8,128)}, f32[1024,512]{0,1:T(8,128)S(1)}, u32[]{:S(2)}) copy-start(f32[1024,512]{0,1:T(8,128)S(1)} %get-tuple-element.379) | copy-start | bytes 6291460
  41.5 17.7 %copy-start.53 = (f32[1024]{0:T(1024)}, f32[1024]{0:T(1024)S(1)}, u32[]{:S(2)}) copy-start(f32[1024]{0:T(1024)S(1)} %broadcast_multiply_fusion.2) | copy-start | bytes 12292
  41.9 17.4 %copy-start.51 = (f32[1024]{0:T(1024)}, f32[1024]{0:T(1024)S(1)}, u32[]{:S(2)}) copy-start(f32[1024]{0:T(1024)S(1)} %multiply_reduce_fusion.9) | copy-start | bytes 12292
  41.9 17.3 %copy-start.61 = (f32[1024]{0:T(1024)}, f32[1024]{0:T(1024)S(1)}, u32[]{:S(2)}) copy-start(f32[1024]{0:T(1024)S(1)} %fusion.73) | copy-start | bytes 12292
  64.0 109.0 %all-to-all-start = ((bf16[1024,8,192]{0,2,1:T(8,128)(2,1)}), bf16[1024,8,192]{0,2,1:T(8,128)(2,1)}, u32[]{:S(2)}, u32[]{:S(2)}) async-start(bf16[1024,8,192]{0,2,1:T(8,128)(2,1)} %bitcast.280), calls=%async_computation | async-start | bytes 6291456 | tf_op jit(solution)/shard_map/all_to_all | solution.py:135
  68.8 322.5 %all-gather.8.cloned.1.call-start = ((), (), s32[]{:S(2)}) async-start(), calls=%async_computation.5 | async-start | bytes 2621440 | tf_op jit(solution)/shard_map/all_gather | solution.py:109
  69.7 329.6 %all-gather.10.cloned.1.call-start = ((), (), s32[]{:S(2)}) async-start(), calls=%async_computation.6 | async-start | bytes 2621440 | tf_op jit(solution)/shard_map/all_gather | solution.py:110
  177.1 47.1 %collective-permute-start.1 = (bf16[4096,2,128]{0,2,1:T(8,128)(2,1)S(1)}, bf16[4096,2,128]{0,2,1:T(8,128)(2,1)}, u32[]{:S(2)}, u32[]{:S(2)}) collective-permute-start(bf16[4096,2,128]{0,2,1:T(8,128)(2,1)S(1)} %slice.75), channel_id=1, source_target_pairs={{4,0},{8,4},{12,8},{16,12},{20,16},{24,20},{28,24},{0,28},{5,1},{9... | collective-permute-start | bytes 6291464 | tf_op jit(solution)/shard_map/ppermute | solution.py:31
  178.2 47.9 %collective-permute-start = (bf16[4096,2,128]{0,2,1:T(8,128)(2,1)S(1)}, bf16[4096,2,128]{0,2,1:T(8,128)(2,1)}, u32[]{:S(2)}, u32[]{:S(2)}) collective-permute-start(bf16[4096,2,128]{0,2,1:T(8,128)(2,1)S(1)} %slice.75), channel_id=1, source_target_pairs={{0,4},{4,8},{8,12},{12,16},{16,20},{20,24},{24,28},{28,0},{1,5},{5... | collective-permute-start | bytes 6291464 | tf_op jit(solution)/shard_map/ppermute | solution.py:29
  339.8 38.2 %all-to-all-start.1 = ((bf16[4,2,65536]{2,1,0:T(2,128)(2,1)}), bf16[4,2,65536]{2,1,0:T(2,128)(2,1)S(1)}, u32[]{:S(2)}, u32[]{:S(2)}) async-start(bf16[4,2,65536]{2,1,0:T(2,128)(2,1)} %reshape.566), calls=%async_computation.1 | async-start | bytes 2097152 | tf_op jit(solution)/shard_map/all_to_all | solution.py:204
  389.5 32.6 %copy-start.37 = (f32[1024]{0:T(1024)}, f32[1024]{0:T(1024)S(1)}, u32[]{:S(2)}) copy-start(f32[1024]{0:T(1024)S(1)} %broadcast_multiply_fusion.1) | copy-start | bytes 12292
  391.2 30.9 %copy-start.49 = (f32[1024]{0:T(1024)}, f32[1024]{0:T(1024)S(1)}, u32[]{:S(2)}) copy-start(f32[1024]{0:T(1024)S(1)} %fusion.74) | copy-start | bytes 12292
  406.2 15.9 %copy-start.6 = (f32[1024,512]{0,1:T(8,128)}, f32[1024,512]{0,1:T(8,128)S(1)}, u32[]{:S(2)}) copy-start(f32[1024,512]{0,1:T(8,128)S(1)} %get-tuple-element.383) | copy-start | bytes 6291460
  426.6 26.9 %all-to-all-start.2 = ((bf16[1024,8,64]{0,2,1:T(8,128)(2,1)}), bf16[1024,8,64]{0,2,1:T(8,128)(2,1)S(1)}, u32[]{:S(2)}, u32[]{:S(2)}) async-start(bf16[1024,8,64]{0,2,1:T(8,128)(2,1)} %bitcast.27), calls=%async_computation.2 | async-start | bytes 2097152 | tf_op jit(solution)/shard_map/all_to_all | solution.py:248
  885.1 46.5 %collective-permute-start.3 = (bf16[4096,2,128]{2,0,1:T(8,128)(2,1)}, bf16[4096,2,128]{2,0,1:T(8,128)(2,1)}, u32[]{:S(2)}, u32[]{:S(2)}) collective-permute-start(bf16[4096,2,128]{2,0,1:T(8,128)(2,1)} %bitcast.34), channel_id=1, source_target_pairs={{0,4},{4,8},{8,12},{12,16},{16,20},{20,24},{24,28},{28,0},{1,5},{5... | collective-permute-start | bytes 6291464 | tf_op jit(solution)/shard_map/ppermute | solution.py:41
  885.1 47.3 %collective-permute-start.2 = (bf16[4096,2,128]{2,0,1:T(8,128)(2,1)}, bf16[4096,2,128]{2,0,1:T(8,128)(2,1)}, u32[]{:S(2)}, u32[]{:S(2)}) collective-permute-start(bf16[4096,2,128]{2,0,1:T(8,128)(2,1)} %bitcast.33), channel_id=1, source_target_pairs={{0,28},{4,0},{8,4},{12,8},{16,12},{20,16},{24,20},{28,24},{1,29},{... | collective-permute-start | bytes 6291464 | tf_op jit(solution)/shard_map/ppermute | solution.py:41
  901.6 30.8 %slice-start = ((f32[96,128,2,128]{3,1,0,2:T(8,128)}), f32[32,128,2,128]{3,1,0,2:T(8,128)S(1)}, s32[]{:S(2)}) async-start(f32[96,128,2,128]{3,1,0,2:T(8,128)} %copy.229), calls=%async_computation.10 | async-start | bytes 8388608 | tf_op jit(solution)/shard_map/slice | solution.py:306
  964.7 99.5 %all-to-all-start.3 = ((bf16[4096,2,192]{2,1,0:T(2,128)(2,1)}), bf16[4096,2,192]{2,1,0:T(2,128)(2,1)}, u32[]{:S(2)}, u32[]{:S(2)}) async-start(bf16[4096,2,192]{2,1,0:T(2,128)(2,1)} %copy.231), calls=%async_computation.3 | async-start | bytes 8388608 | tf_op jit(solution)/shard_map/all_to_all | solution.py:310
  969.7 371.0 %all-reduce.11.cloned.1.call-start = ((), (), s32[]{:S(2)}) async-start(), calls=%async_computation.9 | async-start | bytes 26214400
  1103.5 334.5 %all-gather.12.cloned.1.call-start = ((), (), s32[]{:S(2)}) async-start(), calls=%async_computation.7 | async-start | bytes 1179648 | tf_op jit(solution)/shard_map/all_gather | solution.py:379
  1342.3 56.0 %copy-start.59 = (f32[6,128]{1,0:T(8,128)S(1)}, f32[6,128]{1,0:T(8,128)}, u32[]{:S(2)}) copy-start(f32[6,128]{1,0:T(8,128)} %param.47) | copy-start | bytes 9220
  1342.3 56.0 %copy-start.72 = (f32[6,128]{1,0:T(8,128)S(1)}, f32[6,128]{1,0:T(8,128)}, u32[]{:S(2)}) copy-start(f32[6,128]{1,0:T(8,128)} %param.48) | copy-start | bytes 9220
  1342.3 56.0 %copy-start.73 = (f32[6,128]{1,0:T(8,128)S(1)}, f32[6,128]{1,0:T(8,128)}, u32[]{:S(2)}) copy-start(f32[6,128]{1,0:T(8,128)} %param.49) | copy-start | bytes 9220
  1342.3 101.7 %all-gather.14.cloned.1.call-start = ((), (), s32[]{:S(2)}) async-start(), calls=%async_computation.8 | async-start | bytes 1179648 | tf_op jit(solution)/shard_map/all_gather | solution.py:380
  1400.5 31.4 %copy-start.30 = (f32[64,512]{1,0:T(8,128)S(1)}, f32[64,512]{1,0:T(8,128)}, u32[]{:S(2)}) copy-start(f32[64,512]{1,0:T(8,128)} %param.32) | copy-start | bytes 393220
  1412.1 21.8 %copy-start.27 = (f32[128,512]{1,0:T(8,128)S(1)}, f32[128,512]{1,0:T(8,128)}, u32[]{:S(2)}) copy-start(f32[128,512]{1,0:T(8,128)} %param.38) | copy-start | bytes 786436
  (99 other events, 500.7 us)
Sparse Core Ops, SparseCore 0:
  10.2 43.9 all-gather.5
  71.7 85.6 all-gather.7
  179.5 44.3 all-gather.9
  1103.7 236.9 all-reduce.10
  1343.0 22.9 all-gather.11
  1422.1 21.9 all-gather.13
where the time goes:
time: 1470 us; the launch traced here: 1460 us
  waiting for transfers between devices  485 us (33%)
  local copies, waits for them, and re-layouts  423 us (29%)
  other arithmetic  193 us (13%)
  matrix products  169 us (11%)
  blocking collectives  144 us (10%)
  starting transfers between devices  23.1 us (2%)
  between operations  18.8 us (1%)
    unnamed x7, waiting for transfers between devices  235 us
    scatter-add x8, other arithmetic, back_step(): pool_grad = pool_grad.at[pos_part.reshape(-1)].add(contrib)  114 us
    all_to_all x1, waiting for transfers between devices, local(): lax.all_to_all(qkv_rows.reshape(row_count, HEADS, 3 * head_size), 'heads'...  103 us
    gather x32, local copies, waits for them, and re-layouts, fetch_keys(): source[pos_part].reshape(4, slot_count * BLOCK, head_local, 2 * head_size)  63.1 us
    concatenate x8, local copies, waits for them, and re-layouts, back_step(): jnp.concatenate([grad_key, grad_value], axis=-1)  48.5 us
    all_to_all x1, waiting for transfers between devices, local(): lax.all_to_all(grad_group, 'heads', split_axis=0, concat_axis=1, tiled=True)  45.8 us
    reshape x8, local copies, waits for them, and re-layouts, back_step(): jnp.concatenate([grad_key, grad_value], axis=-1)  40.5 us
    psum x1, blocking collectives, local(): total_loss = lax.psum(local_loss, ('nodes', 'heads'))  39.7 us
  transfers between devices with their start and end apart: 14, of which 10 were waited for; matrix products, arithmetic and copies ran while one was open for 16% of the time, Pallas kernels for 0%

commit v1 on v0

v1 whole, which is shorter than its diff:
```python
import functools

import jax
import jax.numpy as jnp
from jax import lax
from jax.experimental import pallas as pl
from jax.experimental.pallas import tpu as pltpu
from jax.sharding import PartitionSpec as P

BLOCK = 128
NT = (((1,), (1,)), ((), ()))
NN = (((1,), (0,)), ((), ()))
f32 = jnp.float32
bf16 = jnp.bfloat16


def dotf(a, b, dims):
    return lax.dot_general(a, b, dims, preferred_element_type=f32)


def head_rows(x, hl, hs, cp):
    if hl == 1:
        return x
    lane = lax.broadcasted_iota(jnp.int32, (BLOCK, cp), 1)
    zero = jnp.zeros_like(x)
    return jnp.concatenate([jnp.where(lane // hs == h, x, zero) for h in range(hl)], axis=0)


def ones_lane(hl, cp, ka):
    rows = hl * BLOCK
    lane = lax.broadcasted_iota(jnp.int32, (rows, ka - cp), 1)
    return jnp.where(lane == 0, 1.0, 0.0).astype(bf16)


def attend_kernel(hl, hs, cp, ka, slots, pos_ref, q_ref, brow_ref, kaug_ref, vt_ref, o_ref, lse_ref, s_ref, p_ref):
    b = pl.program_id(0)
    rows = hl * BLOCK
    q2 = head_rows(q_ref[...], hl, hs, cp)
    qa = jnp.concatenate([q2, ones_lane(hl, cp, ka)], axis=1) if ka > cp else q2
    top = None
    for s in range(slots):
        p = pos_ref[b * slots + s]
        ks = kaug_ref[pl.ds(pl.multiple_of(p * BLOCK, BLOCK), BLOCK), :]
        sc = dotf(ks, qa, NT)
        s_ref[s] = sc
        t = jnp.max(sc, axis=0, keepdims=True) + brow_ref[0, s:s + 1, :]
        top = t if top is None else jnp.maximum(top, t)
    tot = jnp.zeros((1, rows), f32)
    for s in range(slots):
        e = jnp.exp(s_ref[s] - (top - brow_ref[0, s:s + 1, :]))
        s_ref[s] = e
        tot = tot + jnp.sum(e, axis=0, keepdims=True)
    lse_ref[0] = top + jnp.log(tot)
    inv = 1.0 / tot
    vs = []
    for s in range(slots):
        p_ref[s * BLOCK:(s + 1) * BLOCK, :] = (s_ref[s] * inv).astype(bf16)
        vs.append(vt_ref[pos_ref[b * slots + s]])
    ot = dotf(jnp.concatenate(vs, axis=1), p_ref[...], NN)
    parts = [ot[h * hs:(h + 1) * hs, h * BLOCK:(h + 1) * BLOCK] for h in range(hl)]
    if hl * hs < cp:
        parts.append(jnp.zeros((cp - hl * hs, BLOCK), f32))
    o_ref[...] = jnp.concatenate(parts, axis=0).T.astype(bf16)


def attend(pos, q, brow, kaug, vt, hl, hs):
    cp, ka = q.shape[1], kaug.shape[1]
    nb = q.shape[0] // BLOCK
    slots = brow.shape[1]
    rows = hl * BLOCK
    whole = lambda a: pl.BlockSpec(a.shape, lambda i, *_: (0,) * a.ndim, pipeline_mode=pl.Buffered(1))
    return pl.pallas_call(
        functools.partial(attend_kernel, hl, hs, cp, ka, slots),
        grid_spec=pltpu.PrefetchScalarGridSpec(
            num_scalar_prefetch=1, grid=(nb,),
            in_specs=[pl.BlockSpec((BLOCK, cp), lambda i, *_: (i, 0)),
                      pl.BlockSpec((1, slots, rows), lambda i, *_: (i, 0, 0)),
                      whole(kaug), whole(vt)],
            out_specs=[pl.BlockSpec((BLOCK, cp), lambda i, *_: (i, 0)),
                       pl.BlockSpec((1, 1, rows), lambda i, *_: (i, 0, 0))],
            scratch_shapes=[pltpu.VMEM((slots, BLOCK, rows), f32), pltpu.VMEM((slots * BLOCK, rows), bf16)]),
        out_shape=[jax.ShapeDtypeStruct(q.shape, bf16), jax.ShapeDtypeStruct((nb, 1, rows), f32)],
        compiler_params=pltpu.CompilerParams(vmem_limit_bytes=60 << 20),
        name="attend",
    )(pos, q, brow, kaug, vt)


def attend_back_kernel(hl, hs, cp, ka, slots, scale, pos_ref, q_ref, do_ref, o_ref, lse_ref, brow_ref, kaug_ref, v_ref, kt_ref,
                       dq_ref, dkv_ref, edge_ref):
    b = pl.program_id(0)
    rows = hl * BLOCK

    @pl.when(b == 0)
    def _():
        dkv_ref[...] = jnp.zeros_like(dkv_ref)

    q2 = head_rows(q_ref[...], hl, hs, cp)
    qa = jnp.concatenate([q2, ones_lane(hl, cp, ka)], axis=1) if ka > cp else q2
    do = do_ref[...]
    do2 = head_rows(do, hl, hs, cp)
    prod = (do.astype(f32) * o_ref[...].astype(f32)).T
    dd = jnp.concatenate([jnp.sum(prod[h * hs:(h + 1) * hs], axis=0, keepdims=True) for h in range(hl)], axis=1)
    lse = lse_ref[0]
    dqt = jnp.zeros((cp, rows), f32)
    for s in range(slots):
        p = pos_ref[b * slots + s]
        at = pl.ds(pl.multiple_of(p * BLOCK, BLOCK), BLOCK)
        sc = dotf(kaug_ref[at, :], qa, NT)
        pr = jnp.exp(sc - (lse - brow_ref[0, s:s + 1, :]))
        dp = dotf(v_ref[at, :], do2, NT)
        ds = pr * (dp - dd)
        edge_ref[0, s:s + 1, :] = jnp.sum(ds, axis=0, keepdims=True)
        dsl = ds.astype(bf16)
        dv = dotf(pr.astype(bf16), do2, NN)
        dk = dotf(dsl, q2, NN)
        dkv_ref[at, 0:cp] += dk
        dkv_ref[at, cp:2 * cp] += dv
        dqt = dqt + dotf(kt_ref[p], dsl, NN)
    parts = [dqt[h * hs:(h + 1) * hs, h * BLOCK:(h + 1) * BLOCK] for h in range(hl)]
    if hl * hs < cp:
        parts.append(jnp.zeros((cp - hl * hs, BLOCK), f32))
    dq_ref[...] = (jnp.concatenate(parts, axis=0).T * scale).astype(bf16)


def attend_back(pos, q, do, o, lse, brow, kaug, v, kt, hl, hs):
    cp, ka = q.shape[1], kaug.shape[1]
    nb = q.shape[0] // BLOCK
    slots = brow.shape[1]
    rows = hl * BLOCK
    whole = lambda a: pl.BlockSpec(a.shape, lambda i, *_: (0,) * a.ndim, pipeline_mode=pl.Buffered(1))
    tile = pl.BlockSpec((BLOCK, cp), lambda i, *_: (i, 0))
    return pl.pallas_call(
        functools.partial(attend_back_kernel, hl, hs, cp, ka, slots, hs ** -0.5),
        grid_spec=pltpu.PrefetchScalarGridSpec(
            num_scalar_prefetch=1, grid=(nb,),
            in_specs=[tile, tile, tile,
                      pl.BlockSpec((1, 1, rows), lambda i, *_: (i, 0, 0)),
                      pl.BlockSpec((1, slots, rows), lambda i, *_: (i, 0, 0)),
                      whole(kaug), whole(v), whole(kt)],
            out_specs=[tile, pl.BlockSpec((v.shape[0], 2 * cp), lambda i, *_: (0, 0), pipeline_mode=pl.Buffered(1)),
                       pl.BlockSpec((1, slots, rows), lambda i, *_: (i, 0, 0))]),
        out_shape=[jax.ShapeDtypeStruct(q.shape, bf16), jax.ShapeDtypeStruct((v.shape[0], 2 * cp), f32),
                   jax.ShapeDtypeStruct((nb, slots, rows), f32)],
        compiler_params=pltpu.CompilerParams(vmem_limit_bytes=60 << 20),
        name="attend_back",
    )(pos, q, do, o, lse, brow, kaug, v, kt)
norm_eps = 1e-05


def encode_kernel(cp, ka, cols, scale, per_group, cnt_ref, fp_ref, fo_ref, fn_ref, enc_ref, bias_ref, gain_ref, w_ref,
                  kaug_ref, kt_ref, v_ref, vt_ref, q_ref, x_ref):
    i = pl.program_id(0)
    group = i // per_group
    tile = x_ref.shape[0]
    for g, ref in enumerate((fp_ref, fo_ref, fn_ref)):
        @pl.when(group == g)
        def _(ref=ref):
            x_ref[...] = ref[...]
    resid = dotf(x_ref[...], enc_ref[...], NN) + bias_ref[...]
    centred = resid - jnp.mean(resid, axis=-1, keepdims=True)
    variance = jnp.mean(centred * centred, axis=-1, keepdims=True)
    act = (centred * lax.rsqrt(variance + norm_eps) * gain_ref[...]).astype(bf16)
    kv = dotf(act, w_ref[:, cp:], NN).astype(bf16)
    key, value = kv[:, :cp], kv[:, cp:]
    row = lax.broadcasted_iota(jnp.int32, (BLOCK, 128), 0)
    lane = lax.broadcasted_iota(jnp.int32, (BLOCK, 128), 1)
    first = i * (tile // BLOCK)
    dead = jnp.concatenate(
        [jnp.where((row >= cnt_ref[first + j]) & (lane == cols % 128), -1e30, 0.0) for j in range(tile // BLOCK)], axis=0).astype(bf16)
    if ka > cp:
        kaug_ref[:, :cp] = key
        kaug_ref[:, cp:] = dead
    else:
        kaug_ref[...] = key + dead
    v_ref[...] = value
    for j in range(tile // BLOCK):
        kt_ref[j] = key[j * BLOCK:(j + 1) * BLOCK].T
        vt_ref[j] = value[j * BLOCK:(j + 1) * BLOCK].T

    @pl.when(group == 1)
    def _():
        q = (dotf(act, w_ref[:, :cp], NN) * scale).astype(bf16)
        if ka == cp:
            lanes = lax.broadcasted_iota(jnp.int32, q.shape, 1)
            q = jnp.where(lanes == cols, jnp.ones_like(q), q)
        q_ref[...] = q


def encode(counts, prev, own, nxt, enc, bias, gain, w, cp, ka, cols, scale, tile=512):
    rows, feat = own.shape
    width = enc.shape[1]
    per = rows // tile
    blocks = tile // BLOCK
    whole = lambda a: pl.BlockSpec(a.shape, lambda i, *_: (0,) * a.ndim, pipeline_mode=pl.Buffered(1))
    part = lambda g: pl.BlockSpec((tile, feat), lambda i, *_: (jnp.clip(i - g * per, 0, per - 1), 0))
    return pl.pallas_call(
        functools.partial(encode_kernel, cp, ka, cols, scale, per),
        grid_spec=pltpu.PrefetchScalarGridSpec(
            num_scalar_prefetch=1, grid=(3 * per,),
            in_specs=[part(0), part(1), part(2), whole(enc), whole(bias), whole(gain), whole(w)],
            out_specs=[pl.BlockSpec((tile, ka), lambda i, *_: (i, 0)),
                       pl.BlockSpec((blocks, cp, BLOCK), lambda i, *_: (i, 0, 0)),
                       pl.BlockSpec((tile, cp), lambda i, *_: (i, 0)),
                       pl.BlockSpec((blocks, cp, BLOCK), lambda i, *_: (i, 0, 0)),
                       pl.BlockSpec((tile, cp), lambda i, *_: (jnp.clip(i - per, 0, per - 1), 0))],
            scratch_shapes=[pltpu.VMEM((tile, feat), bf16)]),
        out_shape=[jax.ShapeDtypeStruct((3 * rows, ka), bf16),
                   jax.ShapeDtypeStruct((3 * rows // BLOCK, cp, BLOCK), bf16),
                   jax.ShapeDtypeStruct((3 * rows, cp), bf16),
                   jax.ShapeDtypeStruct((3 * rows // BLOCK, cp, BLOCK), bf16),
                   jax.ShapeDtypeStruct((rows, cp), bf16)],
        compiler_params=pltpu.CompilerParams(vmem_limit_bytes=60 << 20),
        name="encode",
    )(counts, prev, own, nxt, enc, bias, gain, w)


def encode_back_kernel(cp, per_group, fp_ref, fo_ref, fn_ref, dkv_ref, dq_ref, enct_ref, bias_ref, gain_ref, wq_ref, wkv_ref,
                       dw_ref, denc_ref, dgain_ref, dbias_ref, x_ref, g_ref):
    i = pl.program_id(0)
    group = i // per_group
    tile = x_ref.shape[0]
    width = enct_ref.shape[0]
    reps = tile // 128

    @pl.when(i == 0)
    def _():
        for ref in (dw_ref, denc_ref, dgain_ref, dbias_ref):
            ref[...] = jnp.zeros_like(ref)

    for g, ref in enumerate((fp_ref, fo_ref, fn_ref)):
        @pl.when(group == g)
        def _(ref=ref):
            x_ref[...] = ref[...]
    x = x_ref[...]
    wide = lambda c: jnp.concatenate([c] * reps, axis=1)
    fold = lambda a: functools.reduce(jnp.add, [a[:, r * 128:(r + 1) * 128] for r in range(reps)])
    resid = dotf(enct_ref[...], x, NT) + wide(bias_ref[...])
    centred = resid - jnp.sum(resid, axis=0, keepdims=True) * (1.0 / width)
    variance = jnp.sum(centred * centred, axis=0, keepdims=True) * (1.0 / width)
    inv = lax.rsqrt(variance + norm_eps)
    norm = centred * inv
    gain = wide(gain_ref[...])
    act = (norm * gain).astype(bf16)
    dkv = dkv_ref[...].astype(bf16)
    g_ref[...] = dotf(wkv_ref[...], dkv, NT)
    dw_ref[:, cp:] += dotf(act, dkv, NN)

    @pl.when(group == 1)
    def _():
        dq = dq_ref[...]
        g_ref[...] += dotf(wq_ref[...], dq, NT)
        dw_ref[:, :cp] += dotf(act, dq, NN)

    grad = g_ref[...]
    dgain_ref[...] += fold(grad * norm)
    back = grad * gain
    mean_one = jnp.sum(back, axis=0, keepdims=True) * (1.0 / width)
    mean_two = jnp.sum(back * norm, axis=0, keepdims=True) * (1.0 / width)
    din = inv * (back - mean_one - norm * mean_two)
    dbias_ref[...] += fold(din)
    denc_ref[...] += dotf(din.astype(bf16), x, NN)


def encode_back(prev, own, nxt, dkv, dq, enct, bias, gain, wq, wkv, tile=512):
    rows, feat = own.shape
    width = enct.shape[0]
    cp = dq.shape[1]
    per = rows // tile
    whole = lambda a: pl.BlockSpec(a.shape, lambda i: (0,) * a.ndim, pipeline_mode=pl.Buffered(1))
    part = lambda g: pl.BlockSpec((tile, feat), lambda i: (jnp.clip(i - g * per, 0, per - 1), 0))
    keep = lambda s: pl.BlockSpec(s, lambda i: (0,) * len(s), pipeline_mode=pl.Buffered(1))
    shapes = [(width, 3 * cp), (width, feat), (width, 128), (width, 128)]
    return pl.pallas_call(
        functools.partial(encode_back_kernel, cp, per),
        grid=(3 * per,),
        in_specs=[part(0), part(1), part(2), pl.BlockSpec((tile, 2 * cp), lambda i: (i, 0)),
                  pl.BlockSpec((tile, cp), lambda i: (jnp.clip(i - per, 0, per - 1), 0)),
                  whole(enct), whole(bias), whole(gain), whole(wq), whole(wkv)],
        out_specs=[keep(s) for s in shapes],
        out_shape=[jax.ShapeDtypeStruct(s, f32) for s in shapes],
        scratch_shapes=[pltpu.VMEM((tile, feat), bf16), pltpu.VMEM((width, tile), f32)],
        compiler_params=pltpu.CompilerParams(vmem_limit_bytes=60 << 20),
        name="encode_back",
    )(prev, own, nxt, dkv, dq, enct, bias, gain, wq, wkv)
D = 512
HEADS = 8
NBR = 8
ADAM_STEP = 3
highest = lax.Precision.HIGHEST
beta_one = 0.5
beta_two = 0.5
learn_rate = 0.02
weight_decay = 0.1
adam_eps = 1e-08


def normalize(values):
    average = jnp.mean(values, axis=-1, keepdims=True)
    centred = values - average
    variance = jnp.mean(centred * centred, axis=-1, keepdims=True)
    return centred * lax.rsqrt(variance + norm_eps)


def adamw(weight, first_moment, second, gradient):
    first_new = beta_one * first_moment + (1.0 - beta_one) * gradient
    second_new = beta_two * second + (1.0 - beta_two) * gradient * gradient
    first_hat = first_new / (1.0 - beta_one**ADAM_STEP)
    second_hat = second_new / (1.0 - beta_two**ADAM_STEP)
    weight_new = weight - learn_rate * (
        first_hat / (jnp.sqrt(second_hat) + adam_eps) + weight_decay * weight
    )
    return (weight_new, first_new, second_new)


def spread_flat(gradient, heads_count, nodes_count):
    return jnp.transpose(gradient.reshape(heads_count, nodes_count, -1), (1, 0, 2)).reshape(-1)


def from_behind(value, axis, steps):
    count = lax.axis_size(axis)
    pairs = [(source, (source + steps) % count) for source in range(count)]
    return lax.ppermute(value, axis, pairs)


def local(
    features, target, counts, neighbours, edge_kinds,
    enc_weight, enc_first, enc_second, qkv_weight, qkv_first, qkv_second,
    out_weight, out_first, out_second, up_weight, up_first, up_second,
    down_weight, down_first, down_second, vec_weight, vec_first, vec_second,
):
    heads_count = lax.axis_size("heads")
    nodes_count = lax.axis_size("nodes")
    head_index = lax.axis_index("heads")
    node_index = lax.axis_index("nodes")
    row_count = features.shape[0]
    own_blocks = row_count // BLOCK
    group_blocks = own_blocks * heads_count
    group_rows = group_blocks * BLOCK
    hl = HEADS // heads_count
    hs = D // HEADS
    cols = hl * hs
    cp = -(-cols // 128) * 128
    ka = -(-(cols + 1) // 128) * 128
    kinds = D // HEADS
    slots = NBR + 1
    low = lambda a: a.astype(bf16)
    gather = lambda a, axis: lax.all_gather(low(a), "heads", axis=axis, tiled=True)

    own_feat = lax.all_gather(features, "heads", axis=0, tiled=True)
    prev_feat = from_behind(own_feat, "nodes", 1)
    next_feat = from_behind(own_feat, "nodes", -1)
    enc_b = gather(enc_weight, 0)
    vectors = gather(vec_weight, 1).astype(f32)
    qkv_cols = lax.all_to_all(low(qkv_weight), "heads", split_axis=1, concat_axis=0, tiled=True)
    qkv_cols = jnp.transpose(qkv_cols.reshape(D, hl, 3, hs), (0, 2, 1, 3)).reshape(D, 3, cols)
    qkv_cols = jnp.pad(qkv_cols, ((0, 0), (0, 0), (0, cp - cols))).reshape(D, 3 * cp)
    out_b, up_b, down_b = gather(out_weight, 0), gather(up_weight, 0), gather(down_weight, 0)

    enc_bias, gain_one, gain_two, gain_three, head_vec = (vectors[r] for r in range(5))
    edge_local = lax.dynamic_slice_in_dim(vectors[5].reshape(kinds, HEADS), head_index * hl, hl, 1)
    own_counts = lax.dynamic_slice_in_dim(counts, (node_index * heads_count + head_index) * own_blocks, own_blocks)
    row_live = (jnp.arange(BLOCK, dtype=jnp.int32)[None, :] < own_counts[:, None]).reshape(row_count).astype(f32)
    live_total = jnp.sum(counts).astype(f32)

    def group_counts(offset):
        return lax.dynamic_slice_in_dim(counts, (node_index + offset) % nodes_count * group_blocks, group_blocks)

    pool_counts = jnp.concatenate([group_counts(nodes_count - 1), group_counts(0), group_counts(1)])
    relative = (neighbours // group_blocks - node_index + 1) % nodes_count
    nbr_pos = relative * group_blocks + neighbours % group_blocks
    self_pos = group_blocks + jnp.arange(group_blocks, dtype=jnp.int32)
    key_pos = jnp.concatenate([self_pos[:, None], nbr_pos], axis=1).reshape(-1)
    kind_hot = jax.nn.one_hot(edge_kinds, kinds, dtype=f32)
    slot_bias = jnp.einsum("bst,th->bsh", kind_hot, edge_local, precision=highest)
    bias_rows = jnp.repeat(slot_bias, BLOCK, axis=2)

    kaug, kt, value, vt, query = encode(
        pool_counts, prev_feat, own_feat, next_feat, enc_b, enc_bias[None], gain_one[None], qkv_cols, cp, ka, cols, hs**-0.5)
    attn_group, lse = attend(key_pos, query, bias_rows, kaug, vt, hl, hs)
    attn_rows = lax.all_to_all(attn_group[:, :cols], "heads", split_axis=0, concat_axis=1, tiled=True)

    resid_in = jnp.dot(features, enc_b, preferred_element_type=f32) + enc_bias
    hidden_one = resid_in + jnp.dot(attn_rows, out_b, preferred_element_type=f32)
    norm_two, norm_two_pull = jax.vjp(normalize, hidden_one)
    act_two = low(norm_two * gain_two)
    up_val = jnp.dot(act_two, up_b, preferred_element_type=f32)
    gelu_val, gelu_pull = jax.vjp(jax.nn.gelu, up_val)
    act_up = low(gelu_val)
    hidden_two = hidden_one + jnp.dot(act_up, down_b, preferred_element_type=f32)
    norm_three, norm_three_pull = jax.vjp(normalize, hidden_two)
    scaled = norm_three * gain_three
    predicted = jnp.sum(scaled * head_vec, axis=-1)
    pred_error = predicted - target
    local_loss = jnp.sum(row_live * pred_error * pred_error)
    total_loss = lax.psum(local_loss, ("nodes", "heads"))
    grad_pred = 2.0 * row_live * pred_error / live_total
    grad_scaled = grad_pred[:, None] * head_vec
    grad_head_vec = jnp.sum(grad_pred[:, None] * scaled, axis=0)
    grad_gain_three = jnp.sum(grad_scaled * norm_three, axis=0)
    grad_two = norm_three_pull(grad_scaled * gain_three)[0]
    grad_two_low = low(grad_two)
    grad_down = jnp.einsum("rf,rd->fd", act_up, grad_two_low, preferred_element_type=f32)
    grad_act = jnp.einsum("rd,fd->rf", grad_two_low, down_b, preferred_element_type=f32)
    grad_up_low = low(gelu_pull(grad_act)[0])
    grad_up = jnp.einsum("rd,rf->df", act_two, grad_up_low, preferred_element_type=f32)
    grad_act_two = jnp.einsum("rf,df->rd", grad_up_low, up_b, preferred_element_type=f32)
    grad_gain_two = jnp.sum(grad_act_two * norm_two, axis=0)
    grad_one = grad_two + norm_two_pull(grad_act_two * gain_two)[0]
    grad_one_low = low(grad_one)
    grad_out = jnp.einsum("rc,rd->cd", attn_rows, grad_one_low, preferred_element_type=f32)
    grad_attn = low(jnp.einsum("rd,cd->rc", grad_one_low, out_b, preferred_element_type=f32))

    grad_heads = lax.all_to_all(grad_attn, "heads", split_axis=1, concat_axis=0, tiled=True)
    grad_heads = jnp.pad(grad_heads, ((0, 0), (0, cp - cols)))
    dq, dkv, edge_sums = attend_back(key_pos, query, grad_heads, attn_group, lse, bias_rows, kaug, value, kt, hl, hs)
    slot_sums = jnp.sum(edge_sums.reshape(group_blocks, slots, hl, BLOCK), axis=3)
    edge_grad = jnp.einsum("bst,bsh->th", kind_hot, slot_sums, precision=highest)
    columns = lambda a: jnp.broadcast_to(a[:, None], (D, 128))
    dw, denc_t, dgain, dbias = encode_back(
        prev_feat, own_feat, next_feat, dkv, dq, enc_b.T, columns(enc_bias), columns(gain_one), qkv_cols[:, :cp], qkv_cols[:, cp:])

    grad_qkv = jnp.transpose(dw.reshape(D, 3, cp)[:, :, :cols].reshape(D, 3, hl, hs), (0, 2, 1, 3)).reshape(D, 3 * cols)
    grad_gain_one = jnp.sum(dgain, axis=1)
    grad_enc_bias = jnp.sum(dbias, axis=1) + jnp.sum(grad_one, axis=0)
    grad_enc = denc_t.T + jnp.einsum("rf,rd->fd", features, grad_one_low, preferred_element_type=f32)
    edge_full = lax.dynamic_update_slice(jnp.zeros((kinds, HEADS), f32), edge_grad, (jnp.int32(0), head_index * hl))
    grad_vec = jnp.stack([grad_enc_bias, grad_gain_one, grad_gain_two, grad_gain_three, grad_head_vec, edge_full.reshape(D)])

    vec_rows = jnp.transpose(grad_vec.reshape(6, heads_count, -1), (1, 0, 2))

    def reduced(gradient, like):
        piece = lax.psum_scatter(spread_flat(gradient, heads_count, nodes_count), ("nodes", "heads"), scatter_dimension=0, tiled=True)
        return lax.all_gather(piece, "nodes", axis=0, tiled=True).reshape(like.shape)

    qkv_part = lax.all_to_all(grad_qkv, "heads", split_axis=0, concat_axis=1, tiled=True)
    summed = (
        reduced(grad_enc, enc_weight), lax.psum(qkv_part, "nodes"), reduced(grad_out, out_weight), reduced(grad_up, up_weight),
        reduced(grad_down, down_weight), reduced(vec_rows, vec_weight),
    )
    enc_res = adamw(enc_weight, enc_first, enc_second, summed[0])
    qkv_res = adamw(qkv_weight, qkv_first, qkv_second, summed[1])
    out_res = adamw(out_weight, out_first, out_second, summed[2])
    up_res = adamw(up_weight, up_first, up_second, summed[3])
    down_res = adamw(down_weight, down_first, down_second, summed[4])
    vec_res = adamw(vec_weight, vec_first, vec_second, summed[5])
    loss_value = (total_loss / live_total).reshape(1)
    return (
        loss_value, *enc_res, *qkv_res, *out_res, *up_res, *down_res, *vec_res,
        low(enc_res[0]), low(qkv_res[0]), low(out_res[0]), low(up_res[0]), low(down_res[0]),
    )


def solution(mesh):
    rows = P("heads", None)
    both = P(("nodes", "heads"))
    lanes = P(None, "heads")
    in_specs = (P(("nodes", "heads"), None), both, P(), P("nodes", None), P("nodes", None)) + (rows,) * 15 + (lanes,) * 3
    out_specs = (P(),) + (rows,) * 15 + (lanes,) * 3 + (rows,) * 5
    return jax.shard_map(local, mesh=mesh, in_specs=in_specs, out_specs=out_specs, check_vma=False)
```

time: 1470 us -> 798 us (0.54)
  local copies, waits for them, and re-layouts: 423 us -> 68.8 us
  waiting for transfers between devices: 485 us -> 237 us
  Pallas kernels: 0 us -> 206 us
  other arithmetic: 193 us -> 27.2 us
  matrix products: 169 us -> 49.3 us
  blocking collectives: 144 us -> 170 us
    pallas_call x0 -> x4, Pallas kernels: none -> 206 us  [the longest x1 81.2 us: attend_back(): pl.pallas_call(functools.partial(attend_back_kernel, hl, hs, cp, ka, slot...]
    all_to_all x4 -> x3, waiting for transfers between devices: 171 us -> 0.01 us  [the longest x1 0.01 us: local(): lax.all_to_all(grad_attn, 'heads', split_axis=1, concat_axis=0, tiled=True)]
    dot_general x78 -> x12, matrix products: 169 us -> 49 us  [the longest x1 9.88 us: local(): jnp.einsum('rf,rd->fd', act_up, grad_two_low, preferred_element_type=f32)]
    scatter-add x8 -> x0, other arithmetic: 114 us -> none  [back_step(): pool_grad = pool_grad.at[pos_part.reshape(-1)].add(contrib)]
    concatenate x9 -> x1, local copies, waits for them, and re-layouts: 75.7 us -> 0.08 us  [local(): key_pos = jnp.concatenate([self_pos[:, None], nbr_pos], axis=1).reshape(-1)]
    gather x33 -> x0, local copies, waits for them, and re-layouts: 65.5 us -> none  [the longest x32 63.1 us: fetch_keys(): source[pos_part].reshape(4, slot_count * BLOCK, head_local, 2 * head_size)]
    unnamed x7 -> x8, waiting for transfers between devices: 235 us -> 179 us
    while x125 -> x0, local copies, waits for them, and re-layouts: 48 us -> none
  transfers between devices with their start and end apart: 14 -> 12, of which waited for: 10 -> 3; matrix products, arithmetic and copies ran while one was open for 16% -> 13% of each run, Pallas kernels for 0% -> 10%
where the time goes in v1:
time: 798 us; the launch traced here: 791 us
  waiting for transfers between devices  237 us (30%)
  Pallas kernels  206 us (26%)
  blocking collectives  170 us (21%)
  local copies, waits for them, and re-layouts  68.8 us (9%)
  matrix products  49.3 us (6%)
  other arithmetic  27.2 us (3%)
  between operations  18.4 us (2%)
  starting transfers between devices  14.3 us (2%)
    unnamed x8, waiting for transfers between devices  179 us
    pallas_call x1, Pallas kernels, attend_back(): pl.pallas_call(functools.partial(attend_back_kernel, hl, hs, cp, ka, slot...  81.2 us
    all_gather x3, blocking collectives, local(): lax.all_gather(low(a), 'heads', axis=axis, tiled=True)  70.7 us
    pallas_call x1, Pallas kernels, encode_back(): pl.pallas_call(functools.partial(encode_back_kernel, cp, per), grid=(3 *...  48.8 us
    all_gather x1, waiting for transfers between devices, local(): own_feat = lax.all_gather(features, 'heads', axis=0, tiled=True)  47.8 us
    pallas_call x1, Pallas kernels, attend(): pl.pallas_call(functools.partial(attend_kernel, hl, hs, cp, ka, slots), g...  44.1 us
    psum x1, blocking collectives, local(): total_loss = lax.psum(local_loss, ('nodes', 'heads'))  40.6 us
    pallas_call x1, Pallas kernels, encode(): pl.pallas_call(functools.partial(encode_kernel, cp, ka, cols, scale, per)...  32 us
  transfers between devices with their start and end apart: 12, of which 3 were waited for; matrix products, arithmetic and copies ran while one was open for 13% of the time, Pallas kernels for 10%

profile of v1, /device:TPU:0, one launch (start us, length us, event | category | flops | bytes accessed | tf_op | source)
XLA Modules:
  0.0 791.1 jit_solution(2228486660683490712)
XLA Ops:
  10.2 47.8 %all-gather.6.cloned.1.call-done.fo_ref = bf16[4096,256]{1,0:T(8,128)(2,1)} async-done(((bf16[1024,256]{1,0:T(8,128)(2,1)}), bf16[4096,256]{1,0:T(8,128)(2,1)}) %all-gather.6.cloned.1.call-update) | async-done | bytes 2097168 | tf_op jit(solution)/shard_map/all_gather | solution.py:349
  62.7 3.5 all-to-all-start
  67.2 28.3 %all_gather.34 = bf16[6,512]{1,0:T(8,128)(2,1)S(1)} all-gather(bf16[6,128]{1,0:T(8,128)(2,1)S(1)} %convert_element_type.61), channel_id=1, replica_groups=mesh['nodes'=8,'heads'=4] {'heads'}, dimensions={1}, use_global_device_ids=true | all-gather | bytes 7680 | tf_op jit(solution)/shard_map/all_gather | solution.py:347
  99.6 16.4 %all_gather.33.enc_ref = bf16[256,512]{1,0:T(8,128)(2,1)} all-gather(bf16[64,512]{1,0:T(8,128)(2,1)S(1)} %convert_element_type.60), channel_id=1, replica_groups=mesh['nodes'=8,'heads'=4] {'heads'}, dimensions={0}, use_global_device_ids=true | all-gather | bytes 327680 | tf_op jit(solution)/shard_map/all_gather | solution.py:347
  121.1 32.0 %encode.1 = (bf16[12288,256]{1,0:T(8,128)(2,1)}, bf16[96,128,128]{2,1,0:T(8,128)(2,1)}, bf16[12288,128]{1,0:T(8,128)(2,1)}, bf16[96,128,128]{2,1,0:T(8,128)(2,1)}, bf16[4096,128]{1,0:T(8,128)(2,1)}) custom-call(s32[96]{0:T(128)} %pad_add_fusion.1.cnt_ref, bf16[4096,256]{1,0:T(8,128)(2,1)} %copy-done.3, ...), custom_call_target="tpu_custom_call" | custom-call | tf_op jit(solution)/shard_map/encode/pallas_call | solution.py:196
  153.1 44.1 %attend.1 = (bf16[4096,128]{1,0:T(8,128)(2,1)}, f32[32,1,256]{2,1,0:T(1,128)}) custom-call(s32[288]{0:T(512)} %reshape.224.pos_ref, bf16[4096,128]{1,0:T(8,128)(2,1)} %get-tuple-element.38.q_ref, f32[32,9,256]{2,1,0:T(8,128)} %copy.124.brow_ref, bf16[12288,256]{1,0:T(8,128)(2,1)} %get-tuple-element.39.kaug_ref, bf16[96,128,128]{2,1,0:T(8,128)(2,1)} %get-tuple-element.40.vt_ref), custom_call_target="tpu_custom_call" | custom-call | tf_op jit(solution)/shard_map/attend/pallas_call | solution.py:72
  199.5 3.6 all-to-all-start.1
  205.5 26.0 %all_gather.36 = bf16[512,512]{1,0:T(8,128)(2,1)S(1)} all-gather(bf16[128,512]{1,0:T(8,128)(2,1)S(1)} %convert_element_type.64), channel_id=1, replica_groups=mesh['nodes'=8,'heads'=4] {'heads'}, dimensions={0}, use_global_device_ids=true | all-gather | bytes 655360 | tf_op jit(solution)/shard_map/all_gather | solution.py:347
  239.1 7.3 fusion.38
  246.5 8.2 %fusion.55 = (f32[1024]{0:T(1024)S(1)}, f32[1024,512]{0,1:T(8,128)S(1)}) fusion(f32[1024,512]{0,1:T(8,128)} %copy-done, bf16[2048,512]{1,0:T(8,128)(2,1)} %all-gather.10.cloned.1.call-done, f32[1024,2048]{1,0:T(8,128)} %fusion.38), kind=kOutput, calls=%fused_computation.124 | convolution fusion | flops 2167405568 | bytes 14684160 | tf_op jit(solution)/shard_map/dot_general | solution.py:389
  257.7 7.8 fusion.6
  265.5 2.7 multiply_reduce_fusion.1
  275.3 4.3 all-to-all-start.2
  279.6 9.9 %fusion.16 = f32[2048,512]{1,0:T(8,128)} fusion(f32[1024]{0:T(1024)S(1)} %negate_multiply_fusion.1, f32[1024,2048]{1,0:T(8,128)} %fusion.38, f32[1024,512]{0,1:T(8,128)S(1)} %get-tuple-element.150, f32[1024]{0:T(1024)S(1)} %multiply_multiply_fusion.11, f32[1024]{0:T(1024)S(1)} %get-tuple-element.137, f32[512]{0:T(512)S(1)} %bitcast.133, ...), kind=kOutput, calls=%fused_computation.50 | convolution fusion | flops 2171076608 | bytes 14704640 | tf_op jit(solution)/shard_map/rf,rd->fd/dot_general | solution.py:402
  289.5 5.1 reshape.238
  294.6 4.9 copy.172
  299.5 2.7 copy.165
  303.8 4.3 fusion.37
  308.2 5.0 reshape.235
  313.2 4.9 copy.173
  326.2 81.2 %attend_back.1 = (bf16[4096,128]{1,0:T(8,128)(2,1)}, f32[12288,256]{1,0:T(8,128)}, f32[32,9,256]{2,1,0:T(8,128)}) custom-call(s32[288]{0:T(512)} %reshape.224.pos_ref, bf16[4096,128]{1,0:T(8,128)(2,1)} %get-tuple-element.38.q_ref, bf16[4096,128]{1,0:T(8,128)(2,1)} %bitcast.16.do_ref, bf16[4096,128]{1,0:T(8,128)(2,1)} %get-tuple-element.41.o_ref, ...), custom_call_target="tpu_custom_call" | custom-call | tf_op jit(solution)/shard_map/attend_back/pallas_call | solution.py:132
  409.0 48.8 %encode_back.1 = (f32[512,384]{1,0:T(8,128)}, f32[512,256]{1,0:T(8,128)}, f32[512,128]{1,0:T(8,128)}, f32[512,128]{1,0:T(8,128)}) custom-call(bf16[4096,256]{1,0:T(8,128)(2,1)} %copy-done.3, bf16[4096,256]{1,0:T(8,128)(2,1)} %all-gather.6.cloned.1.call-done.fo_ref, bf16[4096,256]{1,0:T(8,128)(2,1)} %collective-permute-done.1.fn_ref, ...), custom_call_target="tpu_custom_call" | custom-call | tf_op jit(solution)/shard_map/encode_back/pallas_call | solution.py:273
  462.3 27.6 %all_to_all.73 = f32[4,128,384]{1,2,0:T(8,128)} all-to-all(f32[4,128,384]{1,2,0:T(8,128)S(1)} %copy.137), channel_id=1, replica_groups=mesh['nodes'=8,'heads'=4] {'heads'}, dimensions={0} | all-to-all | bytes 1572864 | tf_op jit(solution)/shard_map/all_to_all | solution.py:435
  490.0 177.9 %all-reduce.13.cloned.1.call-done = (f32[131072]{0:T(1024)}, f32[262144]{0:T(1024)}, f32[1048576]{0:T(1024)}, f32[1048576]{0:T(1024)}) async-done(((f32[131072]{0:T(1024)}, f32[262144]{0:T(1024)}, f32[1048576]{0:T(1024)}, f32[1048576]{0:T(1024)}), (f32[131072]{0:T(1024)}, f32[262144]{0:T(1024)}, f32[1048576]{0:T(1024)}, f32[1048576]{0:T(1024)})) %all-reduce.13.cloned.1.call-update) | async-done | bytes 9961488
  675.6 40.6 %all-reduce.6 = (f32[]{:T(128)}, f32[3072]{0:T(1024)S(1)}) all-reduce(f32[]{:T(128)} %get-tuple-element.138, f32[3072]{0:T(1024)S(1)} %reshape.243), channel_id=1, replica_groups=mesh['nodes'=8,'heads'=4] {'nodes','heads'}, use_global_device_ids=true, to_apply=%region_6.7 | all-reduce | flops 3073 | bytes 24584 | tf_op jit(solution)/shard_map/psum | solution.py:395
  717.0 13.2 %all-reduce = f32[768]{0:T(1024)S(1)} all-reduce(f32[768]{0:T(1024)S(1)} %dynamic-slice_dynamic-update-slice_fusion), channel_id=1, replica_groups=mesh['nodes'=8,'heads'=4] {'nodes'}, use_global_device_ids=true, to_apply=%add | all-reduce | flops 768 | bytes 6144
  732.4 2.9 fusion.46
  741.7 10.0 %all_gather.40 = f32[65536]{0:T(1024)S(1)} all-gather(f32[8192]{0:T(1024)S(1)} %dynamic-slice.2), channel_id=1, replica_groups=mesh['nodes'=8,'heads'=4] {'nodes'}, dimensions={0}, use_global_device_ids=true | all-gather | bytes 294912 | tf_op jit(solution)/shard_map/all_gather | solution.py:433
  752.5 8.4 %all_gather.39 = f32[32768]{0:T(1024)S(1)} all-gather(f32[4096]{0:T(1024)S(1)} %dynamic-slice.1), channel_id=1, replica_groups=mesh['nodes'=8,'heads'=4] {'nodes'}, dimensions={0}, use_global_device_ids=true | all-gather | bytes 147456 | tf_op jit(solution)/shard_map/all_gather | solution.py:433
  764.2 3.6 fusion.40
  767.9 10.0 %all-gather.12.cloned.1.call-done = f32[262144]{0:T(1024)} async-done(((f32[32768]{0:T(1024)}), f32[262144]{0:T(1024)}) %all-gather.12.cloned.1.call-update) | async-done | bytes 1048592 | tf_op jit(solution)/shard_map/all_gather | solution.py:433
  779.3 3.6 fusion.42
  (222 shorter events, 76.0 us)
Async XLA Ops:
  7.2 50.8 %all-gather.6.cloned.1.call-start = ((), (), s32[]{:S(2)}) async-start(), calls=%async_computation.4 | async-start | bytes 2621440 | tf_op jit(solution)/shard_map/all_gather | solution.py:349
  7.9 58.4 %copy-start.5 = (f32[512,512]{1,0:T(8,128)S(1)}, f32[512,512]{1,0:T(8,128)}, u32[]{:S(2)}) copy-start(f32[512,512]{1,0:T(8,128)} %param.40) | copy-start | bytes 3145732
  7.9 230.8 %all-gather.8.cloned.1.call-start = ((), (), s32[]{:S(2)}) async-start(), calls=%async_computation.5 | async-start | bytes 2621440 | tf_op jit(solution)/shard_map/all_gather | solution.py:347
  58.0 61.8 %collective-permute-start = (bf16[4096,256]{1,0:T(8,128)(2,1)}, bf16[4096,256]{1,0:T(8,128)(2,1)S(1)}, u32[]{:S(2)}, u32[]{:S(2)}) collective-permute-start(bf16[4096,256]{1,0:T(8,128)(2,1)} %all-gather.6.cloned.1.call-done.fo_ref), channel_id=1, source_target_pairs={{0,4},{4,8},{8,12},{12,16},{16,20},{20,24},{24,28},{28,0},{1,5},{5... | collective-permute-start | bytes 6291464 | tf_op jit(solution)/shard_map/ppermute | solution.py:322
  58.0 61.8 %collective-permute-start.1 = (bf16[4096,256]{1,0:T(8,128)(2,1)}, bf16[4096,256]{1,0:T(8,128)(2,1)}, u32[]{:S(2)}, u32[]{:S(2)}) collective-permute-start(bf16[4096,256]{1,0:T(8,128)(2,1)} %all-gather.6.cloned.1.call-done.fo_ref), channel_id=1, source_target_pairs={{0,28},{4,0},{8,4},{12,8},{16,12},{20,16},{24,20},{28,24},{1,29},{... | collective-permute-start | bytes 6291464 | tf_op jit(solution)/shard_map/ppermute | solution.py:322
  61.8 37.5 %copy-start.30 = (s32[32,9]{0,1:T(8,128)S(1)}, s32[32,9]{0,1:T(8,128)}, u32[]{:S(2)}) copy-start(s32[32,9]{0,1:T(8,128)} %param.27) | copy-start | bytes 3460
  62.7 55.6 %all-to-all-start = ((bf16[128,4,384]{0,2,1:T(8,128)(2,1)}), bf16[128,4,384]{0,2,1:T(8,128)(2,1)S(1)}, u32[]{:S(2)}, u32[]{:S(2)}) async-start(bf16[128,4,384]{0,2,1:T(8,128)(2,1)} %bitcast.116), calls=%async_computation | async-start | bytes 786432 | tf_op jit(solution)/shard_map/all_to_all | solution.py:354
  66.2 180.2 %all-gather.10.cloned.1.call-start = ((), (), s32[]{:S(2)}) async-start(), calls=%async_computation.6 | async-start | bytes 2621440 | tf_op jit(solution)/shard_map/all_gather | solution.py:347
  199.5 32.0 %copy-start.4 = (bf16[1024,256]{1,0:T(8,128)(2,1)S(1)}, bf16[1024,256]{1,0:T(8,128)(2,1)}, u32[]{:S(2)}) copy-start(bf16[1024,256]{1,0:T(8,128)(2,1)} %param.23) | copy-start | bytes 1572868
  199.5 35.2 %all-to-all-start.1 = ((bf16[4,1024,128]{1,2,0:T(8,128)(2,1)}), bf16[4,1024,128]{1,2,0:T(8,128)(2,1)S(1)}, u32[]{:S(2)}, u32[]{:S(2)}) async-start(bf16[4,1024,128]{1,2,0:T(8,128)(2,1)} %copy.125), calls=%async_computation.1 | async-start | bytes 2097152 | tf_op jit(solution)/shard_map/all_to_all | solution.py:380
  204.7 28.7 %copy-start.13 = (bf16[512,384]{1,0:T(8,128)(2,1)S(1)}, bf16[512,384]{1,0:T(8,128)(2,1)}, u32[]{:S(2)}) copy-start(bf16[512,384]{1,0:T(8,128)(2,1)} %copy.121.w_ref) | copy-start | bytes 1179652
  205.5 30.2 %copy-start.29 = (f32[1,512]{1,0:T(1,128)S(1)}, f32[1,512]{1,0:T(1,128)}, u32[]{:S(2)}) copy-start(f32[1,512]{1,0:T(1,128)} %get-tuple-element.143.bias_ref) | copy-start | bytes 6148
  275.3 50.9 %all-to-all-start.2 = ((bf16[1024,4,128]{2,0,1:T(8,128)(2,1)}), bf16[1024,4,128]{2,0,1:T(8,128)(2,1)}, u32[]{:S(2)}, u32[]{:S(2)}) async-start(bf16[1024,4,128]{2,0,1:T(8,128)(2,1)} %copy.127), calls=%async_computation.2 | async-start | bytes 2097152 | tf_op jit(solution)/shard_map/all_to_all | solution.py:413
  279.5 388.3 %all-reduce.13.cloned.1.call-start = ((), (), s32[]{:S(2)}) async-start(), calls=%async_computation.10 | async-start | bytes 19922944
  326.1 82.1 %copy-start.31 = (f32[1,512]{1,0:T(1,128)S(1)}, f32[1,512]{1,0:T(1,128)}, u32[]{:S(2)}) copy-start(f32[1,512]{1,0:T(1,128)} %get-tuple-element.142.gain_ref) | copy-start | bytes 6148
  460.5 272.0 %all-reduce.11.cloned.1.call-start = ((), (), s32[]{:S(2)}) async-start(), calls=%async_computation.7 | async-start | bytes 1572864 | tf_op jit(solution)/shard_map/psum | solution.py:437
  462.2 207.3 %copy-start.14 = (f32[128,1536]{1,0:T(8,128)S(1)}, f32[128,1536]{1,0:T(8,128)}, u32[]{:S(2)}) copy-start(f32[128,1536]{1,0:T(8,128)} %param.31) | copy-start | bytes 2359300
  462.3 207.5 %copy-start.20 = (f32[128,1536]{1,0:T(8,128)S(1)}, f32[128,1536]{1,0:T(8,128)}, u32[]{:S(2)}) copy-start(f32[128,1536]{1,0:T(8,128)} %param.32) | copy-start | bytes 2359300
  489.9 180.2 %copy-start.21 = (f32[128,1536]{1,0:T(8,128)S(1)}, f32[128,1536]{1,0:T(8,128)}, u32[]{:S(2)}) copy-start(f32[128,1536]{1,0:T(8,128)} %param.33) | copy-start | bytes 2359300
  489.9 272.9 %all-gather.14.cloned.1.call-start = ((), (), s32[]{:S(2)}) async-start(), calls=%async_computation.9 | async-start | bytes 1179648 | tf_op jit(solution)/shard_map/all_gather | solution.py:433
  669.5 108.4 %all-gather.12.cloned.1.call-start = ((), (), s32[]{:S(2)}) async-start(), calls=%async_computation.8 | async-start | bytes 1179648 | tf_op jit(solution)/shard_map/all_gather | solution.py:433
  670.1 61.7 %copy-start.33 = (f32[6,128]{1,0:T(8,128)S(1)}, f32[6,128]{1,0:T(8,128)}, u32[]{:S(2)}) copy-start(f32[6,128]{1,0:T(8,128)} %param.43) | copy-start | bytes 9220
  670.1 61.7 %copy-start.37 = (f32[6,128]{1,0:T(8,128)S(1)}, f32[6,128]{1,0:T(8,128)}, u32[]{:S(2)}) copy-start(f32[6,128]{1,0:T(8,128)} %param.44) | copy-start | bytes 9220
  670.1 61.7 %copy-start.38 = (f32[6,128]{1,0:T(8,128)S(1)}, f32[6,128]{1,0:T(8,128)}, u32[]{:S(2)}) copy-start(f32[6,128]{1,0:T(8,128)} %param.45) | copy-start | bytes 9220
  738.8 22.0 %copy-start.23 = (f32[64,512]{1,0:T(8,128)S(1)}, f32[64,512]{1,0:T(8,128)}, u32[]{:S(2)}) copy-start(f32[64,512]{1,0:T(8,128)} %param.28) | copy-start | bytes 393220
  738.8 22.0 %copy-start.27 = (f32[64,512]{1,0:T(8,128)S(1)}, f32[64,512]{1,0:T(8,128)}, u32[]{:S(2)}) copy-start(f32[64,512]{1,0:T(8,128)} %param.29) | copy-start | bytes 393220
  738.8 22.1 %copy-start.28 = (f32[64,512]{1,0:T(8,128)S(1)}, f32[64,512]{1,0:T(8,128)}, u32[]{:S(2)}) copy-start(f32[64,512]{1,0:T(8,128)} %param.30) | copy-start | bytes 393220
  738.8 22.9 %copy-start.19 = (f32[128,512]{1,0:T(8,128)S(1)}, f32[128,512]{1,0:T(8,128)}, u32[]{:S(2)}) copy-start(f32[128,512]{1,0:T(8,128)} %param.34) | copy-start | bytes 786436
  738.8 22.9 %copy-start.24 = (f32[128,512]{1,0:T(8,128)S(1)}, f32[128,512]{1,0:T(8,128)}, u32[]{:S(2)}) copy-start(f32[128,512]{1,0:T(8,128)} %param.35) | copy-start | bytes 786436
  738.8 22.9 %copy-start.25 = (f32[128,512]{1,0:T(8,128)S(1)}, f32[128,512]{1,0:T(8,128)}, u32[]{:S(2)}) copy-start(f32[128,512]{1,0:T(8,128)} %param.36) | copy-start | bytes 786436
  767.9 11.4 %copy-start.7 = (f32[128,2048]{1,0:T(8,128)S(1)}, f32[128,2048]{1,0:T(8,128)}, u32[]{:S(2)}) copy-start(f32[128,2048]{1,0:T(8,128)} %param.37) | copy-start | bytes 3145732
  767.9 11.4 %copy-start.17 = (f32[128,2048]{1,0:T(8,128)S(1)}, f32[128,2048]{1,0:T(8,128)}, u32[]{:S(2)}) copy-start(f32[128,2048]{1,0:T(8,128)} %param.38) | copy-start | bytes 3145732
  (25 other events, 93.8 us)
Sparse Core Ops, SparseCore 0:
  9.6 48.3 all-gather.5
  60.1 55.4 all-gather.7
  117.8 44.0 all-gather.9
  460.6 207.2 all-reduce.12
  670.9 55.7 all-reduce.10
  729.0 23.3 all-gather.13
  754.8 23.0 all-gather.11

commit v2 on v1

--- a/solution.py
+++ b/solution.py
@@ -81,6 +81,7 @@
             scratch_shapes=[pltpu.VMEM((slots, BLOCK, rows), f32), pltpu.VMEM((slots * BLOCK, rows), bf16)]),
         out_shape=[jax.ShapeDtypeStruct(q.shape, bf16), jax.ShapeDtypeStruct((nb, 1, rows), f32)],
         compiler_params=pltpu.CompilerParams(vmem_limit_bytes=60 << 20),
+        cost_estimate=pl.CostEstimate(flops=nb * 10**9, bytes_accessed=3 * 10**7, transcendentals=0),
         name="attend",
     )(pos, q, brow, kaug, vt)
 
@@ -142,6 +143,7 @@
         out_shape=[jax.ShapeDtypeStruct(q.shape, bf16), jax.ShapeDtypeStruct((v.shape[0], 2 * cp), f32),
                    jax.ShapeDtypeStruct((nb, slots, rows), f32)],
         compiler_params=pltpu.CompilerParams(vmem_limit_bytes=60 << 20),
+        cost_estimate=pl.CostEstimate(flops=nb * 2 * 10**9, bytes_accessed=6 * 10**7, transcendentals=0),
         name="attend_back",
     )(pos, q, do, o, lse, brow, kaug, v, kt)
 norm_eps = 1e-05
@@ -210,6 +212,7 @@
                    jax.ShapeDtypeStruct((3 * rows // BLOCK, cp, BLOCK), bf16),
                    jax.ShapeDtypeStruct((rows, cp), bf16)],
         compiler_params=pltpu.CompilerParams(vmem_limit_bytes=60 << 20),
+        cost_estimate=pl.CostEstimate(flops=rows * 6 * 10**6, bytes_accessed=3 * 10**7, transcendentals=0),
         name="encode",
     )(counts, prev, own, nxt, enc, bias, gain, w)
 
@@ -280,8 +283,120 @@
         out_shape=[jax.ShapeDtypeStruct(s, f32) for s in shapes],
         scratch_shapes=[pltpu.VMEM((tile, feat), bf16), pltpu.VMEM((width, tile), f32)],
         compiler_params=pltpu.CompilerParams(vmem_limit_bytes=60 << 20),
+        cost_estimate=pl.CostEstimate(flops=rows * 10**7, bytes_accessed=4 * 10**7, transcendentals=0),
         name="encode_back",
     )(prev, own, nxt, dkv, dq, enct, bias, gain, wq, wkv)
+MESH = pl.DeviceIdType.MESH
+
+
+def send(src, dst, sems, slot, node, head):
+    copy = pltpu.make_async_remote_copy(
+        src_ref=src, dst_ref=dst, send_sem=sems[0].at[slot], recv_sem=sems[1].at[slot], device_id=(node, head), device_id_type=MESH)
+    copy.start()
+    return copy
+
+
+def greet(nodes, heads, node, head):
+    barrier = pltpu.get_barrier_semaphore()
+    for s in range(1, nodes):
+        pl.semaphore_signal(barrier, inc=1, device_id=(lax.rem(node + s, nodes), head), device_id_type=MESH)
+    for s in range(1, heads):
+        pl.semaphore_signal(barrier, inc=1, device_id=(node, lax.rem(head + s, heads)), device_id_type=MESH)
+    pl.semaphore_wait(barrier, nodes + heads - 2)
+
+
+def finish_kernel(nodes, heads, *refs):
+    (qkv, enc, vec, *bulk), refs = refs[:6], refs[6:]
+    (out_q, out_e, out_v, *out_b), refs = refs[:6], refs[6:]
+    (q_half, q_one, q_two, q_part, q_sum, q_own, e_half, e_one, e_two, e_sum, e_three, e_own, v_half, v_two, v_three, v_one, v_sum), refs = refs[:17], refs[17:]
+    s_one, r_one, s_two, r_two, s_three, r_three, s_four, r_four, s_bulk, r_bulk, s_pass, r_pass, l_sem = refs
+    node, head = lax.axis_index("nodes"), lax.axis_index("heads")
+    chips = nodes // 2
+    chip, side = lax.div(node, 2), lax.rem(node, 2)
+    twin = chip * 2 + 1 - side
+    greet(nodes, heads, node, head)
+    first = [send(ref.at[:, :, 1 - side], dst, (s_one, r_one), i, twin, head) for i, (ref, dst) in enumerate(((qkv, q_half), (enc, e_half)))]
+    first.append(send(vec, v_half, (s_one, r_one), 2, twin, head))
+    keep = [pltpu.make_async_copy(src, dst.at[node], l_sem.at[i]) for i, (src, dst) in enumerate(zip(bulk, out_b))]
+    for copy in keep:
+        copy.start()
+    spread = []
+    for s in range(chips):
+        other = lax.rem(chip + s, chips) * 2 + side if s else twin
+        spread.append([send(src, dst.at[node], (s_bulk, r_bulk), s * 3 + i, other, head) for i, (src, dst) in enumerate(zip(bulk, out_b))])
+    for copy in first:
+        copy.wait()
+    q_one[...] = qkv[:, :, side] + q_half[...]
+    e_one[...] = enc[:, :, side] + e_half[...]
+    v_one[...] = vec[...] + v_half[...]
+    second = []
+    for s in range(1, chips):
+        there = lax.rem(chip + s, chips)
+        target = there * 2 + side
+        i = (s - 1) * 3
+        second.append(send(q_one.at[:, there], q_two.at[s - 1], (s_two, r_two), i, target, head))
+        second.append(send(e_one.at[:, there], e_two.at[s - 1], (s_two, r_two), i + 1, target, head))
+        second.append(send(v_one, v_two.at[s - 1], (s_two, r_two), i + 2, target, head))
+    for copy in second:
+        copy.wait()
+    q_part[...] = functools.reduce(jnp.add, [q_two[s] for s in range(chips - 1)], q_one[:, chip])
+    e_sum[...] = functools.reduce(jnp.add, [e_two[s] for s in range(chips - 1)], e_one[:, chip])
+    v_sum[...] = functools.reduce(jnp.add, [v_two[s] for s in range(chips - 1)], v_one[...])
+    third = []
+    for s in range(1, heads):
+        there = lax.rem(head + s, heads)
+        i = (s - 1) * 3
+        third.append(send(q_part.at[there], q_sum.at[head], (s_three, r_three), i, node, there))
+        third.append(send(e_sum.at[there], e_three.at[s - 1], (s_three, r_three), i + 1, node, there))
+        third.append(send(v_sum, v_three.at[s - 1], (s_three, r_three), i + 2, node, there))
+    for copy in third:
+        copy.wait()
+    q_sum[pl.ds(head, 1)] = q_part[pl.ds(head, 1)]
+    e_own[...] = functools.reduce(jnp.add, [e_three[s] for s in range(heads - 1)], e_sum[head])
+    out_v[...] = functools.reduce(jnp.add, [v_three[s] for s in range(heads - 1)], v_sum[...])
+    fourth = []
+    for s in range(1, nodes):
+        there = lax.rem(node + s, nodes)
+        fourth.append(send(q_sum, out_q.at[node], (s_four, r_four), (s - 1) * 2, there, head))
+        fourth.append(send(e_own, out_e.at[node], (s_four, r_four), (s - 1) * 2 + 1, there, head))
+    out_q[node] = q_sum[...]
+    out_e[node] = e_own[...]
+    for copy in keep:
+        copy.wait()
+    passed = []
+    for s in range(chips):
+        for copy in spread[s]:
+            copy.wait()
+        if s:
+            origin = lax.rem(chip + chips - s, chips) * 2 + side
+            passed += [send(dst.at[origin], dst.at[origin], (s_pass, r_pass), (s - 1) * 3 + i, twin, head) for i, dst in enumerate(out_b)]
+    for copy in passed:
+        copy.wait()
+    for copy in fourth:
+        copy.wait()
+
+
+def finish(qkv, enc, vec, bulk, nodes, heads):
+    chips = nodes // 2
+    split = lambda a: a.reshape(heads, chips, 2, -1, a.shape[-1])
+    qkv, enc = split(qkv), split(enc)
+    vm = lambda *s: pltpu.VMEM(s, f32)
+    rq, wq, re, we = *qkv.shape[3:], *enc.shape[3:]
+    dma = pltpu.SemaphoreType.DMA
+    wv = vec.shape
+    scratch = [vm(heads, chips, rq, wq), vm(heads, chips, rq, wq), vm(chips - 1, heads, rq, wq), vm(heads, rq, wq), vm(heads, rq, wq), vm(8, 128),
+               vm(heads, chips, re, we), vm(heads, chips, re, we), vm(chips - 1, heads, re, we), vm(heads, re, we), vm(heads - 1, re, we), vm(re, we),
+               vm(*wv), vm(chips - 1, *wv), vm(heads - 1, *wv), vm(*wv), vm(*wv)]
+    counts = (3, 3, 3 * chips - 3, 3 * chips - 3, 3 * heads - 3, 3 * heads - 3, 2 * nodes - 2, 2 * nodes - 2, 3 * chips, 3 * chips, 3 * chips - 3, 3 * chips - 3, 3)
+    out_shape = [jax.ShapeDtypeStruct(s, f32) for s in [(nodes, heads, rq, wq), (nodes, re, we), wv] + [(nodes, *b.shape) for b in bulk]]
+    spec = pl.BlockSpec(memory_space=pltpu.VMEM)
+    return pl.pallas_call(
+        functools.partial(finish_kernel, nodes, heads),
+        in_specs=[spec] * 6, out_specs=[spec] * 6, out_shape=out_shape,
+        scratch_shapes=scratch + [dma((n,)) for n in counts],
+        compiler_params=pltpu.CompilerParams(collective_id=1, has_side_effects=True, vmem_limit_bytes=48 << 20),
+        name="finish",
+    )(qkv, enc, vec, *bulk)
 D = 512
 HEADS = 8
 NBR = 8
@@ -312,8 +427,27 @@
     return (weight_new, first_new, second_new)
 
 
-def spread_flat(gradient, heads_count, nodes_count):
-    return jnp.transpose(gradient.reshape(heads_count, nodes_count, -1), (1, 0, 2)).reshape(-1)
+def core_sum(gradient, heads_count, nodes_count):
+    node_index = lax.axis_index("nodes")
+    parts = gradient.reshape(heads_count, nodes_count // 2, 2, -1, gradient.shape[-1])
+    side = node_index % 2
+    kept = lax.dynamic_index_in_dim(parts, side, 2, False)
+    sent = lax.dynamic_index_in_dim(parts, 1 - side, 2, False)
+    return kept + lax.ppermute(sent, "nodes", [(i, i ^ 1) for i in range(nodes_count)])
+
+
+def chip_sum(parts, nodes_count):
+    chips = nodes_count // 2
+    chip = lax.axis_index("nodes") // 2
+    total = lax.dynamic_index_in_dim(parts, chip, 1, False)
+    for step in range(1, chips):
+        sent = lax.dynamic_index_in_dim(parts, chip ^ step, 1, False)
+        total = total + lax.ppermute(sent, "nodes", [(i, i ^ (2 * step)) for i in range(nodes_count)])
+    return total
+
+
+def plane_sum(parts):
+    return jnp.sum(lax.all_to_all(parts, "heads", split_axis=0, concat_axis=0, tiled=True), axis=0)
 
 
 def from_behind(value, axis, steps):
@@ -392,7 +526,6 @@
     predicted = jnp.sum(scaled * head_vec, axis=-1)
     pred_error = predicted - target
     local_loss = jnp.sum(row_live * pred_error * pred_error)
-    total_loss = lax.psum(local_loss, ("nodes", "heads"))
     grad_pred = 2.0 * row_live * pred_error / live_total
     grad_scaled = grad_pred[:, None] * head_vec
     grad_head_vec = jnp.sum(grad_pred[:, None] * scaled, axis=0)
@@ -419,24 +552,23 @@
     dw, denc_t, dgain, dbias = encode_back(
         prev_feat, own_feat, next_feat, dkv, dq, enc_b.T, columns(enc_bias), columns(gain_one), qkv_cols[:, :cp], qkv_cols[:, cp:])
 
-    grad_qkv = jnp.transpose(dw.reshape(D, 3, cp)[:, :, :cols].reshape(D, 3, hl, hs), (0, 2, 1, 3)).reshape(D, 3 * cols)
     grad_gain_one = jnp.sum(dgain, axis=1)
     grad_enc_bias = jnp.sum(dbias, axis=1) + jnp.sum(grad_one, axis=0)
     grad_enc = denc_t.T + jnp.einsum("rf,rd->fd", features, grad_one_low, preferred_element_type=f32)
     edge_full = lax.dynamic_update_slice(jnp.zeros((kinds, HEADS), f32), edge_grad, (jnp.int32(0), head_index * hl))
-    grad_vec = jnp.stack([grad_enc_bias, grad_gain_one, grad_gain_two, grad_gain_three, grad_head_vec, edge_full.reshape(D)])
-
-    vec_rows = jnp.transpose(grad_vec.reshape(6, heads_count, -1), (1, 0, 2))
-
-    def reduced(gradient, like):
-        piece = lax.psum_scatter(spread_flat(gradient, heads_count, nodes_count), ("nodes", "heads"), scatter_dimension=0, tiled=True)
-        return lax.all_gather(piece, "nodes", axis=0, tiled=True).reshape(like.shape)
-
-    qkv_part = lax.all_to_all(grad_qkv, "heads", split_axis=0, concat_axis=1, tiled=True)
-    summed = (
-        reduced(grad_enc, enc_weight), lax.psum(qkv_part, "nodes"), reduced(grad_out, out_weight), reduced(grad_up, up_weight),
-        reduced(grad_down, down_weight), reduced(vec_rows, vec_weight),
-    )
+    grad_vec = jnp.stack([grad_enc_bias, grad_gain_one, grad_gain_two, grad_gain_three, grad_head_vec, edge_full.reshape(D),
+                          jnp.full((D,), local_loss)])
+    def reduced(gradient):
+        return plane_sum(chip_sum(core_sum(gradient, heads_count, nodes_count), nodes_count))
+
+    dw_sum, enc_sum, vec_total, *bulk = finish(
+        dw, grad_enc, jnp.pad(grad_vec, ((0, 1), (0, 0))), [reduced(grad_out), reduced(grad_up), reduced(grad_down)], nodes_count, heads_count)
+    total_loss = vec_total[6, 0]
+    vec_sum = lax.dynamic_slice_in_dim(vec_total[:6], head_index * (D // heads_count), D // heads_count, 1)
+    qkv_sum = jnp.transpose(dw_sum, (0, 2, 1, 3)).reshape(-1, heads_count, 3, cp)[..., :cols].reshape(-1, heads_count, 3, hl, hs)
+    qkv_sum = jnp.transpose(qkv_sum, (0, 1, 3, 2, 4)).reshape(qkv_weight.shape)
+    flat = lambda a: a.reshape(-1, a.shape[-1])
+    summed = (flat(enc_sum), qkv_sum, flat(bulk[0]), flat(bulk[1]), flat(bulk[2]), vec_sum)
     enc_res = adamw(enc_weight, enc_first, enc_second, summed[0])
     qkv_res = adamw(qkv_weight, qkv_first, qkv_second, summed[1])
     out_res = adamw(out_weight, out_first, out_second, summed[2])

time: 798 us -> 585 us (0.73)
  waiting for transfers between devices: 237 us -> 72.9 us
  blocking collectives: 170 us -> 72.7 us
  Pallas kernels: 206 us -> 247 us
  starting transfers between devices: 14.3 us -> 39.6 us
  local copies, waits for them, and re-layouts: 68.8 us -> 47.4 us
  other arithmetic: 27.2 us -> 37.9 us
  matrix products: 49.3 us -> 40.2 us
    unnamed x8 -> x3, waiting for transfers between devices: 179 us -> 0.71 us
    pallas_call x0 -> x1, Pallas kernels: none -> 41.7 us  [finish(): pl.pallas_call(functools.partial(finish_kernel, nodes, heads), in_specs=[...]
    psum x1 -> x0, blocking collectives: 40.6 us -> none  [local(): total_loss = lax.psum(local_loss, ('nodes', 'heads'))]
    all_to_all x1 -> x0, blocking collectives: 27.6 us -> none  [local(): lax.all_to_all(grad_qkv, 'heads', split_axis=0, concat_axis=1, tiled=True)]
    reshape x13 -> x0, local copies, waits for them, and re-layouts: 25.1 us -> none  [the longest x8 22.2 us: spread_flat(): gradient.reshape(heads_count, nodes_count, -1)]
    ppermute x0 -> x12, waiting for transfers between devices: none -> 18.8 us  [the longest x9 18.8 us: chip_sum(): lax.ppermute(sent, 'nodes', [(i, i ^ 2 * step) for i in range(nodes_count)])]
    all_gather x2 -> x0, blocking collectives: 18.4 us -> none  [reduced(): lax.all_gather(piece, 'nodes', axis=0, tiled=True).reshape(like.shape)]
    all_to_all x0 -> x3, starting transfers between devices: none -> 15 us  [plane_sum(): lax.all_to_all(parts, 'heads', split_axis=0, concat_axis=0, tiled=True)]
  transfers between devices with their start and end apart: 12 -> 23, of which waited for: 3 -> 5; matrix products, arithmetic and copies ran while one was open for 13% -> 13% of each run, Pallas kernels for 10% -> 36%
where the time goes in v2:
time: 585 us; the launch traced here: 575 us
  Pallas kernels  247 us (42%)
  waiting for transfers between devices  72.9 us (12%)
  blocking collectives  72.7 us (12%)
  local copies, waits for them, and re-layouts  47.4 us (8%)
  matrix products  40.2 us (7%)
  starting transfers between devices  39.6 us (7%)
  other arithmetic  37.9 us (6%)
  between operations  17.3 us (3%)
    pallas_call x1, Pallas kernels, attend_back(): pl.pallas_call(functools.partial(attend_back_kernel, hl, hs, cp, ka, slot...  80.8 us
    all_gather x3, blocking collectives, local(): lax.all_gather(low(a), 'heads', axis=axis, tiled=True)  72.7 us
    pallas_call x1, Pallas kernels, encode_back(): pl.pallas_call(functools.partial(encode_back_kernel, cp, per), grid=(3 *...  48.8 us
    all_gather x1, waiting for transfers between devices, local(): own_feat = lax.all_gather(features, 'heads', axis=0, tiled=True)  47.8 us
    pallas_call x1, Pallas kernels, attend(): pl.pallas_call(functools.partial(attend_kernel, hl, hs, cp, ka, slots), g...  44.2 us
    pallas_call x1, Pallas kernels, finish(): pl.pallas_call(functools.partial(finish_kernel, nodes, heads), in_specs=[...  41.7 us
    pallas_call x1, Pallas kernels, encode(): pl.pallas_call(functools.partial(encode_kernel, cp, ka, cols, scale, per)...  31.9 us
    unnamed x113, local copies, waits for them, and re-layouts  19.8 us
  transfers between devices with their start and end apart: 23, of which 5 were waited for; matrix products, arithmetic and copies ran while one was open for 13% of the time, Pallas kernels for 36%

profile of v2, /device:TPU:0, one launch (start us, length us, event | category | flops | bytes accessed | tf_op | source)
XLA Modules:
  0.0 575.4 jit_solution(3815020170095371244)
XLA Ops:
  10.2 47.8 %all-gather.4.cloned.1.call-done.fo_ref = bf16[4096,256]{1,0:T(8,128)(2,1)} async-done(((bf16[1024,256]{1,0:T(8,128)(2,1)}), bf16[4096,256]{1,0:T(8,128)(2,1)}) %all-gather.4.cloned.1.call-update) | async-done | bytes 2097168 | tf_op jit(solution)/shard_map/all_gather | solution.py:483
  58.0 2.6 collective-permute-start.1
  61.7 3.5 all-to-all-start
  66.1 26.8 %all_gather.20 = bf16[6,512]{1,0:T(8,128)(2,1)S(1)} all-gather(bf16[6,128]{1,0:T(8,128)(2,1)S(1)} %convert_element_type.63), channel_id=1, replica_groups=mesh['nodes'=8,'heads'=4] {'heads'}, dimensions={1}, use_global_device_ids=true | all-gather | bytes 7680 | tf_op jit(solution)/shard_map/all_gather | solution.py:481
  95.8 16.8 %all_gather.19.enc_ref = bf16[256,512]{1,0:T(8,128)(2,1)} all-gather(bf16[64,512]{1,0:T(8,128)(2,1)S(1)} %convert_element_type.62), channel_id=1, replica_groups=mesh['nodes'=8,'heads'=4] {'heads'}, dimensions={0}, use_global_device_ids=true | all-gather | bytes 327680 | tf_op jit(solution)/shard_map/all_gather | solution.py:481
  115.2 31.9 %encode.1 = (bf16[12288,256]{1,0:T(8,128)(2,1)}, bf16[96,128,128]{2,1,0:T(8,128)(2,1)}, bf16[12288,128]{1,0:T(8,128)(2,1)}, bf16[96,128,128]{2,1,0:T(8,128)(2,1)}, bf16[4096,128]{1,0:T(8,128)(2,1)}) custom-call(s32[96]{0:T(128)} %pad_add_fusion.1.cnt_ref, bf16[4096,256]{1,0:T(8,128)(2,1)} %collective-permute-done.fp_ref, ...), custom_call_target="tpu_custom_call" | custom-call | flops 24576000000 | bytes 30000000 | tf_op jit(solution)/shard_map/encode/pallas_call | solution.py:198
  147.1 44.2 %attend.1 = (bf16[4096,128]{1,0:T(8,128)(2,1)}, f32[32,1,256]{2,1,0:T(1,128)}) custom-call(s32[288]{0:T(512)} %reshape.183.pos_ref, bf16[4096,128]{1,0:T(8,128)(2,1)} %get-tuple-element.44.q_ref, f32[32,9,256]{2,1,0:T(8,128)} %copy.96.brow_ref, bf16[12288,256]{1,0:T(8,128)(2,1)} %get-tuple-element.45.kaug_ref, bf16[96,128,128]{2,1,0:T(8,128)(2,1)} %get-tuple-element.46.vt_ref), custom_call_target="tpu_custom_call" | custom-call | flops 32000000000 | bytes 30000000 | tf_op jit(solution)/shard_map/attend/pallas_call | solution.py:72
  193.6 3.6 all-to-all-start.1
  198.7 29.2 %all_gather.21 = bf16[512,512]{1,0:T(8,128)(2,1)} all-gather(bf16[128,512]{1,0:T(8,128)(2,1)S(1)} %convert_element_type.66), channel_id=1, replica_groups=mesh['nodes'=8,'heads'=4] {'heads'}, dimensions={0}, use_global_device_ids=true | all-gather | bytes 655360 | tf_op jit(solution)/shard_map/all_gather | solution.py:481
  230.7 2.8 fusion.62
  233.8 7.4 %fusion.46 = f32[1024,2048]{1,0:T(8,128)} fusion(bf16[512,2048]{1,0:T(8,128)(2,1)} %all-gather.6.cloned.1.call-done, f32[1024,512]{0,1:T(8,128)S(1)} %get-tuple-element.163, f32[512]{0:T(512)S(1)} %bitcast.181, f32[1024]{0:T(1024)S(1)} %fusion.43, f32[1024]{0:T(1024)S(1)} %broadcast_multiply_fusion.1), kind=kOutput, calls=%fused_computation.129 | convolution fusion | flops 2149580800 | bytes 12593152 | tf_op jit(solution)/shard_map/dot_general | solution.py:520
  241.2 6.9 %fusion.63 = (f32[1024]{0:T(1024)S(1)}, f32[1024,512]{0,1:T(8,128)S(1)}) fusion(f32[1024,512]{0,1:T(8,128)S(1)} %get-tuple-element.163, bf16[2048,512]{1,0:T(8,128)(2,1)} %all-gather.8.cloned.1.call-done, f32[1024,2048]{1,0:T(8,128)} %fusion.46), kind=kOutput, calls=%fused_computation.140 | convolution fusion | flops 2167405568 | bytes 14684160 | tf_op jit(solution)/shard_map/dot_general | solution.py:523
  251.5 4.7 fusion.22
  259.3 7.9 %fusion.6 = bf16[1024,2048]{1,0:T(8,128)(2,1)S(1)} fusion(f32[1024,2048]{1,0:T(8,128)S(1)} %copy-done.52, bf16[2048,512]{1,0:T(8,128)(2,1)S(1)} %copy-done.51, f32[1024]{0:T(1024)S(1)} %negate_multiply_fusion.1, f32[1024,512]{0,1:T(8,128)S(1)} %get-tuple-element.165, f32[1024]{0:T(1024)S(1)} %multiply_multiply_fusion.11, f32[1024]{0:T(1024)S(1)} %get-tuple-element.153, ...), kind=kOutput, calls=%fused_computation.8 | convolution fusion | flops 2194145280 | bytes 16801792 | tf_op jit(solution)/shard_map/rd,fd->rf/dot_general | solution.py:536
  267.2 2.5 fusion.45
  269.7 2.7 multiply_reduce_fusion.1
  297.6 4.5 all-to-all-start.3
  302.5 5.5 all-to-all-done.3
  308.0 4.2 all-to-all-start.2
  312.9 2.9 bitcast_add_fusion
  324.3 6.5 %collective-permute-done.11 = f32[4,64,512]{2,1,0:T(8,128)S(1)} collective-permute-done((f32[4,64,512]{2,1,0:T(8,128)S(1)}, f32[4,64,512]{2,1,0:T(8,128)S(1)}, u32[]{:S(2)}, u32[]{:S(2)}) %collective-permute-start.11) | collective-permute-done | bytes 524320 | tf_op jit(solution)/shard_map/ppermute | solution.py:445
  331.9 10.6 %collective-permute-done.12 = f32[4,64,512]{2,1,0:T(8,128)S(1)} collective-permute-done((f32[4,64,512]{2,1,0:T(8,128)S(1)}, f32[4,64,512]{2,1,0:T(8,128)S(1)}, u32[]{:S(2)}, u32[]{:S(2)}) %collective-permute-start.12) | collective-permute-done | bytes 524320 | tf_op jit(solution)/shard_map/ppermute | solution.py:445
  343.6 5.4 all-to-all-start.5
  349.0 80.8 %attend_back.1 = (bf16[4096,128]{1,0:T(8,128)(2,1)}, f32[12288,256]{1,0:T(8,128)}, f32[32,9,256]{2,1,0:T(8,128)}) custom-call(s32[288]{0:T(512)} %reshape.183.pos_ref, bf16[4096,128]{1,0:T(8,128)(2,1)} %get-tuple-element.44.q_ref, bf16[4096,128]{1,0:T(8,128)(2,1)} %bitcast.15.do_ref, bf16[4096,128]{1,0:T(8,128)(2,1)} %get-tuple-element.47.o_ref, ...), custom_call_target="tpu_custom_call" | custom-call | flops 64000000000 | bytes 60000000 | tf_op jit(solution)/shard_map/attend_back/pallas_call | solution.py:133
  432.2 5.1 all-to-all-start.4
  438.9 48.8 %encode_back.1 = (f32[512,384]{1,0:T(8,128)}, f32[512,256]{1,0:T(8,128)}, f32[512,128]{1,0:T(8,128)}, f32[512,128]{1,0:T(8,128)}) custom-call(bf16[4096,256]{1,0:T(8,128)(2,1)} %collective-permute-done.fp_ref, bf16[4096,256]{1,0:T(8,128)(2,1)} %all-gather.4.cloned.1.call-done.fo_ref, bf16[4096,256]{1,0:T(8,128)(2,1)} %collective-permute-done.1.fn_ref, ...), custom_call_target="tpu_custom_call" | custom-call | flops 40960000000 | bytes 40000000 | tf_op jit(solution)/shard_map/encode_back/pallas_call | solution.py:276
  495.9 41.7 %finish.1 = (f32[8,4,16,384]{3,2,1,0:T(8,128)S(1)}, f32[8,8,512]{2,1,0:T(8,128)S(1)}, f32[8,512]{1,0:T(8,128)S(1)}, f32[8,16,512]{2,1,0:T(8,128)S(1)}, f32[8,16,...) custom-call(f32[4,4,2,16,384]{4,3,2,1,0:T(8,128)S(1)} %bitcast.150, f32[4,4,2,8,512]{4,3,2,1,0:T(8,128)S(1)} %bitcast.149, ...), custom_call_target="tpu_custom_call" | custom-call | tf_op jit(solution)/shard_map/finish/pallas_call | solution.py:393
  541.8 3.4 copy.113
  545.2 3.4 fusion.54
  548.7 2.4 copy.117
  557.3 4.5 fusion.48
  561.9 2.5 fusion.50
  (238 shorter events, 84.8 us)
Async XLA Ops:
  7.2 53.4 %copy-start.16 = (f32[128,1536]{1,0:T(8,128)S(1)}, f32[128,1536]{1,0:T(8,128)}, u32[]{:S(2)}) copy-start(f32[128,1536]{1,0:T(8,128)} %param.31) | copy-start | bytes 2359300
  7.2 50.8 %all-gather.4.cloned.1.call-start = ((), (), s32[]{:S(2)}) async-start(), calls=%async_computation.6 | async-start | bytes 2621440 | tf_op jit(solution)/shard_map/all_gather | solution.py:483
  7.9 57.2 %copy-start.12 = (f32[512,512]{1,0:T(8,128)S(1)}, f32[512,512]{1,0:T(8,128)}, u32[]{:S(2)}) copy-start(f32[512,512]{1,0:T(8,128)} %param.40) | copy-start | bytes 3145732
  7.9 225.9 %all-gather.6.cloned.1.call-start = ((), (), s32[]{:S(2)}) async-start(), calls=%async_computation.7 | async-start | bytes 2621440 | tf_op jit(solution)/shard_map/all_gather | solution.py:481
  58.0 57.2 %collective-permute-start = (bf16[4096,256]{1,0:T(8,128)(2,1)}, bf16[4096,256]{1,0:T(8,128)(2,1)}, u32[]{:S(2)}, u32[]{:S(2)}) collective-permute-start(bf16[4096,256]{1,0:T(8,128)(2,1)} %all-gather.4.cloned.1.call-done.fo_ref), channel_id=1, source_target_pairs={{0,4},{4,8},{8,12},{12,16},{16,20},{20,24},{24,28},{28,0},{1,5},{5... | collective-permute-start | bytes 6291464 | tf_op jit(solution)/shard_map/ppermute | solution.py:456
  58.0 57.2 %collective-permute-start.1 = (bf16[4096,256]{1,0:T(8,128)(2,1)}, bf16[4096,256]{1,0:T(8,128)(2,1)}, u32[]{:S(2)}, u32[]{:S(2)}) collective-permute-start(bf16[4096,256]{1,0:T(8,128)(2,1)} %all-gather.4.cloned.1.call-done.fo_ref), channel_id=1, source_target_pairs={{0,28},{4,0},{8,4},{12,8},{16,12},{20,16},{24,20},{28,24},{1,29},{... | collective-permute-start | bytes 6291464 | tf_op jit(solution)/shard_map/ppermute | solution.py:456
  61.7 52.1 %all-to-all-start = ((bf16[128,4,384]{0,2,1:T(8,128)(2,1)}), bf16[128,4,384]{0,2,1:T(8,128)(2,1)S(1)}, u32[]{:S(2)}, u32[]{:S(2)}) async-start(bf16[128,4,384]{0,2,1:T(8,128)(2,1)} %bitcast), calls=%async_computation | async-start | bytes 786432 | tf_op jit(solution)/shard_map/all_to_all | solution.py:488
  65.1 47.4 %copy-start.45 = (s32[256]{0:T(256)S(1)}, s32[256]{0:T(256)}, u32[]{:S(2)}) copy-start(s32[256]{0:T(256)} %param.25) | copy-start | bytes 3076
  65.1 176.1 %all-gather.8.cloned.1.call-start = ((), (), s32[]{:S(2)}) async-start(), calls=%async_computation.8 | async-start | bytes 2621440 | tf_op jit(solution)/shard_map/all_gather | solution.py:481
  193.6 34.3 %copy-start.8 = (bf16[1024,256]{1,0:T(8,128)(2,1)S(1)}, bf16[1024,256]{1,0:T(8,128)(2,1)}, u32[]{:S(2)}) copy-start(bf16[1024,256]{1,0:T(8,128)(2,1)} %param.23) | copy-start | bytes 1572868
  193.6 34.3 %copy-start.19 = (bf16[256,512]{1,0:T(8,128)(2,1)S(1)}, bf16[256,512]{1,0:T(8,128)(2,1)}, u32[]{:S(2)}) copy-start(bf16[256,512]{1,0:T(8,128)(2,1)} %all_gather.19.enc_ref) | copy-start | bytes 786436
  193.6 36.1 %all-to-all-start.1 = ((bf16[4,1024,128]{1,2,0:T(8,128)(2,1)}), bf16[4,1024,128]{1,2,0:T(8,128)(2,1)S(1)}, u32[]{:S(2)}, u32[]{:S(2)}) async-start(bf16[4,1024,128]{1,2,0:T(8,128)(2,1)} %copy.97), calls=%async_computation.1 | async-start | bytes 2097152 | tf_op jit(solution)/shard_map/all_to_all | solution.py:514
  197.2 33.4 %copy-start.40 = (f32[1,512]{1,0:T(1,128)S(1)}, f32[1,512]{1,0:T(1,128)}, u32[]{:S(2)}) copy-start(f32[1,512]{1,0:T(1,128)} %get-tuple-element.158.bias_ref) | copy-start | bytes 6148
  259.0 53.9 %collective-permute-start.10 = (f32[4,4,64,512]{3,2,1,0:T(8,128)}, f32[4,4,64,512]{3,2,1,0:T(8,128)}, u32[]{:S(2)}, u32[]{:S(2)}) collective-permute-start(f32[4,4,64,512]{3,2,1,0:T(8,128)} %dynamic-slice_bitcast_fusion), channel_id=1, source_target_pairs={{0,4},{4,0},{8,12},{12,8},{16,20},{20,16},{24,28},{28,24},{1,5},{5... | collective-permute-start | bytes 6291464 | tf_op jit(solution)/shard_map/ppermute | solution.py:436
  276.3 10.0 %collective-permute-start.2 = (f32[4,4,16,512]{3,2,1,0:T(8,128)}, f32[4,4,16,512]{3,2,1,0:T(8,128)}, u32[]{:S(2)}, u32[]{:S(2)}) collective-permute-start(f32[4,4,16,512]{3,2,1,0:T(8,128)} %dynamic-slice_bitcast_fusion.8), channel_id=1, source_target_pairs={{0,4},{4,0},{8,12},{12,8},{16,20},{20,16},{24,28},{28,24},{1,5},{5... | collective-permute-start | bytes 1572872 | tf_op jit(solution)/shard_map/ppermute | solution.py:436
  278.0 41.4 %collective-permute-start.6 = (f32[4,4,16,2048]{3,2,1,0:T(8,128)}, f32[4,4,16,2048]{3,2,1,0:T(8,128)}, u32[]{:S(2)}, u32[]{:S(2)}) collective-permute-start(f32[4,4,16,2048]{3,2,1,0:T(8,128)} %dynamic-slice_bitcast_fusion.1), channel_id=1, source_target_pairs={{0,4},{4,0},{8,12},{12,8},{16,20},{20,16},{24,28},{28,24},{1,5},{5... | collective-permute-start | bytes 6291464 | tf_op jit(solution)/shard_map/ppermute | solution.py:436
  287.7 7.5 %collective-permute-start.3 = (f32[4,16,512]{2,1,0:T(8,128)S(1)}, f32[4,16,512]{2,1,0:T(8,128)S(1)}, u32[]{:S(2)}, u32[]{:S(2)}) collective-permute-start(f32[4,16,512]{2,1,0:T(8,128)S(1)} %get-tuple-element.149), channel_id=1, source_target_pairs={{0,8},{4,12},{8,0},{12,4},{16,24},{20,28},{24,16},{28,20},{1,9},{5... | collective-permute-start | bytes 393224 | tf_op jit(solution)/shard_map/ppermute | solution.py:445
  288.8 8.1 %collective-permute-start.4 = (f32[4,16,512]{2,1,0:T(8,128)S(1)}, f32[4,16,512]{2,1,0:T(8,128)S(1)}, u32[]{:S(2)}, u32[]{:S(2)}) collective-permute-start(f32[4,16,512]{2,1,0:T(8,128)S(1)} %get-tuple-element.151), channel_id=1, source_target_pairs={{0,16},{4,20},{8,24},{12,28},{16,0},{20,4},{24,8},{28,12},{1,17},{... | collective-permute-start | bytes 393224 | tf_op jit(solution)/shard_map/ppermute | solution.py:445
  289.3 7.6 %collective-permute-start.5 = (f32[4,16,512]{2,1,0:T(8,128)S(1)}, f32[4,16,512]{2,1,0:T(8,128)S(1)}, u32[]{:S(2)}, u32[]{:S(2)}) collective-permute-start(f32[4,16,512]{2,1,0:T(8,128)S(1)} %get-tuple-element.150), channel_id=1, source_target_pairs={{0,24},{4,28},{8,16},{12,20},{16,8},{20,12},{24,0},{28,4},{1,25},{... | collective-permute-start | bytes 393224 | tf_op jit(solution)/shard_map/ppermute | solution.py:445
  297.6 10.4 %all-to-all-start.3 = ((f32[4,16,512]{2,1,0:T(8,128)}), f32[4,16,512]{2,1,0:T(8,128)S(1)}, u32[]{:S(2)}, u32[]{:S(2)}) async-start(f32[4,16,512]{2,1,0:T(8,128)} %fusion.28), calls=%async_computation.3 | async-start | bytes 262144 | tf_op jit(solution)/shard_map/all_to_all | solution.py:450
  308.0 35.6 %all-to-all-start.2 = ((bf16[1024,4,128]{2,0,1:T(8,128)(2,1)}), bf16[1024,4,128]{2,0,1:T(8,128)(2,1)}, u32[]{:S(2)}, u32[]{:S(2)}) async-start(bf16[1024,4,128]{2,0,1:T(8,128)(2,1)} %copy.99), calls=%async_computation.2 | async-start | bytes 2097152 | tf_op jit(solution)/shard_map/all_to_all | solution.py:546
  315.9 14.9 %collective-permute-start.11 = (f32[4,64,512]{2,1,0:T(8,128)S(1)}, f32[4,64,512]{2,1,0:T(8,128)S(1)}, u32[]{:S(2)}, u32[]{:S(2)}) collective-permute-start(f32[4,64,512]{2,1,0:T(8,128)S(1)} %get-tuple-element.143), channel_id=1, source_target_pairs={{0,8},{4,12},{8,0},{12,4},{16,24},{20,28},{24,16},{28,20},{1,9},{5... | collective-permute-start | bytes 1572872 | tf_op jit(solution)/shard_map/ppermute | solution.py:445
  316.5 26.0 %collective-permute-start.12 = (f32[4,64,512]{2,1,0:T(8,128)S(1)}, f32[4,64,512]{2,1,0:T(8,128)S(1)}, u32[]{:S(2)}, u32[]{:S(2)}) collective-permute-start(f32[4,64,512]{2,1,0:T(8,128)S(1)} %get-tuple-element.145), channel_id=1, source_target_pairs={{0,16},{4,20},{8,24},{12,28},{16,0},{20,4},{24,8},{28,12},{1,17},{... | collective-permute-start | bytes 1572872 | tf_op jit(solution)/shard_map/ppermute | solution.py:445
  317.7 24.8 %collective-permute-start.13 = (f32[4,64,512]{2,1,0:T(8,128)S(1)}, f32[4,64,512]{2,1,0:T(8,128)S(1)}, u32[]{:S(2)}, u32[]{:S(2)}) collective-permute-start(f32[4,64,512]{2,1,0:T(8,128)S(1)} %get-tuple-element.144), channel_id=1, source_target_pairs={{0,24},{4,28},{8,16},{12,20},{16,8},{20,12},{24,0},{28,4},{1,25},{... | collective-permute-start | bytes 1572872 | tf_op jit(solution)/shard_map/ppermute | solution.py:445
  322.6 107.3 %collective-permute-start.7 = (f32[4,16,2048]{2,1,0:T(8,128)}, f32[4,16,2048]{2,1,0:T(8,128)}, u32[]{:S(2)}, u32[]{:S(2)}) collective-permute-start(f32[4,16,2048]{2,1,0:T(8,128)} %get-tuple-element.146), channel_id=1, source_target_pairs={{0,8},{4,12},{8,0},{12,4},{16,24},{20,28},{24,16},{28,20},{1,9},{5... | collective-permute-start | bytes 1572872 | tf_op jit(solution)/shard_map/ppermute | solution.py:445
  323.1 106.8 %collective-permute-start.8 = (f32[4,16,2048]{2,1,0:T(8,128)}, f32[4,16,2048]{2,1,0:T(8,128)}, u32[]{:S(2)}, u32[]{:S(2)}) collective-permute-start(f32[4,16,2048]{2,1,0:T(8,128)} %get-tuple-element.148), channel_id=1, source_target_pairs={{0,16},{4,20},{8,24},{12,28},{16,0},{20,4},{24,8},{28,12},{1,17},{... | collective-permute-start | bytes 1572872 | tf_op jit(solution)/shard_map/ppermute | solution.py:445
  330.8 99.1 %collective-permute-start.9 = (f32[4,16,2048]{2,1,0:T(8,128)}, f32[4,16,2048]{2,1,0:T(8,128)}, u32[]{:S(2)}, u32[]{:S(2)}) collective-permute-start(f32[4,16,2048]{2,1,0:T(8,128)} %get-tuple-element.147), channel_id=1, source_target_pairs={{0,24},{4,28},{8,16},{12,20},{16,8},{20,12},{24,0},{28,4},{1,25},{... | collective-permute-start | bytes 1572872 | tf_op jit(solution)/shard_map/ppermute | solution.py:445
  343.6 88.6 %all-to-all-start.5 = ((f32[4,64,512]{2,1,0:T(8,128)}), f32[4,64,512]{2,1,0:T(8,128)S(1)}, u32[]{:S(2)}, u32[]{:S(2)}) async-start(f32[4,64,512]{2,1,0:T(8,128)} %fusion.19), calls=%async_computation.5 | async-start | bytes 1048576 | tf_op jit(solution)/shard_map/all_to_all | solution.py:450
  432.1 55.6 %copy-start.22 = (f32[4,64,512]{2,1,0:T(8,128)}, f32[4,64,512]{2,1,0:T(8,128)S(1)}, u32[]{:S(2)}) copy-start(f32[4,64,512]{2,1,0:T(8,128)S(1)} %all-to-all-done.5) | copy-start | bytes 1572868
  432.2 60.3 %all-to-all-start.4 = ((f32[4,16,2048]{2,1,0:T(8,128)}), f32[4,16,2048]{2,1,0:T(8,128)}, u32[]{:S(2)}, u32[]{:S(2)}) async-start(f32[4,16,2048]{2,1,0:T(8,128)} %fusion.21), calls=%async_computation.4 | async-start | bytes 1048576 | tf_op jit(solution)/shard_map/all_to_all | solution.py:450
  438.9 51.1 %copy-start.33 = (f32[32,9,256]{2,1,0:T(8,128)S(1)}, f32[32,9,256]{2,1,0:T(8,128)}, u32[]{:S(2)}) copy-start(f32[32,9,256]{2,1,0:T(8,128)} %get-tuple-element.57) | copy-start | bytes 884740
  438.9 51.7 %copy-start.39 = (s32[32,9]{0,1:T(8,128)S(1)}, s32[32,9]{0,1:T(8,128)}, u32[]{:S(2)}) copy-start(s32[32,9]{0,1:T(8,128)} %param.27) | copy-start | bytes 3460
  (44 other events, 236.6 us)
Sparse Core Ops, SparseCore 0:
  9.6 48.3 all-gather.3
  60.1 54.5 all-gather.5
  116.9 43.7 all-gather.7

commit v3 on v2

v3 whole, which is shorter than its diff:
```python
import functools

import jax
import jax.numpy as jnp
from jax import lax
from jax.experimental import pallas as pl
from jax.experimental.pallas import tpu as pltpu
from jax.sharding import PartitionSpec as P

BLOCK = 128
NT = (((1,), (1,)), ((), ()))
NN = (((1,), (0,)), ((), ()))
f32 = jnp.float32
bf16 = jnp.bfloat16


def dotf(a, b, dims):
    return lax.dot_general(a, b, dims, preferred_element_type=f32)


def head_rows(x, hl, hs, cp):
    if hl == 1:
        return x
    lane = lax.broadcasted_iota(jnp.int32, (BLOCK, cp), 1)
    zero = jnp.zeros_like(x)
    return jnp.concatenate([jnp.where(lane // hs == h, x, zero) for h in range(hl)], axis=0)


def ones_lane(hl, cp, ka):
    rows = hl * BLOCK
    lane = lax.broadcasted_iota(jnp.int32, (rows, ka - cp), 1)
    return jnp.where(lane == 0, 1.0, 0.0).astype(bf16)


def attend_kernel(hl, hs, cp, ka, slots, block_of, pos_ref, q_ref, brow_ref, kaug_ref, vt_ref, o_ref, lse_ref, s_ref, p_ref):
    b = block_of(pl.program_id(0))
    rows = hl * BLOCK
    q2 = head_rows(q_ref[...], hl, hs, cp)
    qa = jnp.concatenate([q2, ones_lane(hl, cp, ka)], axis=1) if ka > cp else q2
    top = None
    spots = [pl.ds(pl.multiple_of(pos_ref[b * slots + s] * BLOCK, BLOCK), BLOCK) for s in range(slots)]
    scores = dotf(jnp.concatenate([kaug_ref[at, :] for at in spots], axis=0), qa, NT)
    for s in range(slots):
        sc = scores[s * BLOCK:(s + 1) * BLOCK]
        s_ref[s] = sc
        t = jnp.max(sc, axis=0, keepdims=True) + brow_ref[0, s:s + 1, :]
        top = t if top is None else jnp.maximum(top, t)
    tot = jnp.zeros((1, rows), f32)
    for s in range(slots):
        e = jnp.exp(s_ref[s] - (top - brow_ref[0, s:s + 1, :]))
        s_ref[s] = e
        tot = tot + jnp.sum(e, axis=0, keepdims=True)
    lse_ref[0] = top + jnp.log(tot)
    inv = 1.0 / tot
    vs = []
    for s in range(slots):
        p_ref[s * BLOCK:(s + 1) * BLOCK, :] = (s_ref[s] * inv).astype(bf16)
        vs.append(vt_ref[pos_ref[b * slots + s]])
    ot = dotf(jnp.concatenate(vs, axis=1), p_ref[...], NN)
    parts = [ot[h * hs:(h + 1) * hs, h * BLOCK:(h + 1) * BLOCK] for h in range(hl)]
    if hl * hs < cp:
        parts.append(jnp.zeros((cp - hl * hs, BLOCK), f32))
    o_ref[...] = jnp.concatenate(parts, axis=0).T.astype(bf16)


def attend(part, own, pos, q, brow, kaug, vt, hl, hs):
    cp, ka = q.shape[1], kaug.shape[1]
    nb = q.shape[0] // BLOCK // 2
    half = own // 2
    block_of = lambda i: lax.div(i, half) * own + part * half + lax.rem(i, half)
    slots = brow.shape[1]
    rows = hl * BLOCK
    whole = lambda a: pl.BlockSpec(a.shape, lambda i, *_: (0,) * a.ndim, pipeline_mode=pl.Buffered(1))
    return pl.pallas_call(
        functools.partial(attend_kernel, hl, hs, cp, ka, slots, block_of),
        grid_spec=pltpu.PrefetchScalarGridSpec(
            num_scalar_prefetch=1, grid=(nb,),
            in_specs=[pl.BlockSpec((BLOCK, cp), lambda i, *_: (block_of(i), 0)),
                      pl.BlockSpec((1, slots, rows), lambda i, *_: (block_of(i), 0, 0)),
                      whole(kaug), whole(vt)],
            out_specs=[pl.BlockSpec((BLOCK, cp), lambda i, *_: (i, 0)),
                       pl.BlockSpec((1, 1, rows), lambda i, *_: (i, 0, 0))],
            scratch_shapes=[pltpu.VMEM((slots, BLOCK, rows), f32), pltpu.VMEM((slots * BLOCK, rows), bf16)]),
        out_shape=[jax.ShapeDtypeStruct((nb * BLOCK, cp), bf16), jax.ShapeDtypeStruct((nb, 1, rows), f32)],
        cost_estimate=pl.CostEstimate(flops=nb * 10**9, bytes_accessed=3 * 10**7, transcendentals=0),
        compiler_params=pltpu.CompilerParams(vmem_limit_bytes=60 << 20),
        name="attend",
    )(pos, q, brow, kaug, vt)


def attend_back_kernel(hl, hs, cp, ka, slots, scale, block_of, pos_ref, q_ref, do_ref, oa_ref, ob_ref, la_ref, lb_ref, brow_ref, kaug_ref, v_ref, kt_ref,
                       dq_ref, dkv_ref, edge_ref, p_ref, d_ref):
    i = pl.program_id(0)
    b = block_of(i)
    late = i >= pl.num_programs(0) // 2
    rows = hl * BLOCK

    @pl.when(i == 0)
    def _():
        dkv_ref[...] = jnp.zeros_like(dkv_ref)

    q2 = head_rows(q_ref[...], hl, hs, cp)
    qa = jnp.concatenate([q2, ones_lane(hl, cp, ka)], axis=1) if ka > cp else q2
    do = do_ref[...]
    do2 = head_rows(do, hl, hs, cp)
    prod = (do.astype(f32) * jnp.where(late, ob_ref[...], oa_ref[...]).astype(f32)).T
    dd = jnp.concatenate([jnp.sum(prod[h * hs:(h + 1) * hs], axis=0, keepdims=True) for h in range(hl)], axis=1)
    lse = jnp.where(late, lb_ref[0], la_ref[0])
    spots = [pl.ds(pl.multiple_of(pos_ref[b * slots + s] * BLOCK, BLOCK), BLOCK) for s in range(slots)]
    scores = dotf(jnp.concatenate([kaug_ref[at, :] for at in spots], axis=0), qa, NT)
    grads = dotf(jnp.concatenate([v_ref[at, :] for at in spots], axis=0), do2, NT)
    for s in range(slots):
        here = slice(s * BLOCK, (s + 1) * BLOCK)
        pr = jnp.exp(scores[here] - (lse - brow_ref[0, s:s + 1, :]))
        ds = pr * (grads[here] - dd)
        edge_ref[0, s:s + 1, :] = jnp.sum(ds, axis=0, keepdims=True)
        p_ref[here, :] = pr.astype(bf16)
        d_ref[here, :] = ds.astype(bf16)
    dv = dotf(p_ref[...], do2, NN)
    dk = dotf(d_ref[...], q2, NN)
    dqt = dotf(jnp.concatenate([kt_ref[pos_ref[b * slots + s]] for s in range(slots)], axis=1), d_ref[...], NN)
    for s, at in enumerate(spots):
        here = slice(s * BLOCK, (s + 1) * BLOCK)
        dkv_ref[at, 0:cp] += dk[here]
        dkv_ref[at, cp:2 * cp] += dv[here]
    parts = [dqt[h * hs:(h + 1) * hs, h * BLOCK:(h + 1) * BLOCK] for h in range(hl)]
    if hl * hs < cp:
        parts.append(jnp.zeros((cp - hl * hs, BLOCK), f32))
    dq_ref[...] = (jnp.concatenate(parts, axis=0).T * scale).astype(bf16)


def attend_back(own, pos, q, do, outs, lses, brow, kaug, v, kt, hl, hs):
    cp, ka = q.shape[1], kaug.shape[1]
    nb = q.shape[0] // BLOCK
    slots = brow.shape[1]
    rows = hl * BLOCK
    half, mid = own // 2, nb // 2
    block_of = lambda i: lax.div(lax.rem(i, mid), half) * own + lax.div(i, mid) * half + lax.rem(i, half)
    whole = lambda a: pl.BlockSpec(a.shape, lambda i, *_: (0,) * a.ndim, pipeline_mode=pl.Buffered(1))
    tile = pl.BlockSpec((BLOCK, cp), lambda i, *_: (block_of(i), 0))
    early = lambda i: jnp.minimum(i, mid - 1)
    late = lambda i: jnp.maximum(i - mid, 0)
    return pl.pallas_call(
        functools.partial(attend_back_kernel, hl, hs, cp, ka, slots, hs ** -0.5, block_of),
        grid_spec=pltpu.PrefetchScalarGridSpec(
            num_scalar_prefetch=1, grid=(nb,),
            in_specs=[tile, tile,
                      pl.BlockSpec((BLOCK, cp), lambda i, *_: (early(i), 0)), pl.BlockSpec((BLOCK, cp), lambda i, *_: (late(i), 0)),
                      pl.BlockSpec((1, 1, rows), lambda i, *_: (early(i), 0, 0)), pl.BlockSpec((1, 1, rows), lambda i, *_: (late(i), 0, 0)),
                      pl.BlockSpec((1, slots, rows), lambda i, *_: (block_of(i), 0, 0)),
                      whole(kaug), whole(v), whole(kt)],
            out_specs=[tile, pl.BlockSpec((v.shape[0], 2 * cp), lambda i, *_: (0, 0), pipeline_mode=pl.Buffered(1)),
                       pl.BlockSpec((1, slots, rows), lambda i, *_: (block_of(i), 0, 0))],
            scratch_shapes=[pltpu.VMEM((slots * BLOCK, rows), bf16)] * 2),
        out_shape=[jax.ShapeDtypeStruct(q.shape, bf16), jax.ShapeDtypeStruct((v.shape[0], 2 * cp), f32),
                   jax.ShapeDtypeStruct((nb, slots, rows), f32)],
        cost_estimate=pl.CostEstimate(flops=nb * 2 * 10**9, bytes_accessed=6 * 10**7, transcendentals=0),
        compiler_params=pltpu.CompilerParams(vmem_limit_bytes=60 << 20),
        name="attend_back",
    )(pos, q, do, *outs, *lses, brow, kaug, v, kt)
norm_eps = 1e-05


def encode_kernel(cp, ka, cols, scale, per_group, cnt_ref, x_ref, enc_ref, bias_ref, gain_ref, w_ref,
                  kaug_ref, kt_ref, v_ref, vt_ref, q_ref):
    i = pl.program_id(0)
    group = i // per_group
    tile = x_ref.shape[0]
    resid = dotf(x_ref[...], enc_ref[...], NN) + bias_ref[...]
    centred = resid - jnp.mean(resid, axis=-1, keepdims=True)
    variance = jnp.mean(centred * centred, axis=-1, keepdims=True)
    act = (centred * lax.rsqrt(variance + norm_eps) * gain_ref[...]).astype(bf16)
    kv = dotf(act, w_ref[:, cp:], NN).astype(bf16)
    key, value = kv[:, :cp], kv[:, cp:]
    row = lax.broadcasted_iota(jnp.int32, (BLOCK, 128), 0)
    lane = lax.broadcasted_iota(jnp.int32, (BLOCK, 128), 1)
    first = i * (tile // BLOCK)
    dead = jnp.concatenate(
        [jnp.where((row >= cnt_ref[first + j]) & (lane == cols % 128), -1e30, 0.0) for j in range(tile // BLOCK)], axis=0).astype(bf16)
    if ka > cp:
        kaug_ref[:, :cp] = key
        kaug_ref[:, cp:] = dead
    else:
        kaug_ref[...] = key + dead
    v_ref[...] = value
    for j in range(tile // BLOCK):
        kt_ref[j] = key[j * BLOCK:(j + 1) * BLOCK].T
        vt_ref[j] = value[j * BLOCK:(j + 1) * BLOCK].T

    @pl.when(group == 1)
    def _():
        q = (dotf(act, w_ref[:, :cp], NN) * scale).astype(bf16)
        if ka == cp:
            lanes = lax.broadcasted_iota(jnp.int32, q.shape, 1)
            q = jnp.where(lanes == cols, jnp.ones_like(q), q)
        q_ref[...] = q


def encode(counts, feats, enc, bias, gain, w, cp, ka, cols, scale, tile=512):
    rows, feat = feats.shape[0] // 3, feats.shape[1]
    width = enc.shape[1]
    per = rows // tile
    blocks = tile // BLOCK
    whole = lambda a: pl.BlockSpec(a.shape, lambda i, *_: (0,) * a.ndim, pipeline_mode=pl.Buffered(1))
    return pl.pallas_call(
        functools.partial(encode_kernel, cp, ka, cols, scale, per),
        grid_spec=pltpu.PrefetchScalarGridSpec(
            num_scalar_prefetch=1, grid=(3 * per,),
            in_specs=[pl.BlockSpec((tile, feat), lambda i, *_: (i, 0)), whole(enc), whole(bias), whole(gain), whole(w)],
            out_specs=[pl.BlockSpec((tile, ka), lambda i, *_: (i, 0)),
                       pl.BlockSpec((blocks, cp, BLOCK), lambda i, *_: (i, 0, 0)),
                       pl.BlockSpec((tile, cp), lambda i, *_: (i, 0)),
                       pl.BlockSpec((blocks, cp, BLOCK), lambda i, *_: (i, 0, 0)),
                       pl.BlockSpec((tile, cp), lambda i, *_: (jnp.clip(i - per, 0, per - 1), 0))]),
        out_shape=[jax.ShapeDtypeStruct((3 * rows, ka), bf16),
                   jax.ShapeDtypeStruct((3 * rows // BLOCK, cp, BLOCK), bf16),
                   jax.ShapeDtypeStruct((3 * rows, cp), bf16),
                   jax.ShapeDtypeStruct((3 * rows // BLOCK, cp, BLOCK), bf16),
                   jax.ShapeDtypeStruct((rows, cp), bf16)],
        compiler_params=pltpu.CompilerParams(vmem_limit_bytes=60 << 20),
        cost_estimate=pl.CostEstimate(flops=rows * 6 * 10**6, bytes_accessed=3 * 10**7, transcendentals=0),
        name="encode",
    )(counts, feats, enc, bias, gain, w)


def encode_back_kernel(cp, per_group, x_ref, dkv_ref, dq_ref, enct_ref, bias_ref, gain_ref, wq_ref, wkv_ref,
                       dw_ref, denc_ref, dgain_ref, dbias_ref, g_ref):
    i = pl.program_id(0)
    group = i // per_group
    tile = x_ref.shape[0]
    width = enct_ref.shape[0]
    reps = tile // 128

    @pl.when(i == 0)
    def _():
        for ref in (dw_ref, denc_ref, dgain_ref, dbias_ref):
            ref[...] = jnp.zeros_like(ref)

    x = x_ref[...]
    wide = lambda c: jnp.concatenate([c] * reps, axis=1)
    fold = lambda a: functools.reduce(jnp.add, [a[:, r * 128:(r + 1) * 128] for r in range(reps)])
    resid = dotf(enct_ref[...], x, NT) + wide(bias_ref[...])
    centred = resid - jnp.sum(resid, axis=0, keepdims=True) * (1.0 / width)
    variance = jnp.sum(centred * centred, axis=0, keepdims=True) * (1.0 / width)
    inv = lax.rsqrt(variance + norm_eps)
    norm = centred * inv
    gain = wide(gain_ref[...])
    act = (norm * gain).astype(bf16)
    dkv = dkv_ref[...].astype(bf16)
    g_ref[...] = dotf(wkv_ref[...], dkv, NT)
    dw_ref[:, cp:] += dotf(act, dkv, NN)

    @pl.when(group == 1)
    def _():
        dq = dq_ref[...]
        g_ref[...] += dotf(wq_ref[...], dq, NT)
        dw_ref[:, :cp] += dotf(act, dq, NN)

    grad = g_ref[...]
    dgain_ref[...] += fold(grad * norm)
    back = grad * gain
    mean_one = jnp.sum(back, axis=0, keepdims=True) * (1.0 / width)
    mean_two = jnp.sum(back * norm, axis=0, keepdims=True) * (1.0 / width)
    din = inv * (back - mean_one - norm * mean_two)
    dbias_ref[...] += fold(din)
    denc_ref[...] += dotf(din.astype(bf16), x, NN)


def encode_back(feats, dkv, dq, enct, bias, gain, wq, wkv, tile=512):
    rows, feat = feats.shape[0] // 3, feats.shape[1]
    width = enct.shape[0]
    cp = dq.shape[1]
    per = rows // tile
    whole = lambda a: pl.BlockSpec(a.shape, lambda i: (0,) * a.ndim, pipeline_mode=pl.Buffered(1))
    keep = lambda s: pl.BlockSpec(s, lambda i: (0,) * len(s), pipeline_mode=pl.Buffered(1))
    shapes = [(width, 3 * cp), (width, feat), (width, 128), (width, 128)]
    return pl.pallas_call(
        functools.partial(encode_back_kernel, cp, per),
        grid=(3 * per,),
        in_specs=[pl.BlockSpec((tile, feat), lambda i: (i, 0)), pl.BlockSpec((tile, 2 * cp), lambda i: (i, 0)),
                  pl.BlockSpec((tile, cp), lambda i: (jnp.clip(i - per, 0, per - 1), 0)),
                  whole(enct), whole(bias), whole(gain), whole(wq), whole(wkv)],
        out_specs=[keep(s) for s in shapes],
        out_shape=[jax.ShapeDtypeStruct(s, f32) for s in shapes],
        scratch_shapes=[pltpu.VMEM((width, tile), f32)],
        compiler_params=pltpu.CompilerParams(vmem_limit_bytes=60 << 20),
        cost_estimate=pl.CostEstimate(flops=rows * 10**7, bytes_accessed=4 * 10**7, transcendentals=0),
        name="encode_back",
    )(feats, dkv, dq, enct, bias, gain, wq, wkv)


def row_norm(values):
    centred = values - jnp.mean(values, axis=-1, keepdims=True)
    inv = lax.rsqrt(jnp.mean(centred * centred, axis=-1, keepdims=True) + norm_eps)
    return centred * inv, inv


def norm_back(grad, norm, inv):
    return inv * (grad - jnp.mean(grad, axis=-1, keepdims=True) - norm * jnp.mean(grad * norm, axis=-1, keepdims=True))


def dense_kernel(first, chunk, total_ref, attn_ref, feat_ref, side_ref, vec_ref, enc_ref, out_ref, up_ref, down_ref, *refs):
    if not first:
        olds, refs = refs[:5], refs[5:]
    gattn_ref, ddown_ref, dup_ref, dout_ref, denc_ref, dvec_ref, u_ref, g_ref = refs
    i = pl.program_id(0)

    @pl.when(i == 0)
    def _():
        for n, ref in enumerate((ddown_ref, dup_ref, dout_ref, denc_ref, dvec_ref)):
            ref[...] = jnp.zeros_like(ref) if first else olds[n][...]

    heads = attn_ref.shape[0]
    ff = up_ref.shape[1]
    bias, gain_two, gain_three, head_vec = (vec_ref[r:r + 1, :] for r in range(4))
    target, live = side_ref[:, 0:1], side_ref[:, 1:2]
    attn = jnp.concatenate([attn_ref[h] for h in range(heads)], axis=1)
    feat = feat_ref[...]
    hidden_one = dotf(feat, enc_ref[...], NN) + bias + dotf(attn, out_ref[...], NN)
    norm_two, inv_two = row_norm(hidden_one)
    act_two = (norm_two * gain_two).astype(bf16)
    root = 0.7978845608028654
    acts = []
    for c in range(0, ff, chunk):
        u = dotf(act_two, up_ref[:, c:c + chunk], NN)
        square = u * u
        half = 0.5 * (1.0 + jnp.tanh(root * (u + 0.044715 * (u * square))))
        act = (u * half).astype(bf16)
        u_ref[:, c:c + chunk] = half + 2.0 * u * half * (1.0 - half) * (root * (1.0 + 0.134145 * square))
        g_ref[:, c:c + chunk] = act
    hidden_two = hidden_one + dotf(g_ref[...], down_ref[...], NN)
    norm_three, inv_three = row_norm(hidden_two)
    scaled = norm_three * gain_three
    error = jnp.sum(scaled * head_vec, axis=-1, keepdims=True) - target
    weighed = live * error
    grad_pred = 2.0 * weighed / total_ref[0]
    grad_two = norm_back(grad_pred * (head_vec * gain_three), norm_three, inv_three)
    low_two = grad_two.astype(bf16)
    act_two_t = act_two.T
    for c in range(0, ff, chunk):
        ddown_ref[c:c + chunk, :] += dotf(g_ref[:, c:c + chunk].T, low_two, NN)
        grad_up = (u_ref[:, c:c + chunk] * dotf(low_two, down_ref[c:c + chunk, :], NT)).astype(bf16)
        dup_ref[:, c:c + chunk] += dotf(act_two_t, grad_up, NN)
        g_ref[:, c:c + chunk] = grad_up
    grad_act_two = dotf(g_ref[...], up_ref[...], NT)
    grad_one = grad_two + norm_back(grad_act_two * gain_two, norm_two, inv_two)
    low_one = grad_one.astype(bf16)
    dout_ref[...] += dotf(attn.T, low_one, NN)
    denc_ref[...] += dotf(feat.T, low_one, NN)
    gattn = dotf(low_one, out_ref[...], NT).astype(bf16)
    width = gattn.shape[1] // heads
    for h in range(heads):
        gattn_ref[h] = gattn[:, h * width:(h + 1) * width]
    down = lambda a: jnp.sum(a, axis=0, keepdims=True)
    loss = jnp.broadcast_to(jnp.sum(weighed * error, axis=0, keepdims=True), (1, bias.shape[1]))
    dvec_ref[...] += jnp.concatenate(
        [down(grad_one), down(grad_act_two * norm_two), down(grad_pred * head_vec * norm_three), down(grad_pred * scaled), loss,
         jnp.zeros((3, bias.shape[1]), f32)], axis=0)


def dense(part, total, attn, feat, side, vec, enc, out_w, up_w, down_w, olds=None, tile=256, chunk=512):
    heads, rows, cols = attn.shape
    width, ff = up_w.shape
    per = rows // tile
    first = olds is None
    whole = lambda a: pl.BlockSpec(a.shape, lambda i: (0,) * a.ndim, pipeline_mode=pl.Buffered(1))
    keep = lambda s: pl.BlockSpec(s, lambda i: (0,) * len(s), pipeline_mode=pl.Buffered(1))
    shapes = [(ff, width), (width, ff), (width, width), (feat.shape[1], width), (8, width)]
    olds = () if first else tuple(olds)
    return pl.pallas_call(
        functools.partial(dense_kernel, first, chunk),
        grid=(per,),
        in_specs=[pl.BlockSpec(memory_space=pltpu.SMEM),
                  pl.BlockSpec((heads, tile, cols), lambda i: (0, i, 0)),
                  pl.BlockSpec((tile, feat.shape[1]), lambda i: (part * per + i, 0)),
                  pl.BlockSpec((tile, side.shape[1]), lambda i: (part * per + i, 0)),
                  whole(vec), whole(enc), whole(out_w), whole(up_w), whole(down_w)] + [whole(o) for o in olds],
        out_specs=[pl.BlockSpec((heads, tile, cols), lambda i: (0, i, 0))] + [keep(s) for s in shapes],
        out_shape=[jax.ShapeDtypeStruct((heads, rows, cols), bf16)] + [jax.ShapeDtypeStruct(s, f32) for s in shapes],
        scratch_shapes=[pltpu.VMEM((tile, ff), f32), pltpu.VMEM((tile, ff), bf16)],
        compiler_params=pltpu.CompilerParams(vmem_limit_bytes=60 << 20),
        cost_estimate=pl.CostEstimate(flops=rows * 5 * 10**7, bytes_accessed=3 * 10**7, transcendentals=0),
        name="dense",
    )(total, attn, feat, side, vec, enc, out_w, up_w, down_w, *olds)
MESH = pl.DeviceIdType.MESH


def front_kernel(nodes, heads, feat, enc, qkv, vec, out_f, out_e, out_q, out_v, up_s, up_r, down_s, down_r, halo_s, halo_r, w_s, w_r, l_sem):
    node, head = lax.axis_index("nodes"), lax.axis_index("heads")
    after, before = lax.rem(node + 1, nodes), lax.rem(node + nodes - 1, nodes)
    barrier = pltpu.get_barrier_semaphore()
    for other in (after, before):
        pl.semaphore_signal(barrier, inc=1, device_id=(other, head), device_id_type=MESH)
    for s in range(1, heads):
        pl.semaphore_signal(barrier, inc=1, device_id=(node, lax.rem(head + s, heads)), device_id_type=MESH)
    pl.semaphore_wait(barrier, heads + 1)

    own = [pltpu.make_async_copy(feat, out_f.at[1, head], l_sem.at[0]),
           pltpu.make_async_copy(enc, out_e.at[head], l_sem.at[1]),
           pltpu.make_async_copy(qkv.at[head], out_q.at[head], l_sem.at[2]),
           pltpu.make_async_copy(vec, out_v.at[head], l_sem.at[3])]

    def relay(step, upward):
        shard = head - step if upward else head + step
        shard = jnp.clip(shard, 0, heads - 1)
        target = jnp.clip(head + 1 if upward else head - 1, 0, heads - 1)
        sems = (up_s, up_r) if upward else (down_s, down_r)
        src = feat if step == 0 else out_f.at[1, shard]
        return pltpu.make_async_remote_copy(
            src_ref=src, dst_ref=out_f.at[1, shard], send_sem=sems[0].at[step], recv_sem=sems[1].at[step],
            device_id=(node, target), device_id_type=MESH)

    def halo(shard, src, way):
        return pltpu.make_async_remote_copy(
            src_ref=src, dst_ref=out_f.at[0 if way == 0 else 2, shard], send_sem=halo_s.at[way, shard], recv_sem=halo_r.at[way, shard],
            device_id=(after if way == 0 else before, head), device_id_type=MESH)

    def sends(step, upward):
        return (head - step >= 0) & (head + 1 <= heads - 1) if upward else (head + step <= heads - 1) & (head - 1 >= 0)

    def gets(step, upward):
        return head - 1 - step >= 0 if upward else head + 1 + step <= heads - 1

    for step in range(heads - 1):
        for upward in (True, False):
            @pl.when(sends(step, upward))
            def _(step=step, upward=upward):
                relay(step, upward).start()
        if step == 0:
            for way in range(2):
                halo(head, feat, way).start()
            for copy in own:
                copy.start()
        if step == heads - 2:
            weights = []
            for s in range(1, heads):
                there = lax.rem(head + s, heads)
                for i, (src, dst) in enumerate(((enc, out_e.at[head]), (qkv.at[there], out_q.at[head]), (vec, out_v.at[head]))):
                    slot = (s - 1) * 3 + i
                    weights.append(pltpu.make_async_remote_copy(
                        src_ref=src, dst_ref=dst, send_sem=w_s.at[slot], recv_sem=w_r.at[slot], device_id=(node, there), device_id_type=MESH))
                    weights[-1].start()
        for upward in (True, False):
            @pl.when(gets(step, upward))
            def _(step=step, upward=upward):
                relay(step, upward).wait_recv()
                shard = head - 1 - step if upward else head + 1 + step
                for way in range(2):
                    halo(shard, out_f.at[1, shard], way).start()
    for step in range(heads - 1):
        for upward in (True, False):
            @pl.when(sends(step, upward))
            def _(step=step, upward=upward):
                relay(step, upward).wait_send()
    for copy in own + weights:
        copy.wait()
    for shard in range(heads):
        for way in range(2):
            halo(shard, feat, way).wait()


def front(feat, enc, qkv, vec, nodes, heads):
    dma = pltpu.SemaphoreType.DMA
    vmem, anywhere = pl.BlockSpec(memory_space=pltpu.VMEM), pl.BlockSpec(memory_space=pl.ANY)
    n = 3 * (heads - 1)
    return pl.pallas_call(
        functools.partial(front_kernel, nodes, heads),
        in_specs=[vmem] * 4, out_specs=[anywhere] + [vmem] * 3,
        out_shape=[jax.ShapeDtypeStruct((3, heads, *feat.shape), feat.dtype), jax.ShapeDtypeStruct((heads, *enc.shape), enc.dtype),
                   jax.ShapeDtypeStruct(qkv.shape, qkv.dtype), jax.ShapeDtypeStruct((heads, *vec.shape), vec.dtype)],
        scratch_shapes=[dma((heads - 1,))] * 4 + [dma((2, heads))] * 2 + [dma((n,))] * 2 + [dma((4,))],
        compiler_params=pltpu.CompilerParams(collective_id=2, has_side_effects=True, vmem_limit_bytes=24 << 20),
        name="front",
    )(feat, enc, qkv, vec)


def pair_kernel(nodes, heads, down, up, out, slab, got_d, got_u, got_o, own_d, own_u, own_o, s_sem, r_sem, l_sem):
    node, head = lax.axis_index("nodes"), lax.axis_index("heads")
    chips = nodes // 2
    chip, side = lax.div(node, 2), lax.rem(node, 2)
    twin = chip * 2 + 1 - side
    barrier = pltpu.get_barrier_semaphore()
    pl.semaphore_signal(barrier, inc=1, device_id=(twin, head), device_id_type=MESH)
    pl.semaphore_wait(barrier, 1)
    moves = []
    for i, (src, got, own) in enumerate(((down, got_d, own_d), (up, got_u, own_u), (out, got_o, own_o))):
        local = pltpu.make_async_copy(src.at[:, :, side], own, l_sem.at[i])
        remote = pltpu.make_async_remote_copy(
            src_ref=src.at[:, :, 1 - side], dst_ref=got, send_sem=s_sem.at[i], recv_sem=r_sem.at[i], device_id=(twin, head), device_id_type=MESH)
        local.start()
        remote.start()
        moves.append((local, remote))
    width = out.shape[-1]
    at = 0
    for (local, remote), got, own in zip(moves, (got_d, got_u, got_o), (own_d, own_u, own_o)):
        local.wait()
        remote.wait()
        rows = own.shape[2]
        for c in range(0, own.shape[3], width):
            for s in range(chips):
                there = lax.rem(chip + s, chips)
                slab[s, :, at:at + rows, :] = own[:, there, :, c:c + width] + got[:, there, :, c:c + width]
            at += rows


def pair(down, up, out, nodes, heads):
    chips = nodes // 2
    split = lambda a: a.reshape(heads, chips, 2, -1, a.shape[-1])
    down, up, out = split(down), split(up), split(out)
    width = out.shape[-1]
    rows = sum(a.shape[3] * a.shape[4] // width for a in (down, up, out))
    half = [pltpu.VMEM((heads, chips, *a.shape[3:]), f32) for a in (down, up, out)]
    dma = pltpu.SemaphoreType.DMA
    return pl.pallas_call(
        functools.partial(pair_kernel, nodes, heads),
        in_specs=[pl.BlockSpec(memory_space=pl.ANY)] * 3, out_specs=pl.BlockSpec(memory_space=pltpu.VMEM),
        out_shape=jax.ShapeDtypeStruct((chips, heads, rows, width), f32),
        scratch_shapes=half + half + [dma((3,))] * 3,
        compiler_params=pltpu.CompilerParams(collective_id=3, has_side_effects=True, vmem_limit_bytes=32 << 20),
        cost_estimate=pl.CostEstimate(flops=10**10, bytes_accessed=2 * 10**7, transcendentals=0),
        name="pair",
    )(down, up, out)


def send(src, dst, sems, slot, node, head):
    copy = pltpu.make_async_remote_copy(
        src_ref=src, dst_ref=dst, send_sem=sems[0].at[slot], recv_sem=sems[1].at[slot], device_id=(node, head), device_id_type=MESH)
    copy.start()
    return copy


def greet(nodes, heads, node, head):
    barrier = pltpu.get_barrier_semaphore()
    for s in range(1, nodes):
        pl.semaphore_signal(barrier, inc=1, device_id=(lax.rem(node + s, nodes), head), device_id_type=MESH)
    for s in range(1, heads):
        pl.semaphore_signal(barrier, inc=1, device_id=(node, lax.rem(head + s, heads)), device_id_type=MESH)
    pl.semaphore_wait(barrier, nodes + heads - 2)


def finish_kernel(nodes, heads, *refs):
    (qkv, enc, vec, *bulk), refs = refs[:4], refs[4:]
    (out_q, out_e, out_v, *out_b), refs = refs[:4], refs[4:]
    (q_half, q_one, q_two, q_part, q_sum, q_own, e_half, e_one, e_two, e_sum, e_three, e_own, v_half, v_two, v_three, v_one, v_sum), refs = refs[:17], refs[17:]
    s_one, r_one, s_two, r_two, s_three, r_three, s_four, r_four, s_bulk, r_bulk, s_pass, r_pass, l_sem = refs
    node, head = lax.axis_index("nodes"), lax.axis_index("heads")
    chips = nodes // 2
    chip, side = lax.div(node, 2), lax.rem(node, 2)
    twin = chip * 2 + 1 - side
    greet(nodes, heads, node, head)
    first = [send(ref.at[:, :, 1 - side], dst, (s_one, r_one), i, twin, head) for i, (ref, dst) in enumerate(((qkv, q_half), (enc, e_half)))]
    first.append(send(vec, v_half, (s_one, r_one), 2, twin, head))
    keep = [pltpu.make_async_copy(src, dst.at[node], l_sem.at[i]) for i, (src, dst) in enumerate(zip(bulk, out_b))]
    for copy in keep:
        copy.start()
    spread = []
    for s in range(chips):
        other = lax.rem(chip + s, chips) * 2 + side if s else twin
        spread.append([send(src, dst.at[node], (s_bulk, r_bulk), s + i, other, head) for i, (src, dst) in enumerate(zip(bulk, out_b))])
    for copy in first:
        copy.wait()
    q_one[...] = qkv[:, :, side] + q_half[...]
    e_one[...] = enc[:, :, side] + e_half[...]
    v_one[...] = vec[...] + v_half[...]
    second = []
    for s in range(1, chips):
        there = lax.rem(chip + s, chips)
        target = there * 2 + side
        i = (s - 1) * 3
        second.append(send(q_one.at[:, there], q_two.at[s - 1], (s_two, r_two), i, target, head))
        second.append(send(e_one.at[:, there], e_two.at[s - 1], (s_two, r_two), i + 1, target, head))
        second.append(send(v_one, v_two.at[s - 1], (s_two, r_two), i + 2, target, head))
    for copy in second:
        copy.wait()
    q_part[...] = functools.reduce(jnp.add, [q_two[s] for s in range(chips - 1)], q_one[:, chip])
    e_sum[...] = functools.reduce(jnp.add, [e_two[s] for s in range(chips - 1)], e_one[:, chip])
    v_sum[...] = functools.reduce(jnp.add, [v_two[s] for s in range(chips - 1)], v_one[...])
    third = []
    for s in range(1, heads):
        there = lax.rem(head + s, heads)
        i = (s - 1) * 3
        third.append(send(q_part.at[there], q_sum.at[head], (s_three, r_three), i, node, there))
        third.append(send(e_sum.at[there], e_three.at[s - 1], (s_three, r_three), i + 1, node, there))
        third.append(send(v_sum, v_three.at[s - 1], (s_three, r_three), i + 2, node, there))
    for copy in third:
        copy.wait()
    q_sum[pl.ds(head, 1)] = q_part[pl.ds(head, 1)]
    e_own[...] = functools.reduce(jnp.add, [e_three[s] for s in range(heads - 1)], e_sum[head])
    out_v[...] = functools.reduce(jnp.add, [v_three[s] for s in range(heads - 1)], v_sum[...])
    fourth = []
    for s in range(1, nodes):
        there = lax.rem(node + s, nodes)
        fourth.append(send(q_sum, out_q.at[node], (s_four, r_four), (s - 1) * 2, there, head))
        fourth.append(send(e_own, out_e.at[node], (s_four, r_four), (s - 1) * 2 + 1, there, head))
    out_q[node] = q_sum[...]
    out_e[node] = e_own[...]
    for copy in keep:
        copy.wait()
    passed = []
    for s in range(chips):
        for copy in spread[s]:
            copy.wait()
        if s:
            origin = lax.rem(chip + chips - s, chips) * 2 + side
            passed += [send(dst.at[origin], dst.at[origin], (s_pass, r_pass), (s - 1) + i, twin, head) for i, dst in enumerate(out_b)]
    for copy in passed:
        copy.wait()
    for copy in fourth:
        copy.wait()


def finish(qkv, enc, vec, bulk, nodes, heads):
    chips = nodes // 2
    split = lambda a: a.reshape(heads, chips, 2, -1, a.shape[-1])
    qkv, enc = split(qkv), split(enc)
    vm = lambda *s: pltpu.VMEM(s, f32)
    rq, wq, re, we = *qkv.shape[3:], *enc.shape[3:]
    dma = pltpu.SemaphoreType.DMA
    wv = vec.shape
    scratch = [vm(heads, chips, rq, wq), vm(heads, chips, rq, wq), vm(chips - 1, heads, rq, wq), vm(heads, rq, wq), vm(heads, rq, wq), vm(8, 128),
               vm(heads, chips, re, we), vm(heads, chips, re, we), vm(chips - 1, heads, re, we), vm(heads, re, we), vm(heads - 1, re, we), vm(re, we),
               vm(*wv), vm(chips - 1, *wv), vm(heads - 1, *wv), vm(*wv), vm(*wv)]
    counts = (3, 3, 3 * chips - 3, 3 * chips - 3, 3 * heads - 3, 3 * heads - 3, 2 * nodes - 2, 2 * nodes - 2, chips, chips, chips - 1, chips - 1, 1)
    out_shape = [jax.ShapeDtypeStruct(s, f32) for s in [(nodes, heads, rq, wq), (nodes, re, we), wv] + [(nodes, *b.shape) for b in bulk]]
    spec = pl.BlockSpec(memory_space=pltpu.VMEM)
    return pl.pallas_call(
        functools.partial(finish_kernel, nodes, heads),
        in_specs=[spec] * 4, out_specs=[spec] * 4, out_shape=out_shape,
        scratch_shapes=scratch + [dma((n,)) for n in counts],
        compiler_params=pltpu.CompilerParams(collective_id=1, has_side_effects=True, vmem_limit_bytes=48 << 20),
        name="finish",
    )(qkv, enc, vec, *bulk)
D = 512
HEADS = 8
NBR = 8
ADAM_STEP = 3
highest = lax.Precision.HIGHEST
beta_one = 0.5
beta_two = 0.5
learn_rate = 0.02
weight_decay = 0.1
adam_eps = 1e-08


def adamw(weight, first_moment, second, gradient):
    first_new = beta_one * first_moment + (1.0 - beta_one) * gradient
    second_new = beta_two * second + (1.0 - beta_two) * gradient * gradient
    first_hat = first_new / (1.0 - beta_one**ADAM_STEP)
    second_hat = second_new / (1.0 - beta_two**ADAM_STEP)
    weight_new = weight - learn_rate * (
        first_hat / (jnp.sqrt(second_hat) + adam_eps) + weight_decay * weight
    )
    return (weight_new, first_new, second_new)


def local(
    features, target, counts, neighbours, edge_kinds,
    enc_weight, enc_first, enc_second, qkv_weight, qkv_first, qkv_second,
    out_weight, out_first, out_second, up_weight, up_first, up_second,
    down_weight, down_first, down_second, vec_weight, vec_first, vec_second,
):
    heads_count = lax.axis_size("heads")
    nodes_count = lax.axis_size("nodes")
    head_index = lax.axis_index("heads")
    node_index = lax.axis_index("nodes")
    row_count = features.shape[0]
    own_blocks = row_count // BLOCK
    group_blocks = own_blocks * heads_count
    group_rows = group_blocks * BLOCK
    hl = HEADS // heads_count
    hs = D // HEADS
    cols = hl * hs
    cp = -(-cols // 128) * 128
    ka = -(-(cols + 1) // 128) * 128
    kinds = D // HEADS
    slots = NBR + 1
    low = lambda a: a.astype(bf16)
    gather = lambda a, axis: lax.all_gather(low(a), "heads", axis=axis, tiled=True)

    qkv_parts = jnp.transpose(low(qkv_weight).reshape(-1, heads_count, hl, 3, hs), (1, 0, 3, 2, 4)).reshape(heads_count, -1, 3, cols)
    qkv_parts = jnp.pad(qkv_parts, ((0, 0), (0, 0), (0, 0), (0, cp - cols))).reshape(heads_count, -1, 3 * cp)
    vec_part = jnp.pad(low(vec_weight).astype(f32), ((0, 2), (0, 0)))
    feats, enc_b, qkv_cols, vectors = front(features, low(enc_weight), qkv_parts, vec_part, nodes_count, heads_count)
    feats = feats.reshape(3 * group_rows, -1)
    enc_b = enc_b.reshape(-1, D)
    qkv_cols = qkv_cols.reshape(D, 3 * cp)
    vectors = jnp.transpose(vectors, (1, 0, 2)).reshape(8, D)
    up_low, out_low, down_low, enc_b = lax.optimization_barrier((low(up_weight), low(out_weight), low(down_weight), enc_b))
    wide_b = lax.all_gather(jnp.concatenate([up_low, out_low], axis=1), "heads", axis=0, tiled=True)
    down_b = lax.all_gather(down_low, "heads", axis=0, tiled=True)

    enc_bias, gain_one, gain_two, gain_three, head_vec = (vectors[r] for r in range(5))
    edge_local = lax.dynamic_slice_in_dim(vectors[5].reshape(kinds, HEADS), head_index * hl, hl, 1)
    own_counts = lax.dynamic_slice_in_dim(counts, (node_index * heads_count + head_index) * own_blocks, own_blocks)
    row_live = (jnp.arange(BLOCK, dtype=jnp.int32)[None, :] < own_counts[:, None]).reshape(row_count).astype(f32)
    live_total = jnp.sum(counts).astype(f32)

    def group_counts(offset):
        return lax.dynamic_slice_in_dim(counts, (node_index + offset) % nodes_count * group_blocks, group_blocks)

    pool_counts = jnp.concatenate([group_counts(nodes_count - 1), group_counts(0), group_counts(1)])
    relative = (neighbours // group_blocks - node_index + 1) % nodes_count
    nbr_pos = relative * group_blocks + neighbours % group_blocks
    self_pos = group_blocks + jnp.arange(group_blocks, dtype=jnp.int32)
    key_pos = jnp.concatenate([self_pos[:, None], nbr_pos], axis=1).reshape(-1)
    kind_hot = jax.nn.one_hot(edge_kinds, kinds, dtype=f32)
    slot_bias = jnp.einsum("bst,th->bsh", kind_hot, edge_local, precision=highest)
    bias_rows = jnp.repeat(slot_bias, BLOCK, axis=2)

    kaug, kt, value, vt, query = encode(
        pool_counts, feats, enc_b, enc_bias[None], gain_one[None], qkv_cols, cp, ka, cols, hs**-0.5)
    side = jnp.stack([target, row_live], axis=1)
    dense_vec = jnp.stack([enc_bias, gain_two, gain_three, head_vec])
    half = lambda a: a.reshape(heads_count, 2, row_count // 2, -1)
    exchange = lambda a: lax.all_to_all(a, "heads", split_axis=0, concat_axis=0, tiled=True)
    attn_parts, lse_parts, grad_parts, totals = [], [], [], None
    for part in range(2):
        attn_part, lse_part = attend(part, own_blocks, key_pos, query, bias_rows, kaug, vt, hl, hs)
        attn_parts.append(attn_part)
        lse_parts.append(lse_part)
    wide_b, down_b, attn_parts[1] = lax.optimization_barrier((wide_b, down_b, attn_parts[1]))
    up_b, out_b = wide_b[:, :up_weight.shape[1]], wide_b[:, up_weight.shape[1]:]
    for part in range(2):
        attn_rows = exchange(attn_parts[part].reshape(heads_count, row_count // 2, cp)[..., :cols])
        grad_part, *totals = dense(part, live_total[None], attn_rows, features, side, dense_vec, enc_b, out_b, up_b, down_b, totals)
        grad_parts.append(exchange(grad_part))
    grad_down, grad_up, grad_out, denc_own, dense_sums = totals
    grad_parts[0], grad_down = lax.optimization_barrier((grad_parts[0], grad_down))
    slab = pair(grad_down, grad_up, grad_out, nodes_count, heads_count)
    moved = [slab[0]] + [
        lax.ppermute(slab[s], "nodes", [(i, (i + 2 * s) % nodes_count) for i in range(nodes_count)]) for s in range(1, nodes_count // 2)]
    grad_heads = jnp.concatenate([g[:, None] for g in grad_parts], axis=1).reshape(group_rows, cols)
    grad_heads = jnp.pad(grad_heads, ((0, 0), (0, cp - cols)))
    dq, dkv, edge_sums = attend_back(own_blocks, key_pos, query, grad_heads, attn_parts, lse_parts, bias_rows, kaug, value, kt, hl, hs)
    moved, dkv = lax.optimization_barrier((moved, dkv))
    planes = exchange(functools.reduce(jnp.add, moved))
    slot_sums = jnp.sum(edge_sums.reshape(group_blocks, slots, hl, BLOCK), axis=3)
    edge_grad = jnp.einsum("bst,bsh->th", kind_hot, slot_sums, precision=highest)
    columns = lambda a: jnp.broadcast_to(a[:, None], (D, 128))
    dw, denc_t, dgain, dbias = encode_back(
        feats, dkv, dq, enc_b.T, columns(enc_bias), columns(gain_one), qkv_cols[:, :cp], qkv_cols[:, cp:])

    grad_gain_one = jnp.sum(dgain, axis=1)
    grad_enc_bias = jnp.sum(dbias, axis=1) + dense_sums[0]
    grad_enc = denc_t.T + denc_own
    edge_full = lax.dynamic_update_slice(jnp.zeros((kinds, HEADS), f32), edge_grad, (jnp.int32(0), head_index * hl))
    grad_vec = jnp.concatenate([grad_enc_bias[None], grad_gain_one[None], dense_sums[1:5], edge_full.reshape(1, D), jnp.zeros((1, D), f32)])
    planes, dw = lax.optimization_barrier((planes, dw))
    dw_sum, enc_sum, vec_total, bulk = finish(dw, grad_enc, grad_vec, [jnp.sum(planes, axis=0)], nodes_count, heads_count)
    total_loss = vec_total[5, 0]
    vec_sum = lax.dynamic_slice_in_dim(jnp.concatenate([vec_total[:5], vec_total[6:7]]), head_index * (D // heads_count), D // heads_count, 1)
    qkv_sum = jnp.transpose(dw_sum, (0, 2, 1, 3)).reshape(-1, heads_count, 3, cp)[..., :cols].reshape(-1, heads_count, 3, hl, hs)
    qkv_sum = jnp.transpose(qkv_sum, (0, 1, 3, 2, 4)).reshape(qkv_weight.shape)
    flat = lambda a: a.reshape(-1, a.shape[-1])
    rows_down, rows_out = down_weight.shape[0] // nodes_count, out_weight.shape[0] // nodes_count
    up_sum = bulk[:, rows_down:-rows_out].reshape(nodes_count, -1, rows_out, D)
    up_sum = jnp.transpose(up_sum, (0, 2, 1, 3)).reshape(up_weight.shape)
    summed = (flat(enc_sum), qkv_sum, flat(bulk[:, -rows_out:]), up_sum, flat(bulk[:, :rows_down]), vec_sum)
    enc_res = adamw(enc_weight, enc_first, enc_second, summed[0])
    qkv_res = adamw(qkv_weight, qkv_first, qkv_second, summed[1])
    out_res = adamw(out_weight, out_first, out_second, summed[2])
    up_res = adamw(up_weight, up_first, up_second, summed[3])
    down_res = adamw(down_weight, down_first, down_second, summed[4])
    vec_res = adamw(vec_weight, vec_first, vec_second, summed[5])
    loss_value = (total_loss / live_total).reshape(1)
    return (
        loss_value, *enc_res, *qkv_res, *out_res, *up_res, *down_res, *vec_res,
        low(enc_res[0]), low(qkv_res[0]), low(out_res[0]), low(up_res[0]), low(down_res[0]),
    )


def solution(mesh):
    rows = P("heads", None)
    both = P(("nodes", "heads"))
    lanes = P(None, "heads")
    in_specs = (P(("nodes", "heads"), None), both, P(), P("nodes", None), P("nodes", None)) + (rows,) * 15 + (lanes,) * 3
    out_specs = (P(),) + (rows,) * 15 + (lanes,) * 3 + (rows,) * 5
    return jax.shard_map(local, mesh=mesh, in_specs=in_specs, out_specs=out_specs, check_vma=False)
```

time: 585 us -> 459 us (0.78); the launches traced: 575 us -> 457 us
  Pallas kernels: 247 us -> 320 us
  blocking collectives: 72.7 us -> 0 us
  waiting for transfers between devices: 72.9 us -> 21.4 us
  matrix products: 40.2 us -> 0.67 us
  other arithmetic: 37.9 us -> 24.3 us
  starting transfers between devices: 39.6 us -> 26.8 us
    pallas_call x1 -> x6, Pallas kernels: 44.2 us -> 155 us  [the longest x1 61 us: front(): pl.pallas_call(functools.partial(front_kernel, nodes, heads), in_specs=[v...]
    all_gather x3 -> x0, blocking collectives: 72.7 us -> none  [local(): lax.all_gather(low(a), 'heads', axis=axis, tiled=True)]
    dot_general x11 -> x0, matrix products: 39.6 us -> none  [the longest x1 7.87 us: local(): jnp.einsum('rd,fd->rf', grad_two_low, down_b, preferred_element_type=f32)]
    pallas_call x1, Pallas kernels: 80.8 us -> 45.4 us  [attend_back(): pl.pallas_call(functools.partial(attend_back_kernel, hl, hs, cp, ka, slot...]
    all_gather x3 -> x2, waiting for transfers between devices: 47.8 us -> 20.5 us  [the longest x1 20.5 us: local(): lax.all_gather(jnp.concatenate([up_low, out_low], axis=1), 'heads', axis=...]
    ppermute x14 -> x3, waiting for transfers between devices: 18.8 us -> 0.91 us  [local(): lax.ppermute(slab[s], 'nodes', [(i, (i + 2 * s) % nodes_count) for i in r...]
    ppermute x14 -> x3, starting transfers between devices: 13.2 us -> 4.41 us  [local(): lax.ppermute(slab[s], 'nodes', [(i, (i + 2 * s) % nodes_count) for i in r...]
    reduce_sum x12 -> x2, other arithmetic: 8.31 us -> 1.54 us  [the longest x1 1.4 us: local(): jnp.sum(planes, axis=0)]
  transfers between devices with their start and end apart: 23 -> 10, of which waited for: 5 -> 3; matrix products, arithmetic and copies ran while one was open for 13% -> 6% of each run, Pallas kernels for 36% -> 48%
where the time goes in v3:
time: 459 us; the launch traced here: 457 us
  Pallas kernels  320 us (70%)
  local copies, waits for them, and re-layouts  46.6 us (10%)
  starting transfers between devices  26.8 us (6%)
  other arithmetic  24.3 us (5%)
  waiting for transfers between devices  21.4 us (5%)
  between operations  17.2 us (4%)
    pallas_call x1, Pallas kernels, front(): pl.pallas_call(functools.partial(front_kernel, nodes, heads), in_specs=[v...  61 us
    pallas_call x1, Pallas kernels, encode_back(): pl.pallas_call(functools.partial(encode_back_kernel, cp, per), grid=(3 *...  47 us
    pallas_call x1, Pallas kernels, attend_back(): pl.pallas_call(functools.partial(attend_back_kernel, hl, hs, cp, ka, slot...  45.4 us
    pallas_call x2, Pallas kernels, attend(): pl.pallas_call(functools.partial(attend_kernel, hl, hs, cp, ka, slots, bl...  44.1 us
    pallas_call x2, Pallas kernels, dense(): pl.pallas_call(functools.partial(dense_kernel, first, chunk), grid=(per,)...  41.6 us
    pallas_call x1, Pallas kernels, finish(): pl.pallas_call(functools.partial(finish_kernel, nodes, heads), in_specs=[...  41.3 us
    pallas_call x1, Pallas kernels, encode(): pl.pallas_call(functools.partial(encode_kernel, cp, ka, cols, scale, per)...  31.3 us
    all_to_all x5, starting transfers between devices, local(): lax.all_to_all(a, 'heads', split_axis=0, concat_axis=0, tiled=True)  22.3 us
  transfers between devices with their start and end apart: 10, of which 3 were waited for; matrix products, arithmetic and copies ran while one was open for 6% of the time, Pallas kernels for 48%

profile of v3, /device:TPU:0, one launch (start us, length us, event | category | flops | bytes accessed | tf_op | source)
XLA Modules:
  0.0 457.0 jit_solution(979567867021061103)
XLA Ops:
  12.7 61.0 %front.1 = (bf16[3,4,1024,256]{3,2,1,0:T(8,128)(2,1)S(1)}, bf16[4,64,512]{2,1,0:T(8,128)(2,1)S(1)}, bf16[4,128,384]{2,1,0:T(8,128)(2,1)S(1)}, f32[4,8,128]{2,1,0:T(8,128)S(1)}) custom-call(bf16[1024,256]{1,0:T(8,128)(2,1)S(1)} %copy-done.1, bf16[64,512]{1,0:T(8,128)(2,1)S(1)} %convert_element_type.55.enc, bf16[4,128,384]{2,1,0:T(8,128)(2,1)S(1)} %copy.90.qkv, ...), custom_call_target="tpu_custom_call" | custom-call | tf_op jit(solution)/shard_map/front/pallas_call | solution.py:466
  75.2 2.6 copy-done.6
  80.1 31.3 %encode.1 = (bf16[12288,256]{1,0:T(8,128)(2,1)}, bf16[96,128,128]{2,1,0:T(8,128)(2,1)}, bf16[12288,128]{1,0:T(8,128)(2,1)}, bf16[96,128,128]{2,1,0:T(8,128)(2,1)}, bf16[4096,128]{1,0:T(8,128)(2,1)}) custom-call(s32[96]{0:T(128)} %pad_add_fusion.1.cnt_ref, bf16[12288,256]{1,0:T(8,128)(2,1)} %bitcast.101, bf16[256,512]{1,0:T(8,128)(2,1)} %bitcast.95, ...), custom_call_target="tpu_custom_call" | custom-call | flops 24576000000 | bytes 30000000 | tf_op jit(solution)/shard_map/encode/pallas_call | solution.py:205
  114.2 22.0 %attend.2 = (bf16[2048,128]{1,0:T(8,128)(2,1)}, f32[16,1,256]{2,1,0:T(1,128)}) custom-call(s32[288]{0:T(512)} %reshape.170.pos_ref, bf16[4096,128]{1,0:T(8,128)(2,1)} %get-tuple-element.81.q_ref, f32[32,9,256]{2,1,0:T(8,128)} %copy.93.brow_ref, bf16[12288,256]{1,0:T(8,128)(2,1)} %get-tuple-element.82.kaug_ref, bf16[96,128,128]{2,1,0:T(8,128)(2,1)} %get-tuple-element.83.vt_ref), custom_call_target="tpu_custom_call" | custom-call | flops 16000000000 | bytes 30000000 | tf_op jit(solution)/shard_map/attend/pallas_call | solution.py:74
  136.2 3.5 all-to-all-start
  139.7 22.1 %attend.3 = (bf16[2048,128]{1,0:T(8,128)(2,1)}, f32[16,1,256]{2,1,0:T(1,128)}) custom-call(s32[288]{0:T(512)} %reshape.170.pos_ref, bf16[4096,128]{1,0:T(8,128)(2,1)} %get-tuple-element.81.q_ref, f32[32,9,256]{2,1,0:T(8,128)} %copy.93.brow_ref, bf16[12288,256]{1,0:T(8,128)(2,1)} %get-tuple-element.82.kaug_ref, bf16[96,128,128]{2,1,0:T(8,128)(2,1)} %get-tuple-element.83.vt_ref), custom_call_target="tpu_custom_call" | custom-call | flops 16000000000 | bytes 30000000 | tf_op jit(solution)/shard_map/attend/pallas_call | solution.py:74
  169.5 20.5 %all-gather.3.cloned.1.call-done = bf16[512,2560]{1,0:T(8,128)(2,1)} async-done(((bf16[128,2560]{1,0:T(8,128)(2,1)}), bf16[512,2560]{1,0:T(8,128)(2,1)}) %all-gather.3.cloned.1.call-update) | async-done | bytes 2621456 | tf_op jit(solution)/shard_map/all_gather | solution.py:689
  190.0 1.9 slice.93.out_ref
  191.8 3.1 slice.94.up_ref
  195.0 3.7 all-to-all-start.2
  198.7 19.4 %dense.2 = (bf16[4,512,128]{2,1,0:T(8,128)(2,1)}, f32[2048,512]{1,0:T(8,128)}, f32[512,2048]{1,0:T(8,128)}, f32[512,512]{1,0:T(8,128)}, f32[256,512]{1,0:T(8,128)}, /*index=5*/f32[8,512]{1,0:T(8,128)}) custom-call(f32[1]{0:T(128)} %bitcast.total_ref, bf16[4,512,128]{2,1,0:T(8,128)(2,1)} %copy-done.31, bf16[1024,256]{1,0:T(8,128)(2,1)} %feat_ref.3, ...), custom_call_target="tpu_custom_call" | custom-call | flops 25600000000 | bytes 30000000 | tf_op jit(solution)/shard_map/dense/pallas_call | solution.py:370
  218.1 4.9 %all-to-all-start.1 = ((bf16[4,512,128]{2,1,0:T(8,128)(2,1)}), bf16[4,512,128]{2,1,0:T(8,128)(2,1)S(1)}, u32[]{:S(2)}, u32[]{:S(2)}) async-start(bf16[4,512,128]{2,1,0:T(8,128)(2,1)} %get-tuple-element.91), calls=%async_computation.1 | async-start | bytes 1048576 | tf_op jit(solution)/shard_map/all_to_all | solution.py:715
  223.0 22.2 %dense.3 = (bf16[4,512,128]{2,1,0:T(8,128)(2,1)}, f32[2048,512]{1,0:T(8,128)}, f32[512,2048]{1,0:T(8,128)}, f32[512,512]{1,0:T(8,128)}, f32[256,512]{1,0:T(8,128)}, /*index=5*/f32[8,512]{1,0:T(8,128)}) custom-call(f32[1]{0:T(128)} %bitcast.total_ref, bf16[4,512,128]{2,1,0:T(8,128)(2,1)} %copy-done.33, bf16[1024,256]{1,0:T(8,128)(2,1)} %feat_ref.3, ...), custom_call_target="tpu_custom_call" | custom-call | flops 25600000000 | bytes 30000000 | tf_op jit(solution)/shard_map/dense/pallas_call | solution.py:370
  245.2 5.1 %all-to-all-start.3 = ((bf16[4,512,128]{2,1,0:T(8,128)(2,1)}), bf16[4,512,128]{2,1,0:T(8,128)(2,1)S(1)}, u32[]{:S(2)}, u32[]{:S(2)}) async-start(bf16[4,512,128]{2,1,0:T(8,128)(2,1)} %get-tuple-element.103), calls=%async_computation.3 | async-start | bytes 1048576 | tf_op jit(solution)/shard_map/all_to_all | solution.py:715
  250.3 2.2 copy-done.7
  252.5 2.2 copy-done.8
  255.9 8.2 %pair.1 = f32[4,4,144,512]{3,2,1,0:T(8,128)S(1)} custom-call(f32[4,4,2,64,512]{4,3,2,1,0:T(8,128)S(1)} %bitcast.103, f32[4,4,2,16,2048]{4,3,2,1,0:T(8,128)S(1)} %bitcast.104, f32[4,4,2,16,512]{4,3,2,1,0:T(8,128)S(1)} %bitcast.105), custom_call_target="tpu_custom_call" | custom-call | flops 10000000000 | bytes 20000000 | tf_op jit(solution)/shard_map/pair/pallas_call | solution.py:514
  264.2 2.0 slice_bitcast_fusion
  267.4 1.6 collective-permute-start.1
  269.0 1.5 collective-permute-start.2
  271.9 45.4 %attend_back.1 = (bf16[4096,128]{1,0:T(8,128)(2,1)}, f32[12288,256]{1,0:T(8,128)}, f32[32,9,256]{2,1,0:T(8,128)}) custom-call(s32[288]{0:T(512)} %reshape.170.pos_ref, bf16[4096,128]{1,0:T(8,128)(2,1)} %get-tuple-element.81.q_ref, bf16[4096,128]{1,0:T(8,128)(2,1)} %bitcast.114, bf16[2048,128]{1,0:T(8,128)(2,1)} %get-tuple-element.84.oa_ref, ...), custom_call_target="tpu_custom_call" | custom-call | flops 64000000000 | bytes 60000000 | tf_op jit(solution)/shard_map/attend_back/pallas_call | solution.py:143
  320.7 3.6 add_add_fusion
  324.3 5.2 %all-to-all-start.4 = ((f32[4,144,512]{2,1,0:T(8,128)}), f32[4,144,512]{2,1,0:T(8,128)}, u32[]{:S(2)}, u32[]{:S(2)}) async-start(f32[4,144,512]{2,1,0:T(8,128)} %add_add_fusion), calls=%async_computation.4 | async-start | bytes 2359296 | tf_op jit(solution)/shard_map/all_to_all | solution.py:715
  331.2 47.0 %encode_back.1 = (f32[512,384]{1,0:T(8,128)}, f32[512,256]{1,0:T(8,128)}, f32[512,128]{1,0:T(8,128)}, f32[512,128]{1,0:T(8,128)}) custom-call(bf16[12288,256]{1,0:T(8,128)(2,1)} %bitcast.102, f32[12288,256]{1,0:T(8,128)} %get-tuple-element.113.dkv_ref, bf16[4096,128]{1,0:T(8,128)(2,1)} %get-tuple-element.114.dq_ref, bf16[512,256]{1,0:T(8,128)(2,1)} %bitcast.116, ...), custom_call_target="tpu_custom_call" | custom-call | flops 40960000000 | bytes 40000000 | tf_op jit(solution)/shard_map/encode_back/pallas_call | solution.py:277
  381.4 41.3 %finish.1 = (f32[8,4,16,384]{3,2,1,0:T(8,128)S(1)}, f32[8,8,512]{2,1,0:T(8,128)S(1)}, f32[8,512]{1,0:T(8,128)S(1)}, f32[8,144,512]{2,1,0:T(8,128)S(1)}) custom-call(f32[4,4,2,16,384]{4,3,2,1,0:T(8,128)S(1)} %bitcast.90, f32[4,4,2,8,512]{4,3,2,1,0:T(8,128)S(1)} %bitcast.89, f32[8,512]{1,0:T(8,128)S(1)} %concatenate.22.refs_2_, f32[144,512]{1,0:T(8,128)S(1)} %reduce_sum.52.refs_3_), custom_call_target="tpu_custom_call" | custom-call | tf_op jit(solution)/shard_map/finish/pallas_call | solution.py:626
  422.7 1.5 fusion.32
  427.1 2.2 copy.107
  429.2 3.1 fusion.27
  438.4 1.9 fusion.29
  440.3 2.0 fusion.25
  442.4 2.5 fusion.23
  445.9 2.5 fusion.21
  (180 shorter events, 40.7 us)
Async XLA Ops:
  7.2 162.3 %all-gather.5.cloned.1.call-start = ((), (), s32[]{:S(2)}) async-start(), calls=%async_computation.6 | async-start | bytes 2621440 | tf_op jit(solution)/shard_map/all_gather | solution.py:690
  75.2 2.6 copy-start.6
  77.8 112.2 %all-gather.3.cloned.1.call-start = ((), (), s32[]{:S(2)}) async-start(), calls=%async_computation.5 | async-start | bytes 3276800 | tf_op jit(solution)/shard_map/all_gather | solution.py:689
  80.1 31.3 %copy-start.47 = (s32[32,8]{0,1:T(8,128)S(1)}, s32[32,8]{0,1:T(8,128)}, u32[]{:S(2)}) copy-start(s32[32,8]{0,1:T(8,128)} %param.26) | copy-start | bytes 3076
  80.1 32.3 %copy-start.37 = (s32[32,9]{0,1:T(8,128)S(1)}, s32[32,9]{0,1:T(8,128)}, u32[]{:S(2)}) copy-start(s32[32,9]{0,1:T(8,128)} %param.27) | copy-start | bytes 3460
  136.2 58.8 %all-to-all-start = ((bf16[4,512,128]{2,1,0:T(8,128)(2,1)}), bf16[4,512,128]{2,1,0:T(8,128)(2,1)S(1)}, u32[]{:S(2)}, u32[]{:S(2)}) async-start(bf16[4,512,128]{2,1,0:T(8,128)(2,1)} %bitcast.115), calls=%async_computation | async-start | bytes 1048576 | tf_op jit(solution)/shard_map/all_to_all | solution.py:715
  139.7 22.8 %copy-start.5 = (bf16[4,64,512]{2,1,0:T(8,128)(2,1)S(1)}, bf16[4,64,512]{2,1,0:T(8,128)(2,1)}, u32[]{:S(2)}) copy-start(bf16[4,64,512]{2,1,0:T(8,128)(2,1)} %copy-done.4) | copy-start | bytes 786436
  139.7 23.6 %copy-start.3 = (bf16[4,128,384]{2,1,0:T(8,128)(2,1)S(1)}, bf16[4,128,384]{2,1,0:T(8,128)(2,1)}, u32[]{:S(2)}) copy-start(bf16[4,128,384]{2,1,0:T(8,128)(2,1)} %copy-done.2) | copy-start | bytes 1179652
  161.9 3.7 copy-start.48
  161.9 4.7 %copy-start.28 = (f32[128,1536]{1,0:T(8,128)S(1)}, f32[128,1536]{1,0:T(8,128)}, u32[]{:S(2)}) copy-start(f32[128,1536]{1,0:T(8,128)} %param.32) | copy-start | bytes 2359300
  164.0 3.7 copy-start.29
  195.0 3.7 copy-start.31
  195.0 23.1 %all-to-all-start.2 = ((bf16[4,512,128]{2,1,0:T(8,128)(2,1)}), bf16[4,512,128]{2,1,0:T(8,128)(2,1)S(1)}, u32[]{:S(2)}, u32[]{:S(2)}) async-start(bf16[4,512,128]{2,1,0:T(8,128)(2,1)} %bitcast.17), calls=%async_computation.2 | async-start | bytes 1048576 | tf_op jit(solution)/shard_map/all_to_all | solution.py:715
  218.1 4.9 %copy-start.33 = (bf16[4,512,128]{2,1,0:T(8,128)(2,1)}, bf16[4,512,128]{2,1,0:T(8,128)(2,1)S(1)}, u32[]{:S(2)}) copy-start(bf16[4,512,128]{2,1,0:T(8,128)(2,1)S(1)} %all-to-all-done.2.attn_ref) | copy-start | bytes 1572868
  218.1 27.1 %all-to-all-start.1 = ((bf16[4,512,128]{2,1,0:T(8,128)(2,1)}), bf16[4,512,128]{2,1,0:T(8,128)(2,1)S(1)}, u32[]{:S(2)}, u32[]{:S(2)}) async-start(bf16[4,512,128]{2,1,0:T(8,128)(2,1)} %get-tuple-element.91), calls=%async_computation.1 | async-start | bytes 1048576 | tf_op jit(solution)/shard_map/all_to_all | solution.py:715
  245.2 25.5 %all-to-all-start.3 = ((bf16[4,512,128]{2,1,0:T(8,128)(2,1)}), bf16[4,512,128]{2,1,0:T(8,128)(2,1)S(1)}, u32[]{:S(2)}, u32[]{:S(2)}) async-start(bf16[4,512,128]{2,1,0:T(8,128)(2,1)} %get-tuple-element.103), calls=%async_computation.3 | async-start | bytes 1048576 | tf_op jit(solution)/shard_map/all_to_all | solution.py:715
  264.1 6.4 %copy-start.32 = (f32[256,512]{1,0:T(8,128)S(1)}, f32[256,512]{1,0:T(8,128)}, u32[]{:S(2)}) copy-start(f32[256,512]{1,0:T(8,128)} %get-tuple-element.118) | copy-start | bytes 1572868
  264.1 6.6 %copy-start.45 = (f32[8,512]{1,0:T(8,128)S(1)}, f32[8,512]{1,0:T(8,128)}, u32[]{:S(2)}) copy-start(f32[8,512]{1,0:T(8,128)} %get-tuple-element.120) | copy-start | bytes 49156
  266.1 53.7 %collective-permute-start = (f32[4,144,512]{2,1,0:T(8,128)}, f32[4,144,512]{2,1,0:T(8,128)}, u32[]{:S(2)}, u32[]{:S(2)}) collective-permute-start(f32[4,144,512]{2,1,0:T(8,128)} %get-tuple-element.201), channel_id=1, source_target_pairs={{0,8},{4,12},{8,16},{12,20},{16,24},{20,28},{24,0},{28,4},{1,9},{5... | collective-permute-start | bytes 3538952 | tf_op jit(solution)/shard_map/ppermute | solution.py:731
  267.4 53.2 %collective-permute-start.1 = (f32[4,144,512]{2,1,0:T(8,128)}, f32[4,144,512]{2,1,0:T(8,128)}, u32[]{:S(2)}, u32[]{:S(2)}) collective-permute-start(f32[4,144,512]{2,1,0:T(8,128)} %get-tuple-element.200), channel_id=1, source_target_pairs={{0,16},{4,20},{8,24},{12,28},{16,0},{20,4},{24,8},{28,12},{1,17},{... | collective-permute-start | bytes 3538952 | tf_op jit(solution)/shard_map/ppermute | solution.py:731
  269.0 51.6 %collective-permute-start.2 = (f32[4,144,512]{2,1,0:T(8,128)}, f32[4,144,512]{2,1,0:T(8,128)}, u32[]{:S(2)}, u32[]{:S(2)}) collective-permute-start(f32[4,144,512]{2,1,0:T(8,128)} %get-tuple-element.199), channel_id=1, source_target_pairs={{0,24},{4,28},{8,0},{12,4},{16,8},{20,12},{24,16},{28,20},{1,25},{... | collective-permute-start | bytes 3538952 | tf_op jit(solution)/shard_map/ppermute | solution.py:731
  324.3 5.2 %copy-start.42 = (f32[1,4,128]{2,0,1:T(1,128)S(1)}, f32[1,4,128]{2,0,1:T(1,128)}, u32[]{:S(2)}) copy-start(f32[1,4,128]{2,0,1:T(1,128)} %get-tuple-element.212) | copy-start | bytes 6148
  324.3 6.1 %copy-start.41 = (f32[1,4,128]{2,0,1:T(1,128)S(1)}, f32[1,4,128]{2,0,1:T(1,128)}, u32[]{:S(2)}) copy-start(f32[1,4,128]{2,0,1:T(1,128)} %get-tuple-element.205) | copy-start | bytes 6148
  324.3 55.7 %all-to-all-start.4 = ((f32[4,144,512]{2,1,0:T(8,128)}), f32[4,144,512]{2,1,0:T(8,128)}, u32[]{:S(2)}, u32[]{:S(2)}) async-start(f32[4,144,512]{2,1,0:T(8,128)} %add_add_fusion), calls=%async_computation.4 | async-start | bytes 2359296 | tf_op jit(solution)/shard_map/all_to_all | solution.py:715
  436.8 3.5 copy-start.27
  436.8 3.5 copy-start.34
  437.4 4.9 %copy-start.23 = (f32[128,2048]{1,0:T(8,128)S(1)}, f32[128,2048]{1,0:T(8,128)}, u32[]{:S(2)}) copy-start(f32[128,2048]{1,0:T(8,128)} %param.39) | copy-start | bytes 3145732
  438.4 4.0 copy-start.13
  438.4 4.0 copy-start.22
  442.3 2.5 copy-start.15
  442.4 2.9 copy-start.24
  442.4 3.5 copy-start.25
  (29 other events, 50.2 us)
Sparse Core Ops, SparseCore 0:
  77.9 45.2 all-gather.4
  125.3 64.5 all-gather.2
